TPU v7x, 256 devices: a whole 4x4x8 slice. The times are simulated.
256 devices in a mesh: wide: 64 (over y, z, x_hi), narrow: 4 (over x_lo, core).
Axes of the slice: x: 4 (x_hi: 2, x_lo: 2; x = x_hi * 2 + x_lo), y: 4, z: 8, core: 2. Of those that a mesh axis runs over, the one named last changes fastest.
Arguments:
- rhs: float32 [3, 256, 32, 128], P(None, 'wide', 'narrow'), may hold values from -12 to 12
- start: float32 [3, 256, 32, 128], P(None, 'wide', 'narrow'), may hold values from -2 to 2
- trans: float32 [3, 256, 32, 128], P(None, 'wide', 'narrow'), may hold values from 0.2 to 2
- accum: float32 [256, 32, 128], P('wide', 'narrow'), may hold values from 2 to 8
- coupling: float32 [3, 3, 256, 32, 128], P(None, None, 'wide', 'narrow'), may hold values from -0.3 to 0.3
- well_cells: int32 [64, 4, 64], P('wide', 'narrow'), may hold values from 0 to 4095
- well_index: float32 [64, 4, 64], P('wide', 'narrow'), may hold values from 1 to 20
- agg_map: int32 [256, 32, 128], P('wide', 'narrow'), may hold values from 0 to 31
- tile_factors: bfloat16 [384, 48, 128, 128], P('wide', 'narrow')
- coarse_inverse: float32 [8192, 8192], P(('wide', 'narrow')), as said below
Outputs:
- iterate: float32 [3, 256, 32, 128], P(None, 'wide', 'narrow')
- residual: float32 [3, 256, 32, 128], P(None, 'wide', 'narrow')
Inputs may be any that keep to these rules, and one draw needn't show every extreme that they name: well_cells names, for each device's 64 connections, one of that device's own 4 * 8 * 128 cells, counted by pair, then column, then position in the tile; connections may share a cell. agg_map names one of the 32 aggregates of the device that owns the cell. coarse_inverse is symmetric.
All inputs are finite; a program needn't handle non-finite values.
Results may differ from a plain program's by a relative error of at most 0.00095.
Values sent between devices are 32-bit elements; how exact they have to be, the bound alone decides.
No kernel may reach another device: no remote copies, remote signals or barrier semaphores. Data moves between devices by JAX's collectives and lax.ppermute only.
A program may use at most 64 MiB of HBM per device.

v0:
```python
import functools

import jax
import jax.numpy as jnp
from jax import lax
from jax.experimental import pallas as pl
from jax.experimental.pallas import tpu as pltpu
from jax.sharding import PartitionSpec as P

AGG_LOC = 32
SWEEPS = 3
PAIRS = 8
ROWS = 16
LANES = 128
FULL = 7
THIN = 13
WIDE_ROWS = FULL * 16 + THIN * 8
NARROW_ROWS = FULL * 24 + THIN * 12
TX, TXW, TY, TYS, TZ, TZM, CENTRE, COUP, INV, RHS = 0, 1, 2, 3, 4, 5, 6, 7, 16, 19
N_COEF = 22
VMEM_LIMIT = 24 * 1024 * 1024

f32 = jnp.float32


def swap_halves(v):
    return pltpu.roll(v, 64, axis=1)


def shifted(v, offset, axis):
    return pltpu.roll(v, (-offset) % v.shape[axis], axis=axis)


def lane_index(shape):
    return lax.broadcasted_iota(jnp.int32, shape, 1)


def box_mask():
    row = lax.broadcasted_iota(jnp.int32, (ROWS, LANES), 0)
    return (row < 10) | (row >= 14)


def operate_pair(values, coef, pair, rolled):
    low = lane_index((ROWS, LANES)) < 64
    mids = [values[c, pair] for c in range(3)]

    def halves(c, p):
        if (c, p) not in rolled:
            rolled[c, p] = swap_halves(values[c, p])
        return rolled[c, p]

    out = []
    for c in range(3):
        v = mids[c]
        own = halves(c, pair)
        inflow = coef[TX, pair - 1] * jnp.where(low, own, halves(c, pair + 1))
        inflow += coef[TXW, pair - 1] * jnp.where(low, halves(c, pair - 1), own)
        inflow += coef[TY, pair - 1] * shifted(v, 1, 0)
        inflow += coef[TYS, pair - 1] * shifted(v, -1, 0)
        inflow += coef[TZ, pair - 1] * shifted(v, 1, 1)
        inflow += coef[TZM, pair - 1] * shifted(v, -1, 1)
        total = coef[CENTRE, pair - 1] * v
        for b in range(3):
            total += coef[COUP + 3 * c + b, pair - 1] * mids[b]
        out.append(total - inflow)
    return out


def add_wells_and_pack(cells, index, accum, trans, start, agg, coupling, rhs, accum_w, east, west):
    where_row = (lax.broadcasted_iota(jnp.int32, (32, 64), 0) == cells[...] // LANES).astype(f32)
    lane_no = lax.broadcasted_iota(jnp.int32, (LANES, 64), 0)
    share = jnp.where(lane_no == cells[...] % LANES, index[...], 0.0)
    added = lax.dot_general(
        where_row, share, (((1,), (1,)), ((), ())), precision=lax.Precision.HIGHEST, preferred_element_type=f32
    )
    for p in range(4):
        accum_w[p] = accum[p] + added[8 * p : 8 * p + 8]
    for out, first, thin in ((east, 2, 3), (west, 0, 0)):
        for f in range(FULL):
            for p in range(2):
                if f < 3:
                    value = trans[f, first + p]
                elif f < 6:
                    value = start[f - 3, first + p]
                else:
                    value = agg[first + p].astype(f32)
                out[f * 16 + p * 8 : f * 16 + p * 8 + 8] = value
        for t in range(THIN):
            at = FULL * 16 + t * 8
            if t == 0:
                value = accum_w[thin]
            elif t < 10:
                value = coupling[(t - 1) // 3, (t - 1) % 3, thin]
            else:
                value = rhs[t - 10, thin]
            out[at : at + 8] = value


def pack_narrow(from_west, from_east, accum_w, trans, start, agg, coupling, rhs, north, south):
    def rows_of_full(f, a):
        if a < 2:
            return from_west[f * 16 + a * 8 : f * 16 + a * 8 + 8]
        if a >= 6:
            return from_east[f * 16 + (a - 6) * 8 : f * 16 + (a - 6) * 8 + 8]
        if f < 3:
            return trans[f, a - 2]
        if f < 6:
            return start[f - 3, a - 2]
        return agg[a - 2].astype(f32)

    def rows_of_thin(t, a):
        at = FULL * 16 + t * 8
        if a < 2:
            return from_west[at : at + 8]
        if a >= 6:
            return from_east[at : at + 8]
        if t == 0:
            return accum_w[a - 2]
        if t < 10:
            return coupling[(t - 1) // 3, (t - 1) % 3, a - 2]
        return rhs[t - 10, a - 2]

    for f in range(FULL):
        for a in range(8):
            v = rows_of_full(f, a)
            at = (f * 8 + a) * 3
            north[at : at + 3] = v[5:8]
            south[at : at + 3] = v[0:3]
    for t in range(THIN):
        for a in range(1, 7):
            v = rows_of_thin(t, a)
            at = FULL * 24 + (t * 6 + a - 1) * 2
            north[at : at + 2] = v[6:8]
            south[at : at + 2] = v[0:2]


def pack_current(current, from_west, from_east, north, south):
    for c in range(3):
        for a in range(8):
            v = from_west[c, a] if a < 2 else from_east[c, a - 6] if a >= 6 else current[c, a - 2]
            at = (c * 8 + a) * 3
            north[at : at + 3] = v[5:8]
            south[at : at + 3] = v[0:3]


def coarse_part(misfit0, agg, coarse, sums, spread, payload):
    for g in range(AGG_LOC):
        picked = jnp.where(agg[0] == g, misfit0[0], 0.0)
        for p in range(1, 4):
            picked += jnp.where(agg[p] == g, misfit0[p], 0.0)
        sums[g : g + 1, :] = jnp.sum(picked, axis=0, keepdims=True)
    weight = jnp.broadcast_to(jnp.sum(sums[...], axis=1, keepdims=True), (AGG_LOC, LANES))
    count = coarse.shape[1] // LANES
    for w in range(count):
        row = jnp.sum(coarse[:, w * LANES : (w + 1) * LANES] * weight, axis=0, keepdims=True)
        spread[1, w + 1 : w + 2, :] = row
    middle = spread[1, 1 : count + 1, :]
    for n in range(4):
        turned = middle if n == 1 else shifted(middle, 32 * (n - 1), 1)
        if n != 1:
            spread[n, 1 : count + 1, :] = turned
        spread[n, 0:1, :] = turned[count - 1 : count]
        spread[n, count + 1 : count + 2, :] = turned[0:1]
    for w in range(count):
        for n in range(4):
            payload[w * 4 + n] = spread[n, w : w + 3, :]


def misfit_part(values, coef, agg, coarse, misfit, payload, sums, spread):
    inside = box_mask()
    rolled = {}
    for c in range(3):
        misfit[c, 0] = jnp.zeros((ROWS, LANES), f32)
        misfit[c, 7] = jnp.zeros((ROWS, LANES), f32)
    for a in range(1, 7):
        applied = operate_pair(values, coef, a, rolled)
        for c in range(3):
            misfit[c, a] = jnp.where(inside, coef[RHS + c, a - 1] - applied[c], 0.0)
    coarse_part([misfit[0, a, 0:8] for a in range(2, 6)], agg, coarse, sums, spread, payload)


def first_misfit(
    from_west,
    from_east,
    from_south,
    from_north,
    accum_w,
    trans,
    start,
    agg,
    coupling,
    rhs,
    coarse,
    coef,
    slots,
    misfit,
    payload,
    rim,
    values,
    sums,
    spread,
):
    blank = jnp.zeros((ROWS, LANES), f32)

    def place(target, rows, at_north, at_south, width):
        target[...] = blank
        target[0:8] = rows
        target[8 : 8 + width] = from_north[at_north : at_north + width]
        target[16 - width : 16] = from_south[at_south : at_south + width]

    for f in range(FULL):
        for a in range(8):
            if a < 2:
                rows = from_west[f * 16 + a * 8 : f * 16 + a * 8 + 8]
            elif a >= 6:
                rows = from_east[f * 16 + (a - 6) * 8 : f * 16 + (a - 6) * 8 + 8]
            elif f < 3:
                rows = trans[f, a - 2]
            elif f < 6:
                rows = start[f - 3, a - 2]
            else:
                rows = agg[a - 2].astype(f32)
            at = (f * 8 + a) * 3
            target = values.at[f - 3, a] if 3 <= f < 6 else rim.at[f if f < 3 else 3, a]
            place(target, rows, at, at, 3)
    for t in range(THIN):
        for a in range(1, 7):
            at = FULL * 16 + t * 8
            if a < 2:
                rows = from_west[at : at + 8]
            elif a >= 6:
                rows = from_east[at : at + 8]
            elif t == 0:
                rows = accum_w[a - 2]
            elif t < 10:
                rows = coupling[(t - 1) // 3, (t - 1) % 3, a - 2]
            else:
                rows = rhs[t - 10, a - 2]
            at = FULL * 24 + (t * 6 + a - 1) * 2
            target = coef.at[CENTRE if t == 0 else COUP + t - 1 if t < 10 else RHS + t - 10, a - 1]
            place(target, rows, at, at, 2)
    row = lax.broadcasted_iota(jnp.int32, (ROWS, LANES), 0)
    lane = lane_index((ROWS, LANES))
    low = lane < 64
    offset = jnp.where(row < 8, 32, jnp.where(row < 12, 64, 0))
    inside = box_mask()
    for a in range(8):
        slots[a] = rim[3, a].astype(jnp.int32) + offset
    for a in range(1, 7):
        tx, ty = rim[0, a], rim[1, a]
        tz = jnp.where((lane % 64) < 63, rim[2, a], 0.0)
        txw = jnp.where(low, swap_halves(rim[0, a - 1]), swap_halves(tx))
        tys = shifted(ty, -1, 0)
        tzm = shifted(tz, -1, 1)
        centre = coef[CENTRE, a - 1] + (tx + txw + ty + tys + tz + tzm)
        coef[TX, a - 1] = tx
        coef[TXW, a - 1] = txw
        coef[TY, a - 1] = ty
        coef[TYS, a - 1] = tys
        coef[TZ, a - 1] = tz
        coef[TZM, a - 1] = tzm
        coef[CENTRE, a - 1] = centre
        for c in range(3):
            diagonal = jnp.where(inside, centre + coef[COUP + 4 * c, a - 1], 1.0)
            coef[INV + c, a - 1] = jnp.where(inside, 1.0 / diagonal, 0.0)
    misfit_part(values, coef, agg, coarse, misfit, payload, sums, spread)


def gather_values(current, from_west, from_east, from_south, from_north, received, slots, values):
    total = jnp.sum(received[...], axis=0)
    blank = jnp.zeros((2, LANES), f32)
    for a in range(8):
        block = 0 if a < 2 else 2 if a >= 6 else 1
        table = jnp.broadcast_to(total[block : block + 1], (8, LANES))
        for c in range(3):
            rows = from_west[c, a] if a < 2 else from_east[c, a - 6] if a >= 6 else current[c, a - 2]
            at = (c * 8 + a) * 3
            values[c, a, 0:8] = rows
            values[c, a, 8:11] = from_north[at : at + 3]
            values[c, a, 11:13] = blank
            values[c, a, 13:16] = from_south[at : at + 3]
        for half in range(2):
            where = slots[a, 8 * half : 8 * half + 8]
            lifted = jnp.take_along_axis(table, where, axis=1, mode="promise_in_bounds")
            values[0, a, 8 * half : 8 * half + 8] += lifted


def next_misfit(
    current,
    from_west,
    from_east,
    from_south,
    from_north,
    received,
    slots,
    coef,
    agg,
    coarse,
    moved,
    misfit,
    payload,
    values,
    sums,
    spread,
):
    gather_values(current, from_west, from_east, from_south, from_north, received, slots, values)
    for c in range(3):
        for p in range(4):
            moved[c, p] = values[c, p + 2, 0:8]
    misfit_part(values, coef, agg, coarse, misfit, payload, sums, spread)


def last_misfit(
    current, from_west, from_east, from_south, from_north, received, slots, coef, iterate, residual, values
):
    gather_values(current, from_west, from_east, from_south, from_north, received, slots, values)
    rolled = {}
    for a in range(2, 6):
        applied = operate_pair(values, coef, a, rolled)
        for c in range(3):
            iterate[c, a - 2] = values[c, a, 0:8]
            residual[c, a - 2] = (coef[RHS + c, a - 1] - applied[c])[0:8]


def local_solve(misfit, coef, current, factors, moved, one, two):
    own_cols = list(range(8))
    row8 = lax.broadcasted_iota(jnp.int32, (24, LANES), 0) % 8

    def tiles(values, pair, cols, half):
        scaled = [coef[INV + c, pair - 1, 8 * half : 8 * half + 8] * values[c] for c in range(3)]
        left = jnp.concatenate(scaled, axis=0).astype(jnp.bfloat16)
        total = jnp.zeros((24, LANES), f32)
        for y in cols:
            product = lax.dot_general(
                left, factors[pair - 1, y + 2], (((1,), (1,)), ((), ())), preferred_element_type=f32
            )
            total = jnp.where(row8 == y % 8, product, total)
        return [total[8 * c : 8 * c + 8] for c in range(3)]

    blank = jnp.zeros((ROWS, LANES), f32)
    for c in range(3):
        for ref in (one, two):
            ref[c, 0] = blank
            ref[c, 7] = blank
    for a in range(1, 7):
        edge = a in (1, 6)
        for half, cols in ((0, own_cols), (1, [8, -1] if edge else [8, 9, -2, -1])):
            part = tiles([misfit[c, a, 8 * half : 8 * half + 8] for c in range(3)], a, cols, half)
            for c in range(3):
                one[c, a, 8 * half : 8 * half + 8] = part[c]
    rolled = {}
    for a in range(1, 7):
        edge = a in (1, 6)
        applied = operate_pair(one, coef, a, rolled)
        left = [misfit[c, a] - applied[c] for c in range(3)]
        for half, cols in ((0, own_cols), (1, [] if edge else [8, -1])):
            if not cols:
                for c in range(3):
                    two[c, a, 8:16] = one[c, a, 8:16]
                continue
            part = tiles([v[8 * half : 8 * half + 8] for v in left], a, cols, half)
            for c in range(3):
                two[c, a, 8 * half : 8 * half + 8] = one[c, a, 8 * half : 8 * half + 8] + part[c]
    rolled = {}
    for a in range(2, 6):
        applied = operate_pair(two, coef, a, rolled)
        part = tiles([(misfit[c, a] - applied[c])[0:8] for c in range(3)], a, own_cols, 0)
        for c in range(3):
            moved[c, a - 2] = current[c, a - 2] + (two[c, a, 0:8] + part[c])


def call(body, name, outs, scratch, *operands, flops=1000000):
    vmem = pl.BlockSpec(memory_space=pltpu.VMEM)
    return pl.pallas_call(
        body,
        out_shape=[jax.ShapeDtypeStruct(shape, dtype) for shape, dtype in outs],
        in_specs=[vmem] * len(operands),
        out_specs=[vmem] * len(outs),
        scratch_shapes=[pltpu.VMEM(shape, f32) for shape in scratch],
        compiler_params=pltpu.CompilerParams(vmem_limit_bytes=VMEM_LIMIT),
        cost_estimate=pl.CostEstimate(flops=flops, bytes_accessed=0, transcendentals=0),
        name=name,
    )(*operands)


def both_ways(axis, up, down):
    count = lax.axis_size(axis)
    from_previous = lax.ppermute(up, axis, [(i, (i + 1) % count) for i in range(count)])
    from_next = lax.ppermute(down, axis, [((i + 1) % count, i) for i in range(count)])
    return from_previous, from_next


def per_device(
    rhs, start, trans, accum, coupling, well_cells, well_index, agg_map, tile_factors, coarse_inverse
):
    devices = lax.axis_size("wide") * lax.axis_size("narrow")
    spread = ((4, devices // 4 + 8, LANES), (AGG_LOC, LANES))
    own = ((3, 4, 8, LANES), f32)
    box = ((3, PAIRS, ROWS, LANES), f32)
    payload_type = ((devices, 3, LANES), f32)
    narrow_type = ((72, LANES), f32)

    accum_w, east, west = call(
        add_wells_and_pack,
        "pack_wide",
        [((4, 8, LANES), f32), ((WIDE_ROWS, LANES), f32), ((WIDE_ROWS, LANES), f32)],
        [],
        well_cells.reshape(1, -1),
        well_index.reshape(1, -1),
        accum,
        trans,
        start,
        agg_map,
        coupling,
        rhs,
    )
    from_west, from_east = both_ways("wide", east, west)
    mine = (accum_w, trans, start, agg_map, coupling, rhs)
    north, south = call(
        pack_narrow,
        "pack_narrow",
        [((NARROW_ROWS, LANES), f32)] * 2,
        [],
        from_west,
        from_east,
        *mine,
    )
    from_south, from_north = both_ways("narrow", north, south)
    coef, slots, misfit, payload = call(
        first_misfit,
        "first_misfit",
        [((N_COEF, 6, ROWS, LANES), f32), ((PAIRS, ROWS, LANES), jnp.int32), box, payload_type],
        [(4, PAIRS, ROWS, LANES), (3, PAIRS, ROWS, LANES), spread[1], spread[0]],
        from_west,
        from_east,
        from_south,
        from_north,
        *mine,
        coarse_inverse,
    )
    current = start
    for sweep in range(SWEEPS):
        received = lax.all_to_all(payload, ("wide", "narrow"), 0, 0)
        (current,) = call(
            local_solve, "local_solve", [own], [box[0], box[0]], misfit, coef, current, tile_factors, flops=30000000
        )
        from_west, from_east = both_ways("wide", current[:, 2:4], current[:, 0:2])
        north, south = call(
            pack_current, "pack_current", [narrow_type] * 2, [], current, from_west, from_east
        )
        from_south, from_north = both_ways("narrow", north, south)
        known = (current, from_west, from_east, from_south, from_north, received, slots, coef)
        if sweep < SWEEPS - 1:
            current, misfit, payload = call(
                next_misfit,
                "next_misfit",
                [own, box, payload_type],
                [box[0], spread[1], spread[0]],
                *known,
                agg_map,
                coarse_inverse,
            )
        else:
            iterate, residual = call(last_misfit, "last_misfit", [own, own], [box[0]], *known)
    return iterate, residual


def solution(mesh):
    return jax.shard_map(
        per_device,
        mesh=mesh,
        in_specs=(
            P(None, "wide", "narrow", None),
            P(None, "wide", "narrow", None),
            P(None, "wide", "narrow", None),
            P("wide", "narrow", None),
            P(None, None, "wide", "narrow", None),
            P("wide", "narrow", None),
            P("wide", "narrow", None),
            P("wide", "narrow", None),
            P("wide", "narrow", None, None),
            P(("wide", "narrow"), None),
        ),
        out_specs=(P(None, "wide", "narrow", None), P(None, "wide", "narrow", None)),
        check_vma=False,
    )
```

profile of v0, /device:TPU:1, one launch (start us, length us, event | category | flops | bytes accessed | tf_op | source)
XLA Modules:
  0.0 165.5 jit_solution(3202997408605228962)
XLA Ops:
  7.1 3.6 %collective-permute-start = (f32[216,128]{1,0:T(8,128)S(1)}, f32[216,128]{1,0:T(8,128)S(1)}, u32[]{:S(2)}, u32[]{:S(2)}) collective-permute-start(f32[216,128]{1,0:T(8,128)S(1)} %get-tuple-element.23), channel_id=1, source_target_pairs={{0,4},{4,8},{8,12},{12,16},{16,20},{20,24},{24,28},{28,32},{32,36}... | collective-permute-start | bytes 331784 | tf_op jit(solution)/shard_map/ppermute | solution.py:388
  10.6 7.8 %collective-permute-start.1 = (f32[216,128]{1,0:T(8,128)S(1)}, f32[216,128]{1,0:T(8,128)S(1)}, u32[]{:S(2)}, u32[]{:S(2)}) collective-permute-start(f32[216,128]{1,0:T(8,128)S(1)} %get-tuple-element.24), channel_id=1, source_target_pairs={{4,0},{8,4},{12,8},{16,12},{20,16},{24,20},{28,24},{32,28},{36,32}... | collective-permute-start | bytes 331784 | tf_op jit(solution)/shard_map/ppermute | solution.py:389
  18.5 2.7 %collective-permute-done.from_west = f32[216,128]{1,0:T(8,128)S(1)} collective-permute-done((f32[216,128]{1,0:T(8,128)S(1)}, f32[216,128]{1,0:T(8,128)S(1)}, u32[]{:S(2)}, u32[]{:S(2)}) %collective-permute-start) | collective-permute-done | bytes 110624 | tf_op jit(solution)/shard_map/ppermute | solution.py:388
  24.6 2.3 %collective-permute-done.2.from_south = f32[324,128]{1,0:T(8,128)S(1)} collective-permute-done((f32[324,128]{1,0:T(8,128)S(1)}, f32[324,128]{1,0:T(8,128)S(1)}, u32[]{:S(2)}, u32[]{:S(2)}) %collective-permute-start.2) | collective-permute-done | bytes 165920 | tf_op jit(solution)/shard_map/ppermute | solution.py:388
  26.9 3.4 %collective-permute-done.3.from_north = f32[324,128]{1,0:T(8,128)S(1)} collective-permute-done((f32[324,128]{1,0:T(8,128)S(1)}, f32[324,128]{1,0:T(8,128)S(1)}, u32[]{:S(2)}, u32[]{:S(2)}) %collective-permute-start.3) | collective-permute-done | bytes 165920 | tf_op jit(solution)/shard_map/ppermute | solution.py:389
  36.6 11.2 %all-to-all-start = ((f32[256,3,128]{2,1,0:T(4,128)}), f32[256,3,128]{2,1,0:T(4,128)}, u32[]{:S(2)}, u32[]{:S(2)}) async-start(f32[256,3,128]{2,1,0:T(4,128)} %copy-done.12), calls=%async_computation | async-start | bytes 1048576 | tf_op jit(solution)/shard_map/all_to_all | solution.py:443
  48.7 2.8 %local_solve.3.current = f32[3,4,8,128]{3,2,1,0:T(8,128)S(1)} custom-call(f32[3,8,16,128]{3,2,1,0:T(8,128)S(1)} %copy-done.24, f32[22,6,16,128]{3,2,1,0:T(8,128)S(1)} %get-tuple-element.29.coef, f32[3,4,8,128]{3,2,1,0:T(8,128)S(1)} %copy-done.8, bf16[6,12,128,128]{3,2,1,0:T(8,128)(2,1)S(1)} %copy-done), custom_call_target="tpu_custom_call" | custom-call | flops 30000000 | tf_op jit(solution)/shard_map/local_solve/pallas_call | solution.py:374
  51.5 9.1 %collective-permute-start.5 = (f32[3,2,8,128]{3,2,1,0:T(8,128)S(1)}, f32[3,2,8,128]{3,2,1,0:T(8,128)S(1)}, u32[]{:S(2)}, u32[]{:S(2)}) collective-permute-start(f32[3,2,8,128]{3,2,1,0:T(8,128)S(1)} %get-tuple-element.48), channel_id=1, source_target_pairs={{4,0},{8,4},{12,8},{16,12},{20,16},{24,20},{28,24},{32,28},{36,32}... | collective-permute-start | bytes 73736 | tf_op jit(solution)/shard_map/ppermute | solution.py:389
  61.6 7.6 %collective-permute-done.4.from_west = f32[3,2,8,128]{3,2,1,0:T(8,128)S(1)} collective-permute-done((f32[3,2,8,128]{3,2,1,0:T(8,128)S(1)}, f32[3,2,8,128]{3,2,1,0:T(8,128)S(1)}, u32[]{:S(2)}, u32[]{:S(2)}) %collective-permute-start.4) | collective-permute-done | bytes 24608 | tf_op jit(solution)/shard_map/ppermute | solution.py:388
  69.2 2.1 %collective-permute-start.6 = (f32[72,128]{1,0:T(8,128)S(1)}, f32[72,128]{1,0:T(8,128)S(1)}, u32[]{:S(2)}, u32[]{:S(2)}) collective-permute-start(f32[72,128]{1,0:T(8,128)S(1)} %get-tuple-element.30), channel_id=1, source_target_pairs={{0,1},{1,2},{2,3},{3,0},{4,5},{5,6},{6,7},{7,4},{8,9},{9,10},{10,1... | collective-permute-start | bytes 110600 | tf_op jit(solution)/shard_map/ppermute | solution.py:388
  78.9 2.0 %next_misfit.2 = (f32[3,4,8,128]{3,2,1,0:T(8,128)S(1)}, f32[3,8,16,128]{3,2,1,0:T(8,128)S(1)}, f32[256,3,128]{2,1,0:T(4,128)S(1)}) custom-call(f32[3,4,8,128]{3,2,1,0:T(8,128)S(1)} %local_solve.3.current, f32[3,2,8,128]{3,2,1,0:T(8,128)S(1)} %collective-permute-done.4.from_west, f32[3,2,8,128]{3,2,1,0:T(8,128)S(1)} %collective-permute-done.5.from_east, ...), custom_call_target="tpu_custom_call" | custom-call | flops 1000000 | tf_op jit(solution)/shard_map/next_misfit/pallas_call | solution.py:374
  82.9 7.2 %all-to-all-start.1 = ((f32[256,3,128]{2,1,0:T(4,128)}), f32[256,3,128]{2,1,0:T(4,128)}, u32[]{:S(2)}, u32[]{:S(2)}) async-start(f32[256,3,128]{2,1,0:T(4,128)} %copy-done.13), calls=%async_computation.1 | async-start | bytes 1048576 | tf_op jit(solution)/shard_map/all_to_all | solution.py:443
  91.8 2.8 %local_solve.4.current = f32[3,4,8,128]{3,2,1,0:T(8,128)S(1)} custom-call(f32[3,8,16,128]{3,2,1,0:T(8,128)S(1)} %copy-done.26, f32[22,6,16,128]{3,2,1,0:T(8,128)S(1)} %get-tuple-element.29.coef, f32[3,4,8,128]{3,2,1,0:T(8,128)S(1)} %copy-done.34, bf16[6,12,128,128]{3,2,1,0:T(8,128)(2,1)S(1)} %copy-done), custom_call_target="tpu_custom_call" | custom-call | flops 30000000 | tf_op jit(solution)/shard_map/local_solve/pallas_call | solution.py:374
  94.6 9.3 %collective-permute-start.9 = (f32[3,2,8,128]{3,2,1,0:T(8,128)S(1)}, f32[3,2,8,128]{3,2,1,0:T(8,128)S(1)}, u32[]{:S(2)}, u32[]{:S(2)}) collective-permute-start(f32[3,2,8,128]{3,2,1,0:T(8,128)S(1)} %get-tuple-element.46), channel_id=1, source_target_pairs={{4,0},{8,4},{12,8},{16,12},{20,16},{24,20},{28,24},{32,28},{36,32}... | collective-permute-start | bytes 73736 | tf_op jit(solution)/shard_map/ppermute | solution.py:389
  104.8 7.5 %collective-permute-done.8.from_west = f32[3,2,8,128]{3,2,1,0:T(8,128)S(1)} collective-permute-done((f32[3,2,8,128]{3,2,1,0:T(8,128)S(1)}, f32[3,2,8,128]{3,2,1,0:T(8,128)S(1)}, u32[]{:S(2)}, u32[]{:S(2)}) %collective-permute-start.8) | collective-permute-done | bytes 24608 | tf_op jit(solution)/shard_map/ppermute | solution.py:388
  113.5 2.0 %collective-permute-start.10 = (f32[72,128]{1,0:T(8,128)S(1)}, f32[72,128]{1,0:T(8,128)S(1)}, u32[]{:S(2)}, u32[]{:S(2)}) collective-permute-start(f32[72,128]{1,0:T(8,128)S(1)} %get-tuple-element.36), channel_id=1, source_target_pairs={{0,1},{1,2},{2,3},{3,0},{4,5},{5,6},{6,7},{7,4},{8,9},{9,10},{10,1... | collective-permute-start | bytes 110600 | tf_op jit(solution)/shard_map/ppermute | solution.py:388
  124.5 2.0 %next_misfit.3 = (f32[3,4,8,128]{3,2,1,0:T(8,128)S(1)}, f32[3,8,16,128]{3,2,1,0:T(8,128)S(1)}, f32[256,3,128]{2,1,0:T(4,128)S(1)}) custom-call(f32[3,4,8,128]{3,2,1,0:T(8,128)S(1)} %local_solve.4.current, f32[3,2,8,128]{3,2,1,0:T(8,128)S(1)} %copy-done.32, f32[3,2,8,128]{3,2,1,0:T(8,128)S(1)} %copy-done.30, f32[72,128]{1,0:T(8,128)S(1)} %copy-done.40, ...), custom_call_target="tpu_custom_call" | custom-call | flops 1000000 | tf_op jit(solution)/shard_map/next_misfit/pallas_call | solution.py:374
  128.5 7.1 %all-to-all-start.2 = ((f32[256,3,128]{2,1,0:T(4,128)}), f32[256,3,128]{2,1,0:T(4,128)}, u32[]{:S(2)}, u32[]{:S(2)}) async-start(f32[256,3,128]{2,1,0:T(4,128)} %copy-done.14), calls=%async_computation.2 | async-start | bytes 1048576 | tf_op jit(solution)/shard_map/all_to_all | solution.py:443
  137.4 2.8 %local_solve.5.current = f32[3,4,8,128]{3,2,1,0:T(8,128)S(1)} custom-call(f32[3,8,16,128]{3,2,1,0:T(8,128)S(1)} %copy-done.28, f32[22,6,16,128]{3,2,1,0:T(8,128)S(1)} %get-tuple-element.29.coef, f32[3,4,8,128]{3,2,1,0:T(8,128)S(1)} %copy-done.36, bf16[6,12,128,128]{3,2,1,0:T(8,128)(2,1)S(1)} %copy-done), custom_call_target="tpu_custom_call" | custom-call | flops 30000000 | tf_op jit(solution)/shard_map/local_solve/pallas_call | solution.py:374
  140.2 9.3 %collective-permute-start.13 = (f32[3,2,8,128]{3,2,1,0:T(8,128)S(1)}, f32[3,2,8,128]{3,2,1,0:T(8,128)S(1)}, u32[]{:S(2)}, u32[]{:S(2)}) collective-permute-start(f32[3,2,8,128]{3,2,1,0:T(8,128)S(1)} %get-tuple-element.44), channel_id=1, source_target_pairs={{4,0},{8,4},{12,8},{16,12},{20,16},{24,20},{28,24},{32,28},{36,32}... | collective-permute-start | bytes 73736 | tf_op jit(solution)/shard_map/ppermute | solution.py:389
  150.4 7.5 %collective-permute-done.12.from_west = f32[3,2,8,128]{3,2,1,0:T(8,128)S(1)} collective-permute-done((f32[3,2,8,128]{3,2,1,0:T(8,128)S(1)}, f32[3,2,8,128]{3,2,1,0:T(8,128)S(1)}, u32[]{:S(2)}, u32[]{:S(2)}) %collective-permute-start.12) | collective-permute-done | bytes 24608 | tf_op jit(solution)/shard_map/ppermute | solution.py:388
  158.0 2.1 %collective-permute-start.14 = (f32[72,128]{1,0:T(8,128)S(1)}, f32[72,128]{1,0:T(8,128)S(1)}, u32[]{:S(2)}, u32[]{:S(2)}) collective-permute-start(f32[72,128]{1,0:T(8,128)S(1)} %get-tuple-element.41), channel_id=1, source_target_pairs={{0,1},{1,2},{2,3},{3,0},{4,5},{5,6},{6,7},{7,4},{8,9},{9,10},{10,1... | collective-permute-start | bytes 110600 | tf_op jit(solution)/shard_map/ppermute | solution.py:388
  161.1 2.3 %collective-permute-done.15.from_north = f32[72,128]{1,0:T(8,128)S(1)} collective-permute-done((f32[72,128]{1,0:T(8,128)S(1)}, f32[72,128]{1,0:T(8,128)S(1)}, u32[]{:S(2)}, u32[]{:S(2)}) %collective-permute-start.15) | collective-permute-done | bytes 36896 | tf_op jit(solution)/shard_map/ppermute | solution.py:389
  163.4 2.1 %last_misfit.1 = (f32[3,4,8,128]{3,2,1,0:T(8,128)}, f32[3,4,8,128]{3,2,1,0:T(8,128)}) custom-call(f32[3,4,8,128]{3,2,1,0:T(8,128)S(1)} %local_solve.5.current, f32[3,2,8,128]{3,2,1,0:T(8,128)S(1)} %collective-permute-done.12.from_west, f32[3,2,8,128]{3,2,1,0:T(8,128)S(1)} %collective-permute-done.13.from_east, ...), custom_call_target="tpu_custom_call" | custom-call | flops 1000000 | tf_op jit(solution)/shard_map/last_misfit/pallas_call | solution.py:374
  (125 shorter events, 46.4 us)
Async XLA Ops:
  0.6 47.2 %copy-start = (bf16[6,12,128,128]{3,2,1,0:T(8,128)(2,1)S(1)}, bf16[6,12,128,128]{3,2,1,0:T(8,128)(2,1)}, u32[]{:S(2)}) copy-start(bf16[6,12,128,128]{3,2,1,0:T(8,128)(2,1)} %factors.5) | copy-start | bytes 7077892
  7.1 14.1 %collective-permute-start = (f32[216,128]{1,0:T(8,128)S(1)}, f32[216,128]{1,0:T(8,128)S(1)}, u32[]{:S(2)}, u32[]{:S(2)}) collective-permute-start(f32[216,128]{1,0:T(8,128)S(1)} %get-tuple-element.23), channel_id=1, source_target_pairs={{0,4},{4,8},{8,12},{12,16},{16,20},{20,24},{24,28},{28,32},{32,36}... | collective-permute-start | bytes 331784 | tf_op jit(solution)/shard_map/ppermute | solution.py:388
  10.6 10.5 %collective-permute-start.1 = (f32[216,128]{1,0:T(8,128)S(1)}, f32[216,128]{1,0:T(8,128)S(1)}, u32[]{:S(2)}, u32[]{:S(2)}) collective-permute-start(f32[216,128]{1,0:T(8,128)S(1)} %get-tuple-element.24), channel_id=1, source_target_pairs={{4,0},{8,4},{12,8},{16,12},{20,16},{24,20},{28,24},{32,28},{36,32}... | collective-permute-start | bytes 331784 | tf_op jit(solution)/shard_map/ppermute | solution.py:389
  22.9 3.9 %collective-permute-start.2 = (f32[324,128]{1,0:T(8,128)S(1)}, f32[324,128]{1,0:T(8,128)S(1)}, u32[]{:S(2)}, u32[]{:S(2)}) collective-permute-start(f32[324,128]{1,0:T(8,128)S(1)} %get-tuple-element.26), channel_id=1, source_target_pairs={{0,1},{1,2},{2,3},{3,0},{4,5},{5,6},{6,7},{7,4},{8,9},{9,10},{10,1... | collective-permute-start | bytes 497672 | tf_op jit(solution)/shard_map/ppermute | solution.py:388
  24.6 5.7 %collective-permute-start.3 = (f32[324,128]{1,0:T(8,128)S(1)}, f32[324,128]{1,0:T(8,128)S(1)}, u32[]{:S(2)}, u32[]{:S(2)}) collective-permute-start(f32[324,128]{1,0:T(8,128)S(1)} %get-tuple-element.27), channel_id=1, source_target_pairs={{1,0},{2,1},{3,2},{0,3},{5,4},{6,5},{7,6},{4,7},{9,8},{10,9},{11,1... | collective-permute-start | bytes 497672 | tf_op jit(solution)/shard_map/ppermute | solution.py:389
  33.8 14.0 %copy-start.8 = (f32[3,4,8,128]{3,2,1,0:T(8,128)S(1)}, f32[3,4,8,128]{3,2,1,0:T(8,128)}, u32[]{:S(2)}) copy-start(f32[3,4,8,128]{3,2,1,0:T(8,128)} %current.1) | copy-start | bytes 147460
  36.6 38.7 %copy-start.21 = (s32[4,8,128]{2,1,0:T(8,128)S(1)}, s32[4,8,128]{2,1,0:T(8,128)}, u32[]{:S(2)}) copy-start(s32[4,8,128]{2,1,0:T(8,128)} %agg.9) | copy-start | bytes 49156
  36.6 38.7 %all-to-all-start = ((f32[256,3,128]{2,1,0:T(4,128)}), f32[256,3,128]{2,1,0:T(4,128)}, u32[]{:S(2)}, u32[]{:S(2)}) async-start(f32[256,3,128]{2,1,0:T(4,128)} %copy-done.12), calls=%async_computation | async-start | bytes 1048576 | tf_op jit(solution)/shard_map/all_to_all | solution.py:443
  51.5 10.1 %collective-permute-start.5 = (f32[3,2,8,128]{3,2,1,0:T(8,128)S(1)}, f32[3,2,8,128]{3,2,1,0:T(8,128)S(1)}, u32[]{:S(2)}, u32[]{:S(2)}) collective-permute-start(f32[3,2,8,128]{3,2,1,0:T(8,128)S(1)} %get-tuple-element.48), channel_id=1, source_target_pairs={{4,0},{8,4},{12,8},{16,12},{20,16},{24,20},{28,24},{32,28},{36,32}... | collective-permute-start | bytes 73736 | tf_op jit(solution)/shard_map/ppermute | solution.py:389
  60.6 8.5 %collective-permute-start.4 = (f32[3,2,8,128]{3,2,1,0:T(8,128)S(1)}, f32[3,2,8,128]{3,2,1,0:T(8,128)S(1)}, u32[]{:S(2)}, u32[]{:S(2)}) collective-permute-start(f32[3,2,8,128]{3,2,1,0:T(8,128)S(1)} %get-tuple-element.49), channel_id=1, source_target_pairs={{0,4},{4,8},{8,12},{12,16},{16,20},{20,24},{24,28},{28,32},{32,36}... | collective-permute-start | bytes 73736 | tf_op jit(solution)/shard_map/ppermute | solution.py:388
  69.2 3.1 %collective-permute-start.6 = (f32[72,128]{1,0:T(8,128)S(1)}, f32[72,128]{1,0:T(8,128)S(1)}, u32[]{:S(2)}, u32[]{:S(2)}) collective-permute-start(f32[72,128]{1,0:T(8,128)S(1)} %get-tuple-element.30), channel_id=1, source_target_pairs={{0,1},{1,2},{2,3},{3,0},{4,5},{5,6},{6,7},{7,4},{8,9},{9,10},{10,1... | collective-permute-start | bytes 110600 | tf_op jit(solution)/shard_map/ppermute | solution.py:388
  71.2 3.4 %collective-permute-start.7 = (f32[72,128]{1,0:T(8,128)S(1)}, f32[72,128]{1,0:T(8,128)S(1)}, u32[]{:S(2)}, u32[]{:S(2)}) collective-permute-start(f32[72,128]{1,0:T(8,128)S(1)} %get-tuple-element.31), channel_id=1, source_target_pairs={{1,0},{2,1},{3,2},{0,3},{5,4},{6,5},{7,6},{4,7},{9,8},{10,9},{11,1... | collective-permute-start | bytes 110600 | tf_op jit(solution)/shard_map/ppermute | solution.py:389
  75.3 1.2 copy-start.2
  82.9 36.6 %copy-start.11 = (s32[8,16,128]{2,1,0:T(8,128)S(1)}, s32[8,16,128]{2,1,0:T(8,128)}, u32[]{:S(2)}) copy-start(s32[8,16,128]{2,1,0:T(8,128)} %copy-done.9) | copy-start | bytes 196612
  82.9 36.6 %all-to-all-start.1 = ((f32[256,3,128]{2,1,0:T(4,128)}), f32[256,3,128]{2,1,0:T(4,128)}, u32[]{:S(2)}, u32[]{:S(2)}) async-start(f32[256,3,128]{2,1,0:T(4,128)} %copy-done.13), calls=%async_computation.1 | async-start | bytes 1048576 | tf_op jit(solution)/shard_map/all_to_all | solution.py:443
  94.6 10.2 %collective-permute-start.9 = (f32[3,2,8,128]{3,2,1,0:T(8,128)S(1)}, f32[3,2,8,128]{3,2,1,0:T(8,128)S(1)}, u32[]{:S(2)}, u32[]{:S(2)}) collective-permute-start(f32[3,2,8,128]{3,2,1,0:T(8,128)S(1)} %get-tuple-element.46), channel_id=1, source_target_pairs={{4,0},{8,4},{12,8},{16,12},{20,16},{24,20},{28,24},{32,28},{36,32}... | collective-permute-start | bytes 73736 | tf_op jit(solution)/shard_map/ppermute | solution.py:389
  103.9 8.4 %collective-permute-start.8 = (f32[3,2,8,128]{3,2,1,0:T(8,128)S(1)}, f32[3,2,8,128]{3,2,1,0:T(8,128)S(1)}, u32[]{:S(2)}, u32[]{:S(2)}) collective-permute-start(f32[3,2,8,128]{3,2,1,0:T(8,128)S(1)} %get-tuple-element.47), channel_id=1, source_target_pairs={{0,4},{4,8},{8,12},{12,16},{16,20},{20,24},{24,28},{28,32},{32,36}... | collective-permute-start | bytes 73736 | tf_op jit(solution)/shard_map/ppermute | solution.py:388
  113.5 3.1 %collective-permute-start.10 = (f32[72,128]{1,0:T(8,128)S(1)}, f32[72,128]{1,0:T(8,128)S(1)}, u32[]{:S(2)}, u32[]{:S(2)}) collective-permute-start(f32[72,128]{1,0:T(8,128)S(1)} %get-tuple-element.36), channel_id=1, source_target_pairs={{0,1},{1,2},{2,3},{3,0},{4,5},{5,6},{6,7},{7,4},{8,9},{9,10},{10,1... | collective-permute-start | bytes 110600 | tf_op jit(solution)/shard_map/ppermute | solution.py:388
  115.5 3.4 %collective-permute-start.11 = (f32[72,128]{1,0:T(8,128)S(1)}, f32[72,128]{1,0:T(8,128)S(1)}, u32[]{:S(2)}, u32[]{:S(2)}) collective-permute-start(f32[72,128]{1,0:T(8,128)S(1)} %get-tuple-element.37), channel_id=1, source_target_pairs={{1,0},{2,1},{3,2},{0,3},{5,4},{6,5},{7,6},{4,7},{9,8},{10,9},{11,1... | collective-permute-start | bytes 110600 | tf_op jit(solution)/shard_map/ppermute | solution.py:389
  128.5 34.9 %all-to-all-start.2 = ((f32[256,3,128]{2,1,0:T(4,128)}), f32[256,3,128]{2,1,0:T(4,128)}, u32[]{:S(2)}, u32[]{:S(2)}) async-start(f32[256,3,128]{2,1,0:T(4,128)} %copy-done.14), calls=%async_computation.2 | async-start | bytes 1048576 | tf_op jit(solution)/shard_map/all_to_all | solution.py:443
  140.2 10.2 %collective-permute-start.13 = (f32[3,2,8,128]{3,2,1,0:T(8,128)S(1)}, f32[3,2,8,128]{3,2,1,0:T(8,128)S(1)}, u32[]{:S(2)}, u32[]{:S(2)}) collective-permute-start(f32[3,2,8,128]{3,2,1,0:T(8,128)S(1)} %get-tuple-element.44), channel_id=1, source_target_pairs={{4,0},{8,4},{12,8},{16,12},{20,16},{24,20},{28,24},{32,28},{36,32}... | collective-permute-start | bytes 73736 | tf_op jit(solution)/shard_map/ppermute | solution.py:389
  149.4 8.5 %collective-permute-start.12 = (f32[3,2,8,128]{3,2,1,0:T(8,128)S(1)}, f32[3,2,8,128]{3,2,1,0:T(8,128)S(1)}, u32[]{:S(2)}, u32[]{:S(2)}) collective-permute-start(f32[3,2,8,128]{3,2,1,0:T(8,128)S(1)} %get-tuple-element.45), channel_id=1, source_target_pairs={{0,4},{4,8},{8,12},{12,16},{16,20},{20,24},{24,28},{28,32},{32,36}... | collective-permute-start | bytes 73736 | tf_op jit(solution)/shard_map/ppermute | solution.py:388
  158.0 3.1 %collective-permute-start.14 = (f32[72,128]{1,0:T(8,128)S(1)}, f32[72,128]{1,0:T(8,128)S(1)}, u32[]{:S(2)}, u32[]{:S(2)}) collective-permute-start(f32[72,128]{1,0:T(8,128)S(1)} %get-tuple-element.41), channel_id=1, source_target_pairs={{0,1},{1,2},{2,3},{3,0},{4,5},{5,6},{6,7},{7,4},{8,9},{9,10},{10,1... | collective-permute-start | bytes 110600 | tf_op jit(solution)/shard_map/ppermute | solution.py:388
  160.0 3.4 %collective-permute-start.15 = (f32[72,128]{1,0:T(8,128)S(1)}, f32[72,128]{1,0:T(8,128)S(1)}, u32[]{:S(2)}, u32[]{:S(2)}) collective-permute-start(f32[72,128]{1,0:T(8,128)S(1)} %get-tuple-element.42), channel_id=1, source_target_pairs={{1,0},{2,1},{3,2},{0,3},{5,4},{6,5},{7,6},{4,7},{9,8},{10,9},{11,1... | collective-permute-start | bytes 110600 | tf_op jit(solution)/shard_map/ppermute | solution.py:389
  (43 other events, 33.2 us)
where the time goes:
time: 167 us; the launch traced here: 166 us
  starting transfers between devices  72.3 us (43%)
  waiting for transfers between devices  42.7 us (26%)
  local copies, waits for them, and re-layouts  34.4 us (21%)
  Pallas kernels  15.3 us (9%)
    ppermute x8, starting transfers between devices, both_ways(): lax.ppermute(down, axis, [((i + 1) % count, i) for i in range(count)])  35.5 us
    unnamed x96, local copies, waits for them, and re-layouts  34.3 us
    ppermute x8, waiting for transfers between devices, both_ways(): lax.ppermute(up, axis, [(i, (i + 1) % count) for i in range(count)])  30.7 us
    all_to_all x3, starting transfers between devices, per_device(): received = lax.all_to_all(payload, ('wide', 'narrow'), 0, 0)  25.5 us
    pallas_call x12, Pallas kernels, call(): pl.pallas_call(body, out_shape=[jax.ShapeDtypeStruct(shape, dtype) for sh...  15.3 us
    ppermute x8, waiting for transfers between devices, both_ways(): lax.ppermute(down, axis, [((i + 1) % count, i) for i in range(count)])  12 us
    ppermute x8, starting transfers between devices, both_ways(): lax.ppermute(up, axis, [(i, (i + 1) % count) for i in range(count)])  11.4 us
  transfers between devices with their start and end apart: 19, of which 15 were waited for; matrix products, arithmetic and copies ran while one was open for 0% of the time, Pallas kernels for 5%

commit v1 on v0

v1 whole, which is shorter than its diff:
```python
import functools

import jax
import jax.numpy as jnp
from jax import lax
from jax.experimental import pallas as pl
from jax.experimental.pallas import tpu as pltpu
from jax.sharding import PartitionSpec as P

AGG_LOC = 32
SWEEPS = 3
PAIRS = 8
ROWS = 16
LANES = 128
FULL = 7
THIN = 13
WIDE_ROWS = FULL * 16 + THIN * 8
NARROW_ROWS = FULL * 24 + THIN * 12
TX, TXW, TY, TYS, TZ, TZM, CENTRE, COUP, INV, RHS = 0, 1, 2, 3, 4, 5, 6, 7, 16, 19
N_COEF = 22
VMEM_LIMIT = 24 * 1024 * 1024

f32 = jnp.float32


def swap_halves(v):
    return pltpu.roll(v, 64, axis=1)


def shifted(v, offset, axis):
    return pltpu.roll(v, (-offset) % v.shape[axis], axis=axis)


def lane_index(shape):
    return lax.broadcasted_iota(jnp.int32, shape, 1)


def box_mask():
    row = lax.broadcasted_iota(jnp.int32, (ROWS, LANES), 0)
    return (row < 10) | (row >= 14)


def operate_pair(values, coef, pair, rolled):
    low = lane_index((ROWS, LANES)) < 64
    mids = [values[c, pair] for c in range(3)]

    def halves(c, p):
        if (c, p) not in rolled:
            rolled[c, p] = swap_halves(values[c, p])
        return rolled[c, p]

    out = []
    for c in range(3):
        v = mids[c]
        own = halves(c, pair)
        inflow = coef[TX, pair - 1] * jnp.where(low, own, halves(c, pair + 1))
        inflow += coef[TXW, pair - 1] * jnp.where(low, halves(c, pair - 1), own)
        inflow += coef[TY, pair - 1] * shifted(v, 1, 0)
        inflow += coef[TYS, pair - 1] * shifted(v, -1, 0)
        inflow += coef[TZ, pair - 1] * shifted(v, 1, 1)
        inflow += coef[TZM, pair - 1] * shifted(v, -1, 1)
        total = coef[CENTRE, pair - 1] * v
        for b in range(3):
            total += coef[COUP + 3 * c + b, pair - 1] * mids[b]
        out.append(total - inflow)
    return out


def pick(odd, when_odd, when_even):
    return jnp.where(odd, when_odd, when_even)


def is_odd(axis):
    return lax.axis_index(axis) % 2 == 1


def add_wells_and_pack(
    cells_in,
    index_in,
    accum,
    trans,
    start,
    agg,
    coupling,
    rhs,
    mine,
    agg_float,
    far,
    near,
    cells,
    index,
    accum_in,
    agg_in,
    sems,
):
    sources = (
        (cells_in, cells),
        (index_in, index),
        (agg, agg_in),
        (accum, accum_in),
        (trans, mine.at[0:3]),
        (start, mine.at[3:6]),
        (coupling, mine.at[8:17]),
        (rhs, mine.at[17:20]),
    )
    copies = [pltpu.make_async_copy(source, target, sems.at[i]) for i, (source, target) in enumerate(sources)]
    for copy in copies:
        copy.start()
    for copy in copies[:2]:
        copy.wait()
    where_row = (lax.broadcasted_iota(jnp.int32, (32, 64), 0) == cells[...] // LANES).astype(f32)
    lane_no = lax.broadcasted_iota(jnp.int32, (LANES, 64), 0)
    share = jnp.where(lane_no == cells[...] % LANES, index[...], 0.0)
    added = lax.dot_general(
        where_row, share, (((1,), (1,)), ((), ())), precision=lax.Precision.HIGHEST, preferred_element_type=f32
    )
    for copy in copies[2:]:
        copy.wait()
    for p in range(4):
        mine[7, p] = accum_in[p] + added[8 * p : 8 * p + 8]
        mine[6, p] = agg_in[p].astype(f32)
        agg_float[p] = agg_in[p].astype(f32)
    odd = is_odd("wide")
    for f in range(FULL):
        for p in range(2):
            east, west = mine[f, 2 + p], mine[f, p]
            at = f * 16 + p * 8
            far[at : at + 8] = pick(odd, east, west)
            near[at : at + 8] = pick(odd, west, east)
    for t in range(THIN):
        east, west = mine[FULL + t, 3], mine[FULL + t, 0]
        at = FULL * 16 + t * 8
        far[at : at + 8] = pick(odd, east, west)
        near[at : at + 8] = pick(odd, west, east)


def rim_rows(odd, far, near, mine, channel_no, at, depth, pair):
    if pair < 2:
        at += 8 * pair if depth == 2 else 0
        return pick(odd, near[at : at + 8], far[at : at + 8])
    if pair >= 6:
        at += 8 * (pair - 6) if depth == 2 else 0
        return pick(odd, far[at : at + 8], near[at : at + 8])
    return mine[channel_no, pair - 2]


def pack_narrow(far, near, mine, low, high):
    odd = is_odd("wide")
    narrow_odd = is_odd("narrow")
    for f in range(FULL):
        for a in range(8):
            v = rim_rows(odd, far, near, mine, f, f * 16, 2, a)
            at = (f * 8 + a) * 3
            low[at : at + 3] = pick(narrow_odd, v[5:8], v[0:3])
            high[at : at + 3] = pick(narrow_odd, v[0:3], v[5:8])
    for t in range(THIN):
        for a in range(1, 7):
            v = rim_rows(odd, far, near, mine, FULL + t, FULL * 16 + t * 8, 1, a)
            at = FULL * 24 + (t * 6 + a - 1) * 2
            low[at : at + 2] = pick(narrow_odd, v[6:8], v[0:2])
            high[at : at + 2] = pick(narrow_odd, v[0:2], v[6:8])


def pack_current(current, far, near, low, high):
    odd = is_odd("wide")
    narrow_odd = is_odd("narrow")
    for c in range(3):
        for a in range(8):
            v = rim_rows(odd, far, near, current, c, c * 16, 2, a)
            at = (c * 8 + a) * 3
            low[at : at + 3] = pick(narrow_odd, v[5:8], v[0:3])
            high[at : at + 3] = pick(narrow_odd, v[0:3], v[5:8])


def coarse_part(misfit0, agg, coarse, fetch, sums, spread, payload):
    for g in range(AGG_LOC):
        picked = jnp.where(agg[0] == float(g), misfit0[0], 0.0)
        for p in range(1, 4):
            picked += jnp.where(agg[p] == float(g), misfit0[p], 0.0)
        sums[g : g + 1, :] = jnp.sum(picked, axis=0, keepdims=True)
    weight = jnp.broadcast_to(jnp.sum(sums[...], axis=1, keepdims=True), (AGG_LOC, LANES))
    count = coarse.shape[1] // LANES
    fetch.wait()
    for w in range(count):
        row = jnp.sum(coarse[:, w * LANES : (w + 1) * LANES] * weight, axis=0, keepdims=True)
        spread[1, w + 1 : w + 2, :] = row
    middle = spread[1, 1 : count + 1, :]
    for n in range(4):
        turned = middle if n == 1 else shifted(middle, 32 * (n - 1), 1)
        if n != 1:
            spread[n, 1 : count + 1, :] = turned
        spread[n, 0:1, :] = turned[count - 1 : count]
        spread[n, count + 1 : count + 2, :] = turned[0:1]
    for w in range(count):
        for n in range(4):
            payload[w * 4 + n] = spread[n, w : w + 3, :]


def misfit_part(values, coef, agg, coarse, fetch, misfit, payload, sums, spread):
    inside = box_mask()
    rolled = {}
    for c in range(3):
        misfit[c, 0] = jnp.zeros((ROWS, LANES), f32)
        misfit[c, 7] = jnp.zeros((ROWS, LANES), f32)
    for a in range(1, 7):
        applied = operate_pair(values, coef, a, rolled)
        for c in range(3):
            misfit[c, a] = jnp.where(inside, coef[RHS + c, a - 1] - applied[c], 0.0)
    coarse_part([misfit[0, a, 0:8] for a in range(2, 6)], agg, coarse, fetch, sums, spread, payload)


def first_misfit(
    far,
    near,
    low,
    high,
    mine,
    agg,
    coarse_hbm,
    coef,
    slots,
    misfit,
    payload,
    rim,
    values,
    sums,
    spread,
    coarse,
    sem,
):
    fetch = pltpu.make_async_copy(coarse_hbm, coarse, sem)
    fetch.start()
    odd = is_odd("wide")
    narrow_odd = is_odd("narrow")
    blank = jnp.zeros((ROWS, LANES), f32)

    def place(target, rows, at, width):
        target[...] = blank
        target[0:8] = rows
        a, b = low[at : at + width], high[at : at + width]
        target[8 : 8 + width] = pick(narrow_odd, a, b)
        target[16 - width : 16] = pick(narrow_odd, b, a)

    for f in range(FULL):
        for a in range(8):
            rows = rim_rows(odd, far, near, mine, f, f * 16, 2, a)
            target = values.at[f - 3, a] if 3 <= f < 6 else rim.at[f if f < 3 else 3, a]
            place(target, rows, (f * 8 + a) * 3, 3)
    for t in range(THIN):
        for a in range(1, 7):
            rows = rim_rows(odd, far, near, mine, FULL + t, FULL * 16 + t * 8, 1, a)
            target = coef.at[CENTRE if t == 0 else COUP + t - 1 if t < 10 else RHS + t - 10, a - 1]
            place(target, rows, FULL * 24 + (t * 6 + a - 1) * 2, 2)
    row = lax.broadcasted_iota(jnp.int32, (ROWS, LANES), 0)
    lane = lane_index((ROWS, LANES))
    low = lane < 64
    offset = jnp.where(row < 8, 32, jnp.where(row < 12, 64, 0))
    inside = box_mask()
    for a in range(8):
        slots[a] = rim[3, a].astype(jnp.int32) + offset
    for a in range(1, 7):
        tx, ty = rim[0, a], rim[1, a]
        tz = jnp.where((lane % 64) < 63, rim[2, a], 0.0)
        txw = jnp.where(low, swap_halves(rim[0, a - 1]), swap_halves(tx))
        tys = shifted(ty, -1, 0)
        tzm = shifted(tz, -1, 1)
        centre = coef[CENTRE, a - 1] + (tx + txw + ty + tys + tz + tzm)
        coef[TX, a - 1] = tx
        coef[TXW, a - 1] = txw
        coef[TY, a - 1] = ty
        coef[TYS, a - 1] = tys
        coef[TZ, a - 1] = tz
        coef[TZM, a - 1] = tzm
        coef[CENTRE, a - 1] = centre
        for c in range(3):
            diagonal = jnp.where(inside, centre + coef[COUP + 4 * c, a - 1], 1.0)
            coef[INV + c, a - 1] = jnp.where(inside, 1.0 / diagonal, 0.0)
    misfit_part(values, coef, agg, coarse, fetch, misfit, payload, sums, spread)


def gather_values(current, far, near, low, high, received, slots, values):
    odd = is_odd("wide")
    narrow_odd = is_odd("narrow")
    total = jnp.sum(received[...], axis=0)
    blank = jnp.zeros((2, LANES), f32)
    for a in range(8):
        block = 0 if a < 2 else 2 if a >= 6 else 1
        table = jnp.broadcast_to(total[block : block + 1], (8, LANES))
        for c in range(3):
            at = (c * 8 + a) * 3
            first, second = low[at : at + 3], high[at : at + 3]
            values[c, a, 0:8] = rim_rows(odd, far, near, current, c, c * 16, 2, a)
            values[c, a, 8:11] = pick(narrow_odd, first, second)
            values[c, a, 11:13] = blank
            values[c, a, 13:16] = pick(narrow_odd, second, first)
        for half in range(2):
            where = slots[a, 8 * half : 8 * half + 8]
            lifted = jnp.take_along_axis(table, where, axis=1, mode="promise_in_bounds")
            values[0, a, 8 * half : 8 * half + 8] += lifted


def next_misfit(
    current,
    far,
    near,
    low,
    high,
    received,
    slots,
    coef,
    agg,
    coarse_hbm,
    moved,
    misfit,
    payload,
    values,
    sums,
    spread,
    coarse,
    sem,
):
    fetch = pltpu.make_async_copy(coarse_hbm, coarse, sem)
    fetch.start()
    gather_values(current, far, near, low, high, received, slots, values)
    for c in range(3):
        for p in range(4):
            moved[c, p] = values[c, p + 2, 0:8]
    misfit_part(values, coef, agg, coarse, fetch, misfit, payload, sums, spread)


def last_misfit(current, far, near, low, high, received, slots, coef, iterate, residual, values):
    gather_values(current, far, near, low, high, received, slots, values)
    rolled = {}
    for a in range(2, 6):
        applied = operate_pair(values, coef, a, rolled)
        for c in range(3):
            iterate[c, a - 2] = values[c, a, 0:8]
            residual[c, a - 2] = (coef[RHS + c, a - 1] - applied[c])[0:8]


def local_solve(misfit, coef, current, factors_hbm, moved, far, near, one, two, factors, sems, first=0):
    fetches = [pltpu.make_async_copy(factors_hbm.at[a], factors.at[a], sems.at[a]) for a in range(6)]
    for fetch in fetches:
        fetch.start()
    own_cols = list(range(8))
    row8 = lax.broadcasted_iota(jnp.int32, (24, LANES), 0) % 8

    def tiles(values, pair, cols, half):
        scaled = [coef[INV + c, pair - 1, 8 * half : 8 * half + 8] * values[c] for c in range(3)]
        left = jnp.concatenate(scaled, axis=0).astype(jnp.bfloat16)
        total = jnp.zeros((24, LANES), f32)
        for y in cols:
            product = lax.dot_general(
                left, factors[pair - 1, y + 2], (((1,), (1,)), ((), ())), preferred_element_type=f32
            )
            total = jnp.where(row8 == y % 8, product, total)
        return [total[8 * c : 8 * c + 8] for c in range(3)]

    blank = jnp.zeros((ROWS, LANES), f32)
    for c in range(3):
        for ref in (one, two):
            ref[c, 0] = blank
            ref[c, 7] = blank
    for a in range(1, 7):
        edge = a in (1, 6)
        fetches[a - 1].wait()
        for half, cols in ((0, own_cols), (1, [8, -1] if edge else [8, 9, -2, -1])):
            part = tiles([misfit[c, a, 8 * half : 8 * half + 8] for c in range(3)], a, cols, half)
            for c in range(3):
                one[c, a, 8 * half : 8 * half + 8] = part[c]
    rolled = {}
    for a in range(1, 7):
        edge = a in (1, 6)
        applied = operate_pair(one, coef, a, rolled)
        left = [misfit[c, a] - applied[c] for c in range(3)]
        for half, cols in ((0, own_cols), (1, [] if edge else [8, -1])):
            if not cols:
                for c in range(3):
                    two[c, a, 8:16] = one[c, a, 8:16]
                continue
            part = tiles([v[8 * half : 8 * half + 8] for v in left], a, cols, half)
            for c in range(3):
                two[c, a, 8 * half : 8 * half + 8] = one[c, a, 8 * half : 8 * half + 8] + part[c]
    rolled = {}
    for a in range(2, 6):
        applied = operate_pair(two, coef, a, rolled)
        part = tiles([(misfit[c, a] - applied[c])[0:8] for c in range(3)], a, own_cols, 0)
        for c in range(3):
            moved[c, a - 2] = current[first + c, a - 2] + (two[c, a, 0:8] + part[c])
    odd = is_odd("wide")
    for c in range(3):
        for p in range(2):
            at = c * 16 + p * 8
            far[at : at + 8] = pick(odd, moved[c, 2 + p], moved[c, p])
            near[at : at + 8] = pick(odd, moved[c, p], moved[c, 2 + p])


def call(body, name, outs, scratch, operands, in_hbm=(), flops=1000000):
    vmem = pl.BlockSpec(memory_space=pltpu.VMEM)
    hbm = pl.BlockSpec(memory_space=pltpu.HBM)
    operands = [pltpu.with_memory_space_constraint(x, pltpu.HBM) if i in in_hbm else x for i, x in enumerate(operands)]
    return pl.pallas_call(
        body,
        out_shape=[jax.ShapeDtypeStruct(shape, dtype) for shape, dtype in outs],
        in_specs=[hbm if i in in_hbm else vmem for i in range(len(operands))],
        out_specs=[vmem] * len(outs),
        scratch_shapes=scratch,
        compiler_params=pltpu.CompilerParams(vmem_limit_bytes=VMEM_LIMIT),
        cost_estimate=pl.CostEstimate(flops=flops, bytes_accessed=0, transcendentals=0),
        name=name,
    )(*operands)


def swaps(axis, far, near):
    count = lax.axis_size(axis)
    with jax.named_scope(axis + "_far"):
        far = lax.ppermute(far, axis, [(i, (i + (1 if i % 2 else -1)) % count) for i in range(count)])
    with jax.named_scope(axis + "_near"):
        near = lax.ppermute(near, axis, [(i, i ^ 1) for i in range(count)])
    return far, near


def per_device(
    rhs, start, trans, accum, coupling, well_cells, well_index, agg_map, tile_factors, coarse_inverse
):
    devices = lax.axis_size("wide") * lax.axis_size("narrow")
    dma = pltpu.SemaphoreType.DMA
    own = ((3, 4, 8, LANES), f32)
    box = ((3, PAIRS, ROWS, LANES), f32)
    wide_type = ((48, LANES), f32)
    narrow_type = ((72, LANES), f32)
    payload_type = ((devices, 3, LANES), f32)
    coarse_scratch = [
        pltpu.VMEM(box[0], f32),
        pltpu.VMEM((AGG_LOC, LANES), f32),
        pltpu.VMEM((4, devices // 4 + 8, LANES), f32),
        pltpu.VMEM(coarse_inverse.shape, f32),
        dma,
    ]

    mine, agg, far, near = call(
        add_wells_and_pack,
        "pack_wide",
        [((FULL + THIN, 4, 8, LANES), f32), ((4, 8, LANES), f32)] + [((WIDE_ROWS, LANES), f32)] * 2,
        [
            pltpu.VMEM((1, 64), jnp.int32),
            pltpu.VMEM((1, 64), f32),
            pltpu.VMEM((4, 8, LANES), f32),
            pltpu.VMEM((4, 8, LANES), jnp.int32),
            dma((8,)),
        ],
        [
            well_cells.reshape(1, -1),
            well_index.reshape(1, -1),
            accum,
            trans,
            start,
            agg_map,
            coupling.reshape((9,) + accum.shape),
            rhs,
        ],
        in_hbm=range(8),
    )
    far, near = swaps("wide", far, near)
    low, high = call(pack_narrow, "pack_narrow", [((NARROW_ROWS, LANES), f32)] * 2, [], [far, near, mine])
    low, high = swaps("narrow", low, high)
    coef, slots, misfit, payload = call(
        first_misfit,
        "first_misfit",
        [((N_COEF, 6, ROWS, LANES), f32), ((PAIRS, ROWS, LANES), jnp.int32), box, payload_type],
        [pltpu.VMEM((4, PAIRS, ROWS, LANES), f32)] + coarse_scratch,
        [far, near, low, high, mine, agg, coarse_inverse],
        in_hbm=(6,),
    )
    current, first = mine, 3
    for sweep in range(SWEEPS):
        received = lax.all_to_all(payload, ("wide", "narrow"), 0, 0)
        current, far, near = call(
            functools.partial(local_solve, first=first),
            "local_solve",
            [own, wide_type, wide_type],
            [pltpu.VMEM(box[0], f32)] * 2 + [pltpu.VMEM(tile_factors.shape, tile_factors.dtype), dma((6,))],
            [misfit, coef, current, tile_factors],
            in_hbm=(3,),
            flops=30000000,
        )
        first = 0
        far, near = swaps("wide", far, near)
        low, high = call(pack_current, "pack_current", [narrow_type] * 2, [], [current, far, near])
        low, high = swaps("narrow", low, high)
        known = [current, far, near, low, high, received, slots, coef]
        if sweep < SWEEPS - 1:
            current, misfit, payload = call(
                next_misfit,
                "next_misfit",
                [own, box, payload_type],
                coarse_scratch,
                known + [agg, coarse_inverse],
                in_hbm=(9,),
            )
        else:
            iterate, residual = call(last_misfit, "last_misfit", [own, own], [pltpu.VMEM(box[0], f32)], known)
    return iterate, residual


def solution(mesh):
    return jax.shard_map(
        per_device,
        mesh=mesh,
        in_specs=(
            P(None, "wide", "narrow", None),
            P(None, "wide", "narrow", None),
            P(None, "wide", "narrow", None),
            P("wide", "narrow", None),
            P(None, None, "wide", "narrow", None),
            P("wide", "narrow", None),
            P("wide", "narrow", None),
            P("wide", "narrow", None),
            P("wide", "narrow", None, None),
            P(("wide", "narrow"), None),
        ),
        out_specs=(P(None, "wide", "narrow", None), P(None, "wide", "narrow", None)),
        check_vma=False,
    )
```

time: 167 us -> 126 us (0.75)
  local copies, waits for them, and re-layouts: 34.4 us -> 0 us
  waiting for transfers between devices: 42.7 us -> 31.5 us
  Pallas kernels: 15.3 us -> 23.8 us
  starting transfers between devices: 72.3 us -> 69 us
    unnamed x96 -> x0, local copies, waits for them, and re-layouts: 34.3 us -> none
    ppermute x16, waiting for transfers between devices: 42.7 us -> 31.5 us  [the longest x8 29.2 us: swaps(): lax.ppermute(far, axis, [(i, (i + (1 if i % 2 else -1)) % count) for i in...]
    pallas_call x12, Pallas kernels: 15.3 us -> 23.8 us  [call(): pl.pallas_call(body, out_shape=[jax.ShapeDtypeStruct(shape, dtype) for sh...]
    all_to_all x3, starting transfers between devices: 25.5 us -> 23.3 us  [per_device(): received = lax.all_to_all(payload, ('wide', 'narrow'), 0, 0)]
  transfers between devices with their start and end apart: 19 -> 19, of which waited for: 15 -> 9; matrix products, arithmetic and copies ran while one was open for 0% -> 0% of each run, Pallas kernels for 5% -> 11%
where the time goes in v1:
time: 126 us; the launch traced here: 125 us
  starting transfers between devices  69 us (55%)
  waiting for transfers between devices  31.5 us (25%)
  Pallas kernels  23.8 us (19%)
    ppermute x8, starting transfers between devices, swaps(): lax.ppermute(far, axis, [(i, (i + (1 if i % 2 else -1)) % count) for i in...  45.7 us
    ppermute x8, waiting for transfers between devices, swaps(): lax.ppermute(far, axis, [(i, (i + (1 if i % 2 else -1)) % count) for i in...  29.2 us
    pallas_call x12, Pallas kernels, call(): pl.pallas_call(body, out_shape=[jax.ShapeDtypeStruct(shape, dtype) for sh...  23.8 us
    all_to_all x3, starting transfers between devices, per_device(): received = lax.all_to_all(payload, ('wide', 'narrow'), 0, 0)  23.3 us
  transfers between devices with their start and end apart: 19, of which 9 were waited for; matrix products, arithmetic and copies ran while one was open for 0% of the time, Pallas kernels for 11%

profile of v1, /device:TPU:1, one launch (start us, length us, event | category | flops | bytes accessed | tf_op | source)
XLA Modules:
  0.0 125.1 jit_solution(953448055469425340)
XLA Ops:
  1.8 11.4 %collective-permute-start = (f32[216,128]{1,0:T(8,128)S(1)}, f32[216,128]{1,0:T(8,128)S(1)}, u32[]{:S(2)}, u32[]{:S(2)}) collective-permute-start(f32[216,128]{1,0:T(8,128)S(1)} %get-tuple-element.33), channel_id=1, source_target_pairs={{0,252},{4,8},{8,4},{12,16},{16,12},{20,24},{24,20},{28,32},{32,28... | collective-permute-start | bytes 331784 | tf_op jit(solution)/shard_map/wide_far/ppermute | solution.py:417
  13.2 2.8 %collective-permute-done.far = f32[216,128]{1,0:T(8,128)S(1)} collective-permute-done((f32[216,128]{1,0:T(8,128)S(1)}, f32[216,128]{1,0:T(8,128)S(1)}, u32[]{:S(2)}, u32[]{:S(2)}) %collective-permute-start) | collective-permute-done | bytes 110624 | tf_op jit(solution)/shard_map/wide_far/ppermute | solution.py:417
  15.9 2.3 %collective-permute-done.1.near = f32[216,128]{1,0:T(8,128)S(1)} collective-permute-done((f32[216,128]{1,0:T(8,128)S(1)}, f32[216,128]{1,0:T(8,128)S(1)}, u32[]{:S(2)}, u32[]{:S(2)}) %collective-permute-start.1) | collective-permute-done | bytes 110624 | tf_op jit(solution)/shard_map/wide_near/ppermute | solution.py:419
  18.4 2.4 %collective-permute-start.2 = (f32[324,128]{1,0:T(8,128)S(1)}, f32[324,128]{1,0:T(8,128)S(1)}, u32[]{:S(2)}, u32[]{:S(2)}) collective-permute-start(f32[324,128]{1,0:T(8,128)S(1)} %get-tuple-element.36), channel_id=1, source_target_pairs={{0,3},{1,2},{2,1},{3,0},{4,7},{5,6},{6,5},{7,4},{8,11},{9,10},{10,... | collective-permute-start | bytes 497672 | tf_op jit(solution)/shard_map/narrow_far/ppermute | solution.py:417
  20.8 4.3 %collective-permute-done.2.low = f32[324,128]{1,0:T(8,128)S(1)} collective-permute-done((f32[324,128]{1,0:T(8,128)S(1)}, f32[324,128]{1,0:T(8,128)S(1)}, u32[]{:S(2)}, u32[]{:S(2)}) %collective-permute-start.2) | collective-permute-done | bytes 165920 | tf_op jit(solution)/shard_map/narrow_far/ppermute | solution.py:417
  25.0 2.4 %first_misfit.1 = (f32[22,6,16,128]{3,2,1,0:T(8,128)S(1)}, s32[8,16,128]{2,1,0:T(8,128)S(1)}, f32[3,8,16,128]{3,2,1,0:T(8,128)S(1)}, f32[256,3,128]{2,1,0:T(4,128)}) custom-call(f32[216,128]{1,0:T(8,128)S(1)} %collective-permute-done.far, f32[216,128]{1,0:T(8,128)S(1)} %collective-permute-done.1.near, f32[324,128]{1,0:T(8,128)S(1)} %collective-permute-done.2.low, ...), custom_call_target="tpu_custom_call" | custom-call | flops 1000000 | tf_op jit(solution)/shard_map/first_misfit/pallas_call | solution.py:402
  27.4 8.6 %all-to-all-start = ((f32[256,3,128]{2,1,0:T(4,128)}), f32[256,3,128]{2,1,0:T(4,128)S(1)}, u32[]{:S(2)}, u32[]{:S(2)}) async-start(f32[256,3,128]{2,1,0:T(4,128)} %get-tuple-element.46), calls=%async_computation | async-start | bytes 1048576 | tf_op jit(solution)/shard_map/all_to_all | solution.py:477
  36.0 4.4 %local_solve.3 = (f32[3,4,8,128]{3,2,1,0:T(8,128)S(1)}, f32[48,128]{1,0:T(8,128)S(1)}, f32[48,128]{1,0:T(8,128)S(1)}) custom-call(f32[3,8,16,128]{3,2,1,0:T(8,128)S(1)} %get-tuple-element.39.misfit, f32[22,6,16,128]{3,2,1,0:T(8,128)S(1)} %get-tuple-element.40.coef, f32[20,4,8,128]{3,2,1,0:T(8,128)S(1)} %get-tuple-element.35.mine.current, ...), custom_call_target="tpu_custom_call" | custom-call | flops 30000000 | tf_op jit(solution)/shard_map/local_solve/pallas_call | solution.py:402
  40.4 9.1 %collective-permute-start.4 = (f32[48,128]{1,0:T(8,128)S(1)}, f32[48,128]{1,0:T(8,128)S(1)}, u32[]{:S(2)}, u32[]{:S(2)}) collective-permute-start(f32[48,128]{1,0:T(8,128)S(1)} %get-tuple-element.42), channel_id=1, source_target_pairs={{0,252},{4,8},{8,4},{12,16},{16,12},{20,24},{24,20},{28,32},{32,28... | collective-permute-start | bytes 73736 | tf_op jit(solution)/shard_map/wide_far/ppermute | solution.py:417
  49.6 5.4 %collective-permute-done.4.far = f32[48,128]{1,0:T(8,128)S(1)} collective-permute-done((f32[48,128]{1,0:T(8,128)S(1)}, f32[48,128]{1,0:T(8,128)S(1)}, u32[]{:S(2)}, u32[]{:S(2)}) %collective-permute-start.4) | collective-permute-done | bytes 24608 | tf_op jit(solution)/shard_map/wide_far/ppermute | solution.py:417
  55.0 1.5 %collective-permute-start.6 = (f32[72,128]{1,0:T(8,128)S(1)}, f32[72,128]{1,0:T(8,128)S(1)}, u32[]{:S(2)}, u32[]{:S(2)}) collective-permute-start(f32[72,128]{1,0:T(8,128)S(1)} %get-tuple-element.44), channel_id=1, source_target_pairs={{0,3},{1,2},{2,1},{3,0},{4,7},{5,6},{6,5},{7,4},{8,11},{9,10},{10,... | collective-permute-start | bytes 110600 | tf_op jit(solution)/shard_map/narrow_far/ppermute | solution.py:417
  56.5 2.0 %collective-permute-done.6.low = f32[72,128]{1,0:T(8,128)S(1)} collective-permute-done((f32[72,128]{1,0:T(8,128)S(1)}, f32[72,128]{1,0:T(8,128)S(1)}, u32[]{:S(2)}, u32[]{:S(2)}) %collective-permute-start.6) | collective-permute-done | bytes 36896 | tf_op jit(solution)/shard_map/narrow_far/ppermute | solution.py:417
  58.5 2.9 %next_misfit.2 = (f32[3,4,8,128]{3,2,1,0:T(8,128)S(1)}, f32[3,8,16,128]{3,2,1,0:T(8,128)S(1)}, f32[256,3,128]{2,1,0:T(4,128)}) custom-call(f32[3,4,8,128]{3,2,1,0:T(8,128)S(1)} %get-tuple-element.41.current, f32[48,128]{1,0:T(8,128)S(1)} %collective-permute-done.4.far, f32[48,128]{1,0:T(8,128)S(1)} %collective-permute-done.5.near, ...), custom_call_target="tpu_custom_call" | custom-call | flops 1000000 | tf_op jit(solution)/shard_map/next_misfit/pallas_call | solution.py:402
  61.4 7.4 %all-to-all-start.1 = ((f32[256,3,128]{2,1,0:T(4,128)}), f32[256,3,128]{2,1,0:T(4,128)S(1)}, u32[]{:S(2)}, u32[]{:S(2)}) async-start(f32[256,3,128]{2,1,0:T(4,128)} %get-tuple-element.55), calls=%async_computation.1 | async-start | bytes 1048576 | tf_op jit(solution)/shard_map/all_to_all | solution.py:477
  68.8 4.4 %local_solve.4 = (f32[3,4,8,128]{3,2,1,0:T(8,128)S(1)}, f32[48,128]{1,0:T(8,128)S(1)}, f32[48,128]{1,0:T(8,128)S(1)}) custom-call(f32[3,8,16,128]{3,2,1,0:T(8,128)S(1)} %get-tuple-element.48.misfit, f32[22,6,16,128]{3,2,1,0:T(8,128)S(1)} %get-tuple-element.40.coef, f32[3,4,8,128]{3,2,1,0:T(8,128)S(1)} %get-tuple-element.49.current, ...), custom_call_target="tpu_custom_call" | custom-call | flops 30000000 | tf_op jit(solution)/shard_map/local_solve/pallas_call | solution.py:402
  73.2 9.1 %collective-permute-start.8 = (f32[48,128]{1,0:T(8,128)S(1)}, f32[48,128]{1,0:T(8,128)S(1)}, u32[]{:S(2)}, u32[]{:S(2)}) collective-permute-start(f32[48,128]{1,0:T(8,128)S(1)} %get-tuple-element.51), channel_id=1, source_target_pairs={{0,252},{4,8},{8,4},{12,16},{16,12},{20,24},{24,20},{28,32},{32,28... | collective-permute-start | bytes 73736 | tf_op jit(solution)/shard_map/wide_far/ppermute | solution.py:417
  82.4 5.4 %collective-permute-done.8.far = f32[48,128]{1,0:T(8,128)S(1)} collective-permute-done((f32[48,128]{1,0:T(8,128)S(1)}, f32[48,128]{1,0:T(8,128)S(1)}, u32[]{:S(2)}, u32[]{:S(2)}) %collective-permute-start.8) | collective-permute-done | bytes 24608 | tf_op jit(solution)/shard_map/wide_far/ppermute | solution.py:417
  89.3 2.0 %collective-permute-done.10.low = f32[72,128]{1,0:T(8,128)S(1)} collective-permute-done((f32[72,128]{1,0:T(8,128)S(1)}, f32[72,128]{1,0:T(8,128)S(1)}, u32[]{:S(2)}, u32[]{:S(2)}) %collective-permute-start.10) | collective-permute-done | bytes 36896 | tf_op jit(solution)/shard_map/narrow_far/ppermute | solution.py:417
  91.3 2.9 %next_misfit.3 = (f32[3,4,8,128]{3,2,1,0:T(8,128)S(1)}, f32[3,8,16,128]{3,2,1,0:T(8,128)S(1)}, f32[256,3,128]{2,1,0:T(4,128)}) custom-call(f32[3,4,8,128]{3,2,1,0:T(8,128)S(1)} %get-tuple-element.50.current, f32[48,128]{1,0:T(8,128)S(1)} %collective-permute-done.8.far, f32[48,128]{1,0:T(8,128)S(1)} %collective-permute-done.9.near, ...), custom_call_target="tpu_custom_call" | custom-call | flops 1000000 | tf_op jit(solution)/shard_map/next_misfit/pallas_call | solution.py:402
  94.2 7.4 %all-to-all-start.2 = ((f32[256,3,128]{2,1,0:T(4,128)}), f32[256,3,128]{2,1,0:T(4,128)S(1)}, u32[]{:S(2)}, u32[]{:S(2)}) async-start(f32[256,3,128]{2,1,0:T(4,128)} %get-tuple-element.63), calls=%async_computation.2 | async-start | bytes 1048576 | tf_op jit(solution)/shard_map/all_to_all | solution.py:477
  101.6 4.4 %local_solve.5 = (f32[3,4,8,128]{3,2,1,0:T(8,128)S(1)}, f32[48,128]{1,0:T(8,128)S(1)}, f32[48,128]{1,0:T(8,128)S(1)}) custom-call(f32[3,8,16,128]{3,2,1,0:T(8,128)S(1)} %get-tuple-element.56.misfit, f32[22,6,16,128]{3,2,1,0:T(8,128)S(1)} %get-tuple-element.40.coef, f32[3,4,8,128]{3,2,1,0:T(8,128)S(1)} %get-tuple-element.57.current, ...), custom_call_target="tpu_custom_call" | custom-call | flops 30000000 | tf_op jit(solution)/shard_map/local_solve/pallas_call | solution.py:402
  106.0 9.1 %collective-permute-start.12 = (f32[48,128]{1,0:T(8,128)S(1)}, f32[48,128]{1,0:T(8,128)S(1)}, u32[]{:S(2)}, u32[]{:S(2)}) collective-permute-start(f32[48,128]{1,0:T(8,128)S(1)} %get-tuple-element.59), channel_id=1, source_target_pairs={{0,252},{4,8},{8,4},{12,16},{16,12},{20,24},{24,20},{28,32},{32,28... | collective-permute-start | bytes 73736 | tf_op jit(solution)/shard_map/wide_far/ppermute | solution.py:417
  115.1 5.4 %collective-permute-done.12.far = f32[48,128]{1,0:T(8,128)S(1)} collective-permute-done((f32[48,128]{1,0:T(8,128)S(1)}, f32[48,128]{1,0:T(8,128)S(1)}, u32[]{:S(2)}, u32[]{:S(2)}) %collective-permute-start.12) | collective-permute-done | bytes 24608 | tf_op jit(solution)/shard_map/wide_far/ppermute | solution.py:417
  122.1 2.0 %collective-permute-done.14.low = f32[72,128]{1,0:T(8,128)S(1)} collective-permute-done((f32[72,128]{1,0:T(8,128)S(1)}, f32[72,128]{1,0:T(8,128)S(1)}, u32[]{:S(2)}, u32[]{:S(2)}) %collective-permute-start.14) | collective-permute-done | bytes 36896 | tf_op jit(solution)/shard_map/narrow_far/ppermute | solution.py:417
  (26 shorter events, 5.4 us)
Async XLA Ops:
  1.8 14.2 %collective-permute-start = (f32[216,128]{1,0:T(8,128)S(1)}, f32[216,128]{1,0:T(8,128)S(1)}, u32[]{:S(2)}, u32[]{:S(2)}) collective-permute-start(f32[216,128]{1,0:T(8,128)S(1)} %get-tuple-element.33), channel_id=1, source_target_pairs={{0,252},{4,8},{8,4},{12,16},{16,12},{20,24},{24,20},{28,32},{32,28... | collective-permute-start | bytes 331784 | tf_op jit(solution)/shard_map/wide_far/ppermute | solution.py:417
  13.2 5.1 %collective-permute-start.1 = (f32[216,128]{1,0:T(8,128)S(1)}, f32[216,128]{1,0:T(8,128)S(1)}, u32[]{:S(2)}, u32[]{:S(2)}) collective-permute-start(f32[216,128]{1,0:T(8,128)S(1)} %get-tuple-element.34), channel_id=1, source_target_pairs={{0,4},{4,0},{8,12},{12,8},{16,20},{20,16},{24,28},{28,24},{32,36},... | collective-permute-start | bytes 331784 | tf_op jit(solution)/shard_map/wide_near/ppermute | solution.py:419
  18.4 6.7 %collective-permute-start.2 = (f32[324,128]{1,0:T(8,128)S(1)}, f32[324,128]{1,0:T(8,128)S(1)}, u32[]{:S(2)}, u32[]{:S(2)}) collective-permute-start(f32[324,128]{1,0:T(8,128)S(1)} %get-tuple-element.36), channel_id=1, source_target_pairs={{0,3},{1,2},{2,1},{3,0},{4,7},{5,6},{6,5},{7,4},{8,11},{9,10},{10,... | collective-permute-start | bytes 497672 | tf_op jit(solution)/shard_map/narrow_far/ppermute | solution.py:417
  20.7 4.3 %collective-permute-start.3 = (f32[324,128]{1,0:T(8,128)S(1)}, f32[324,128]{1,0:T(8,128)S(1)}, u32[]{:S(2)}, u32[]{:S(2)}) collective-permute-start(f32[324,128]{1,0:T(8,128)S(1)} %get-tuple-element.37), channel_id=1, source_target_pairs={{0,1},{1,0},{2,3},{3,2},{4,5},{5,4},{6,7},{7,6},{8,9},{9,8},{10,11... | collective-permute-start | bytes 497672 | tf_op jit(solution)/shard_map/narrow_near/ppermute | solution.py:419
  27.4 31.1 %all-to-all-start = ((f32[256,3,128]{2,1,0:T(4,128)}), f32[256,3,128]{2,1,0:T(4,128)S(1)}, u32[]{:S(2)}, u32[]{:S(2)}) async-start(f32[256,3,128]{2,1,0:T(4,128)} %get-tuple-element.46), calls=%async_computation | async-start | bytes 1048576 | tf_op jit(solution)/shard_map/all_to_all | solution.py:477
  40.4 14.5 %collective-permute-start.4 = (f32[48,128]{1,0:T(8,128)S(1)}, f32[48,128]{1,0:T(8,128)S(1)}, u32[]{:S(2)}, u32[]{:S(2)}) collective-permute-start(f32[48,128]{1,0:T(8,128)S(1)} %get-tuple-element.42), channel_id=1, source_target_pairs={{0,252},{4,8},{8,4},{12,16},{16,12},{20,24},{24,20},{28,32},{32,28... | collective-permute-start | bytes 73736 | tf_op jit(solution)/shard_map/wide_far/ppermute | solution.py:417
  49.6 5.4 %collective-permute-start.5 = (f32[48,128]{1,0:T(8,128)S(1)}, f32[48,128]{1,0:T(8,128)S(1)}, u32[]{:S(2)}, u32[]{:S(2)}) collective-permute-start(f32[48,128]{1,0:T(8,128)S(1)} %get-tuple-element.43), channel_id=1, source_target_pairs={{0,4},{4,0},{8,12},{12,8},{16,20},{20,16},{24,28},{28,24},{32,36},... | collective-permute-start | bytes 73736 | tf_op jit(solution)/shard_map/wide_near/ppermute | solution.py:419
  55.0 3.5 %collective-permute-start.6 = (f32[72,128]{1,0:T(8,128)S(1)}, f32[72,128]{1,0:T(8,128)S(1)}, u32[]{:S(2)}, u32[]{:S(2)}) collective-permute-start(f32[72,128]{1,0:T(8,128)S(1)} %get-tuple-element.44), channel_id=1, source_target_pairs={{0,3},{1,2},{2,1},{3,0},{4,7},{5,6},{6,5},{7,4},{8,11},{9,10},{10,... | collective-permute-start | bytes 110600 | tf_op jit(solution)/shard_map/narrow_far/ppermute | solution.py:417
  56.5 2.0 %collective-permute-start.7 = (f32[72,128]{1,0:T(8,128)S(1)}, f32[72,128]{1,0:T(8,128)S(1)}, u32[]{:S(2)}, u32[]{:S(2)}) collective-permute-start(f32[72,128]{1,0:T(8,128)S(1)} %get-tuple-element.45), channel_id=1, source_target_pairs={{0,1},{1,0},{2,3},{3,2},{4,5},{5,4},{6,7},{7,6},{8,9},{9,8},{10,11... | collective-permute-start | bytes 110600 | tf_op jit(solution)/shard_map/narrow_near/ppermute | solution.py:419
  61.4 29.9 %all-to-all-start.1 = ((f32[256,3,128]{2,1,0:T(4,128)}), f32[256,3,128]{2,1,0:T(4,128)S(1)}, u32[]{:S(2)}, u32[]{:S(2)}) async-start(f32[256,3,128]{2,1,0:T(4,128)} %get-tuple-element.55), calls=%async_computation.1 | async-start | bytes 1048576 | tf_op jit(solution)/shard_map/all_to_all | solution.py:477
  73.2 14.5 %collective-permute-start.8 = (f32[48,128]{1,0:T(8,128)S(1)}, f32[48,128]{1,0:T(8,128)S(1)}, u32[]{:S(2)}, u32[]{:S(2)}) collective-permute-start(f32[48,128]{1,0:T(8,128)S(1)} %get-tuple-element.51), channel_id=1, source_target_pairs={{0,252},{4,8},{8,4},{12,16},{16,12},{20,24},{24,20},{28,32},{32,28... | collective-permute-start | bytes 73736 | tf_op jit(solution)/shard_map/wide_far/ppermute | solution.py:417
  82.4 5.4 %collective-permute-start.9 = (f32[48,128]{1,0:T(8,128)S(1)}, f32[48,128]{1,0:T(8,128)S(1)}, u32[]{:S(2)}, u32[]{:S(2)}) collective-permute-start(f32[48,128]{1,0:T(8,128)S(1)} %get-tuple-element.52), channel_id=1, source_target_pairs={{0,4},{4,0},{8,12},{12,8},{16,20},{20,16},{24,28},{28,24},{32,36},... | collective-permute-start | bytes 73736 | tf_op jit(solution)/shard_map/wide_near/ppermute | solution.py:419
  87.8 3.5 %collective-permute-start.10 = (f32[72,128]{1,0:T(8,128)S(1)}, f32[72,128]{1,0:T(8,128)S(1)}, u32[]{:S(2)}, u32[]{:S(2)}) collective-permute-start(f32[72,128]{1,0:T(8,128)S(1)} %get-tuple-element.53), channel_id=1, source_target_pairs={{0,3},{1,2},{2,1},{3,0},{4,7},{5,6},{6,5},{7,4},{8,11},{9,10},{10,... | collective-permute-start | bytes 110600 | tf_op jit(solution)/shard_map/narrow_far/ppermute | solution.py:417
  89.3 2.0 %collective-permute-start.11 = (f32[72,128]{1,0:T(8,128)S(1)}, f32[72,128]{1,0:T(8,128)S(1)}, u32[]{:S(2)}, u32[]{:S(2)}) collective-permute-start(f32[72,128]{1,0:T(8,128)S(1)} %get-tuple-element.54), channel_id=1, source_target_pairs={{0,1},{1,0},{2,3},{3,2},{4,5},{5,4},{6,7},{7,6},{8,9},{9,8},{10,11... | collective-permute-start | bytes 110600 | tf_op jit(solution)/shard_map/narrow_near/ppermute | solution.py:419
  94.2 29.9 %all-to-all-start.2 = ((f32[256,3,128]{2,1,0:T(4,128)}), f32[256,3,128]{2,1,0:T(4,128)S(1)}, u32[]{:S(2)}, u32[]{:S(2)}) async-start(f32[256,3,128]{2,1,0:T(4,128)} %get-tuple-element.63), calls=%async_computation.2 | async-start | bytes 1048576 | tf_op jit(solution)/shard_map/all_to_all | solution.py:477
  106.0 14.5 %collective-permute-start.12 = (f32[48,128]{1,0:T(8,128)S(1)}, f32[48,128]{1,0:T(8,128)S(1)}, u32[]{:S(2)}, u32[]{:S(2)}) collective-permute-start(f32[48,128]{1,0:T(8,128)S(1)} %get-tuple-element.59), channel_id=1, source_target_pairs={{0,252},{4,8},{8,4},{12,16},{16,12},{20,24},{24,20},{28,32},{32,28... | collective-permute-start | bytes 73736 | tf_op jit(solution)/shard_map/wide_far/ppermute | solution.py:417
  115.1 5.4 %collective-permute-start.13 = (f32[48,128]{1,0:T(8,128)S(1)}, f32[48,128]{1,0:T(8,128)S(1)}, u32[]{:S(2)}, u32[]{:S(2)}) collective-permute-start(f32[48,128]{1,0:T(8,128)S(1)} %get-tuple-element.60), channel_id=1, source_target_pairs={{0,4},{4,0},{8,12},{12,8},{16,20},{20,16},{24,28},{28,24},{32,36},... | collective-permute-start | bytes 73736 | tf_op jit(solution)/shard_map/wide_near/ppermute | solution.py:419
  120.6 3.5 %collective-permute-start.14 = (f32[72,128]{1,0:T(8,128)S(1)}, f32[72,128]{1,0:T(8,128)S(1)}, u32[]{:S(2)}, u32[]{:S(2)}) collective-permute-start(f32[72,128]{1,0:T(8,128)S(1)} %get-tuple-element.61), channel_id=1, source_target_pairs={{0,3},{1,2},{2,1},{3,0},{4,7},{5,6},{6,5},{7,4},{8,11},{9,10},{10,... | collective-permute-start | bytes 110600 | tf_op jit(solution)/shard_map/narrow_far/ppermute | solution.py:417
  122.1 2.0 %collective-permute-start.15 = (f32[72,128]{1,0:T(8,128)S(1)}, f32[72,128]{1,0:T(8,128)S(1)}, u32[]{:S(2)}, u32[]{:S(2)}) collective-permute-start(f32[72,128]{1,0:T(8,128)S(1)} %get-tuple-element.62), channel_id=1, source_target_pairs={{0,1},{1,0},{2,3},{3,2},{4,5},{5,4},{6,7},{7,6},{8,9},{9,8},{10,11... | collective-permute-start | bytes 110600 | tf_op jit(solution)/shard_map/narrow_near/ppermute | solution.py:419

commit v2 on v1

--- a/solution.py
+++ b/solution.py
@@ -172,7 +172,7 @@
             high[at : at + 3] = pick(narrow_odd, v[0:3], v[5:8])
 
 
-def coarse_part(misfit0, agg, coarse, fetch, sums, spread, payload):
+def coarse_part(misfit0, agg, coarse, sums, spread, staged):
     for g in range(AGG_LOC):
         picked = jnp.where(agg[0] == float(g), misfit0[0], 0.0)
         for p in range(1, 4):
@@ -180,7 +180,6 @@
         sums[g : g + 1, :] = jnp.sum(picked, axis=0, keepdims=True)
     weight = jnp.broadcast_to(jnp.sum(sums[...], axis=1, keepdims=True), (AGG_LOC, LANES))
     count = coarse.shape[1] // LANES
-    fetch.wait()
     for w in range(count):
         row = jnp.sum(coarse[:, w * LANES : (w + 1) * LANES] * weight, axis=0, keepdims=True)
         spread[1, w + 1 : w + 2, :] = row
@@ -193,10 +192,12 @@
         spread[n, count + 1 : count + 2, :] = turned[0:1]
     for w in range(count):
         for n in range(4):
-            payload[w * 4 + n] = spread[n, w : w + 3, :]
-
-
-def misfit_part(values, coef, agg, coarse, fetch, misfit, payload, sums, spread):
+            at = 3 * (4 * w + n)
+            staged[at : at + 3, :] = spread[n, w : w + 3, :]
+
+
+def solve_box(values, coef, agg, coarse, factors_hbm, payload, current, far, near, scratch):
+    misfit, sums, spread, staged, one, two, factors, tile_sems, sem = scratch
     inside = box_mask()
     rolled = {}
     for c in range(3):
@@ -206,30 +207,44 @@
         applied = operate_pair(values, coef, a, rolled)
         for c in range(3):
             misfit[c, a] = jnp.where(inside, coef[RHS + c, a - 1] - applied[c], 0.0)
-    coarse_part([misfit[0, a, 0:8] for a in range(2, 6)], agg, coarse, fetch, sums, spread, payload)
-
-
-def first_misfit(
+    coarse_part([misfit[0, a, 0:8] for a in range(2, 6)], agg, coarse, sums, spread, staged)
+    write = pltpu.make_async_copy(staged, payload, sem)
+    write.start()
+    local_solve(misfit, coef, values, factors_hbm, factors, tile_sems, current, one, two)
+    odd = is_odd("wide")
+    for c in range(3):
+        for p in range(2):
+            at = c * 16 + p * 8
+            far[at : at + 8] = pick(odd, current[c, 2 + p], current[c, p])
+            near[at : at + 8] = pick(odd, current[c, p], current[c, 2 + p])
+    write.wait()
+
+
+def fetch_tiles(factors_hbm, factors, sems):
+    return [pltpu.make_async_copy(factors_hbm.at[a], factors.at[a], sems.at[a]) for a in range(6)]
+
+
+def first_sweep(
     far,
     near,
     low,
     high,
     mine,
     agg,
-    coarse_hbm,
+    coarse,
+    factors_hbm,
     coef,
     slots,
-    misfit,
     payload,
+    current,
+    far_out,
+    near_out,
     rim,
     values,
-    sums,
-    spread,
-    coarse,
-    sem,
+    *scratch,
 ):
-    fetch = pltpu.make_async_copy(coarse_hbm, coarse, sem)
-    fetch.start()
+    for fetch in fetch_tiles(factors_hbm, scratch[-3], scratch[-2]):
+        fetch.start()
     odd = is_odd("wide")
     narrow_odd = is_odd("narrow")
     blank = jnp.zeros((ROWS, LANES), f32)
@@ -275,17 +290,21 @@
         for c in range(3):
             diagonal = jnp.where(inside, centre + coef[COUP + 4 * c, a - 1], 1.0)
             coef[INV + c, a - 1] = jnp.where(inside, 1.0 / diagonal, 0.0)
-    misfit_part(values, coef, agg, coarse, fetch, misfit, payload, sums, spread)
+    solve_box(values, coef, agg, coarse, factors_hbm, payload, current, far_out, near_out, scratch)
 
 
 def gather_values(current, far, near, low, high, received, slots, values):
     odd = is_odd("wide")
     narrow_odd = is_odd("narrow")
-    total = jnp.sum(received[...], axis=0)
+    total = received[0:24]
+    for i in range(24, received.shape[0], 24):
+        total += received[i : i + 24]
+    block_of = lax.broadcasted_iota(jnp.int32, (24, LANES), 0) % 3
+    totals = [jnp.sum(jnp.where(block_of == k, total, 0.0), axis=0, keepdims=True) for k in range(3)]
     blank = jnp.zeros((2, LANES), f32)
     for a in range(8):
         block = 0 if a < 2 else 2 if a >= 6 else 1
-        table = jnp.broadcast_to(total[block : block + 1], (8, LANES))
+        table = jnp.broadcast_to(totals[block], (8, LANES))
         for c in range(3):
             at = (c * 8 + a) * 3
             first, second = low[at : at + 3], high[at : at + 3]
@@ -299,7 +318,7 @@
             values[0, a, 8 * half : 8 * half + 8] += lifted
 
 
-def next_misfit(
+def next_sweep(
     current,
     far,
     near,
@@ -309,23 +328,19 @@
     slots,
     coef,
     agg,
-    coarse_hbm,
+    coarse,
+    factors_hbm,
+    payload,
     moved,
-    misfit,
-    payload,
+    far_out,
+    near_out,
     values,
-    sums,
-    spread,
-    coarse,
-    sem,
+    *scratch,
 ):
-    fetch = pltpu.make_async_copy(coarse_hbm, coarse, sem)
-    fetch.start()
+    for fetch in fetch_tiles(factors_hbm, scratch[-3], scratch[-2]):
+        fetch.start()
     gather_values(current, far, near, low, high, received, slots, values)
-    for c in range(3):
-        for p in range(4):
-            moved[c, p] = values[c, p + 2, 0:8]
-    misfit_part(values, coef, agg, coarse, fetch, misfit, payload, sums, spread)
+    solve_box(values, coef, agg, coarse, factors_hbm, payload, moved, far_out, near_out, scratch)
 
 
 def last_misfit(current, far, near, low, high, received, slots, coef, iterate, residual, values):
@@ -338,10 +353,8 @@
             residual[c, a - 2] = (coef[RHS + c, a - 1] - applied[c])[0:8]
 
 
-def local_solve(misfit, coef, current, factors_hbm, moved, far, near, one, two, factors, sems, first=0):
-    fetches = [pltpu.make_async_copy(factors_hbm.at[a], factors.at[a], sems.at[a]) for a in range(6)]
-    for fetch in fetches:
-        fetch.start()
+def local_solve(misfit, coef, values, factors_hbm, factors, sems, moved, one, two):
+    fetches = fetch_tiles(factors_hbm, factors, sems)
     own_cols = list(range(8))
     row8 = lax.broadcasted_iota(jnp.int32, (24, LANES), 0) % 8
 
@@ -386,24 +399,21 @@
         applied = operate_pair(two, coef, a, rolled)
         part = tiles([(misfit[c, a] - applied[c])[0:8] for c in range(3)], a, own_cols, 0)
         for c in range(3):
-            moved[c, a - 2] = current[first + c, a - 2] + (two[c, a, 0:8] + part[c])
-    odd = is_odd("wide")
-    for c in range(3):
-        for p in range(2):
-            at = c * 16 + p * 8
-            far[at : at + 8] = pick(odd, moved[c, 2 + p], moved[c, p])
-            near[at : at + 8] = pick(odd, moved[c, p], moved[c, 2 + p])
-
-
-def call(body, name, outs, scratch, operands, in_hbm=(), flops=1000000):
+            moved[c, a - 2] = values[c, a, 0:8] + (two[c, a, 0:8] + part[c])
+
+
+def call(body, name, outs, scratch, operands, in_hbm=(), out_hbm=(), flops=1000000):
     vmem = pl.BlockSpec(memory_space=pltpu.VMEM)
     hbm = pl.BlockSpec(memory_space=pltpu.HBM)
     operands = [pltpu.with_memory_space_constraint(x, pltpu.HBM) if i in in_hbm else x for i, x in enumerate(operands)]
     return pl.pallas_call(
         body,
-        out_shape=[jax.ShapeDtypeStruct(shape, dtype) for shape, dtype in outs],
+        out_shape=[
+            pltpu.HBM(shape, dtype) if i in out_hbm else jax.ShapeDtypeStruct(shape, dtype)
+            for i, (shape, dtype) in enumerate(outs)
+        ],
         in_specs=[hbm if i in in_hbm else vmem for i in range(len(operands))],
-        out_specs=[vmem] * len(outs),
+        out_specs=[hbm if i in out_hbm else vmem for i in range(len(outs))],
         scratch_shapes=scratch,
         compiler_params=pltpu.CompilerParams(vmem_limit_bytes=VMEM_LIMIT),
         cost_estimate=pl.CostEstimate(flops=flops, bytes_accessed=0, transcendentals=0),
@@ -426,15 +436,20 @@
     devices = lax.axis_size("wide") * lax.axis_size("narrow")
     dma = pltpu.SemaphoreType.DMA
     own = ((3, 4, 8, LANES), f32)
-    box = ((3, PAIRS, ROWS, LANES), f32)
+    box = (3, PAIRS, ROWS, LANES)
     wide_type = ((48, LANES), f32)
     narrow_type = ((72, LANES), f32)
-    payload_type = ((devices, 3, LANES), f32)
-    coarse_scratch = [
-        pltpu.VMEM(box[0], f32),
+    payload_type = ((devices * 3, LANES), f32)
+    scratch = [
+        pltpu.VMEM(box, f32),
+        pltpu.VMEM(box, f32),
         pltpu.VMEM((AGG_LOC, LANES), f32),
         pltpu.VMEM((4, devices // 4 + 8, LANES), f32),
-        pltpu.VMEM(coarse_inverse.shape, f32),
+        pltpu.VMEM(payload_type[0], f32),
+        pltpu.VMEM(box, f32),
+        pltpu.VMEM(box, f32),
+        pltpu.VMEM(tile_factors.shape, tile_factors.dtype),
+        dma((6,)),
         dma,
     ]
 
@@ -464,42 +479,34 @@
     far, near = swaps("wide", far, near)
     low, high = call(pack_narrow, "pack_narrow", [((NARROW_ROWS, LANES), f32)] * 2, [], [far, near, mine])
     low, high = swaps("narrow", low, high)
-    coef, slots, misfit, payload = call(
-        first_misfit,
-        "first_misfit",
-        [((N_COEF, 6, ROWS, LANES), f32), ((PAIRS, ROWS, LANES), jnp.int32), box, payload_type],
-        [pltpu.VMEM((4, PAIRS, ROWS, LANES), f32)] + coarse_scratch,
-        [far, near, low, high, mine, agg, coarse_inverse],
-        in_hbm=(6,),
+    coef, slots, payload, current, far, near = call(
+        first_sweep,
+        "first_sweep",
+        [((N_COEF, 6, ROWS, LANES), f32), ((PAIRS, ROWS, LANES), jnp.int32), payload_type, own, wide_type, wide_type],
+        [pltpu.VMEM((4, PAIRS, ROWS, LANES), f32)] + scratch,
+        [far, near, low, high, mine, agg, coarse_inverse, tile_factors],
+        in_hbm=(7,),
+        out_hbm=(2,),
     )
-    current, first = mine, 3
     for sweep in range(SWEEPS):
-        received = lax.all_to_all(payload, ("wide", "narrow"), 0, 0)
-        current, far, near = call(
-            functools.partial(local_solve, first=first),
-            "local_solve",
-            [own, wide_type, wide_type],
-            [pltpu.VMEM(box[0], f32)] * 2 + [pltpu.VMEM(tile_factors.shape, tile_factors.dtype), dma((6,))],
-            [misfit, coef, current, tile_factors],
-            in_hbm=(3,),
-            flops=30000000,
-        )
-        first = 0
+        blocks = payload.reshape(devices, 1, 3 * LANES)
+        received = lax.all_to_all(blocks, ("wide", "narrow"), 0, 0).reshape(payload_type[0])
         far, near = swaps("wide", far, near)
         low, high = call(pack_current, "pack_current", [narrow_type] * 2, [], [current, far, near])
         low, high = swaps("narrow", low, high)
         known = [current, far, near, low, high, received, slots, coef]
         if sweep < SWEEPS - 1:
-            current, misfit, payload = call(
-                next_misfit,
-                "next_misfit",
-                [own, box, payload_type],
-                coarse_scratch,
-                known + [agg, coarse_inverse],
-                in_hbm=(9,),
+            payload, current, far, near = call(
+                next_sweep,
+                "next_sweep",
+                [payload_type, own, wide_type, wide_type],
+                scratch,
+                known + [agg, coarse_inverse, tile_factors],
+                in_hbm=(10,),
+                out_hbm=(0,),
             )
         else:
-            iterate, residual = call(last_misfit, "last_misfit", [own, own], [pltpu.VMEM(box[0], f32)], known)
+            iterate, residual = call(last_misfit, "last_misfit", [own, own], [pltpu.VMEM(box, f32)], known)
     return iterate, residual
 
 

time: 126 us -> 124 us (0.984)
  Pallas kernels: 23.8 us -> 16.8 us
  waiting for transfers between devices: 31.5 us -> 34.6 us
  starting transfers between devices: 69 us -> 70.7 us
    pallas_call x12 -> x9, Pallas kernels: 23.8 us -> 16.8 us  [call(): pl.pallas_call(body, out_shape=[pltpu.HBM(shape, dtype) if i in out_hbm e...]
    ppermute x8, waiting for transfers between devices: 29.2 us -> 32.2 us  [swaps(): lax.ppermute(far, axis, [(i, (i + (1 if i % 2 else -1)) % count) for i in...]
    ppermute x8, starting transfers between devices: 45.7 us -> 47 us  [swaps(): lax.ppermute(far, axis, [(i, (i + (1 if i % 2 else -1)) % count) for i in...]
  transfers between devices with their start and end apart: 19 -> 19, of which waited for: 9 -> 9; matrix products, arithmetic and copies ran while one was open for 0% -> 0% of each run, Pallas kernels for 11% -> 0%
where the time goes in v2:
time: 124 us
  starting transfers between devices  70.7 us (57%)
  waiting for transfers between devices  34.6 us (28%)
  Pallas kernels  16.8 us (14%)
    ppermute x8, starting transfers between devices, swaps(): lax.ppermute(far, axis, [(i, (i + (1 if i % 2 else -1)) % count) for i in...  47 us
    ppermute x8, waiting for transfers between devices, swaps(): lax.ppermute(far, axis, [(i, (i + (1 if i % 2 else -1)) % count) for i in...  32.2 us
    all_to_all x3, starting transfers between devices, per_device(): lax.all_to_all(blocks, ('wide', 'narrow'), 0, 0).reshape(payload_type[0])  23.7 us
    pallas_call x9, Pallas kernels, call(): pl.pallas_call(body, out_shape=[pltpu.HBM(shape, dtype) if i in out_hbm e...  16.8 us
  transfers between devices with their start and end apart: 19, of which 9 were waited for; matrix products, arithmetic and copies ran while one was open for 0% of the time, Pallas kernels for 0%

profile of v2, /device:TPU:1, one launch (start us, length us, event | category | flops | bytes accessed | tf_op | source)
XLA Modules:
  0.0 124.1 jit_solution(18194980514762779162)
XLA Ops:
  1.8 11.4 %collective-permute-start = (f32[216,128]{1,0:T(8,128)S(1)}, f32[216,128]{1,0:T(8,128)S(1)}, u32[]{:S(2)}, u32[]{:S(2)}) collective-permute-start(f32[216,128]{1,0:T(8,128)S(1)} %get-tuple-element.28), channel_id=1, source_target_pairs={{0,252},{4,8},{8,4},{12,16},{16,12},{20,24},{24,20},{28,32},{32,28... | collective-permute-start | bytes 331784 | tf_op jit(solution)/shard_map/wide_far/ppermute | solution.py:427
  13.2 2.8 %collective-permute-done.far = f32[216,128]{1,0:T(8,128)S(1)} collective-permute-done((f32[216,128]{1,0:T(8,128)S(1)}, f32[216,128]{1,0:T(8,128)S(1)}, u32[]{:S(2)}, u32[]{:S(2)}) %collective-permute-start) | collective-permute-done | bytes 110624 | tf_op jit(solution)/shard_map/wide_far/ppermute | solution.py:427
  15.9 2.3 %collective-permute-done.1.near = f32[216,128]{1,0:T(8,128)S(1)} collective-permute-done((f32[216,128]{1,0:T(8,128)S(1)}, f32[216,128]{1,0:T(8,128)S(1)}, u32[]{:S(2)}, u32[]{:S(2)}) %collective-permute-start.1) | collective-permute-done | bytes 110624 | tf_op jit(solution)/shard_map/wide_near/ppermute | solution.py:429
  18.4 2.4 %collective-permute-start.2 = (f32[324,128]{1,0:T(8,128)S(1)}, f32[324,128]{1,0:T(8,128)S(1)}, u32[]{:S(2)}, u32[]{:S(2)}) collective-permute-start(f32[324,128]{1,0:T(8,128)S(1)} %get-tuple-element.31), channel_id=1, source_target_pairs={{0,3},{1,2},{2,1},{3,0},{4,7},{5,6},{6,5},{7,4},{8,11},{9,10},{10,... | collective-permute-start | bytes 497672 | tf_op jit(solution)/shard_map/narrow_far/ppermute | solution.py:427
  20.8 4.3 %collective-permute-done.2.low = f32[324,128]{1,0:T(8,128)S(1)} collective-permute-done((f32[324,128]{1,0:T(8,128)S(1)}, f32[324,128]{1,0:T(8,128)S(1)}, u32[]{:S(2)}, u32[]{:S(2)}) %collective-permute-start.2) | collective-permute-done | bytes 165920 | tf_op jit(solution)/shard_map/narrow_far/ppermute | solution.py:427
  25.0 1.2 copy-done
  26.3 4.7 %first_sweep.1 = (f32[22,6,16,128]{3,2,1,0:T(8,128)S(1)}, s32[8,16,128]{2,1,0:T(8,128)S(1)}, f32[768,128]{1,0:T(8,128)}, f32[3,4,8,128]{3,2,1,0:T(8,128)S(1)}, f...) custom-call(f32[216,128]{1,0:T(8,128)S(1)} %collective-permute-done.far, f32[216,128]{1,0:T(8,128)S(1)} %collective-permute-done.1.near, ...), custom_call_target="tpu_custom_call" | custom-call | flops 1000000 | tf_op jit(solution)/shard_map/first_sweep/pallas_call | solution.py:409
  31.0 8.6 %all-to-all-start = ((f32[256,1,384]{2,1,0:T(1,128)}), f32[256,1,384]{2,1,0:T(1,128)S(1)}, u32[]{:S(2)}, u32[]{:S(2)}) async-start(f32[256,1,384]{2,1,0:T(1,128)} %bitcast.12), calls=%async_computation | async-start | bytes 786432 | tf_op jit(solution)/shard_map/all_to_all | solution.py:493
  39.6 9.1 %collective-permute-start.4 = (f32[48,128]{1,0:T(8,128)S(1)}, f32[48,128]{1,0:T(8,128)S(1)}, u32[]{:S(2)}, u32[]{:S(2)}) collective-permute-start(f32[48,128]{1,0:T(8,128)S(1)} %get-tuple-element.35), channel_id=1, source_target_pairs={{0,252},{4,8},{8,4},{12,16},{16,12},{20,24},{24,20},{28,32},{32,28... | collective-permute-start | bytes 73736 | tf_op jit(solution)/shard_map/wide_far/ppermute | solution.py:427
  48.7 6.8 %collective-permute-done.4.far = f32[48,128]{1,0:T(8,128)S(1)} collective-permute-done((f32[48,128]{1,0:T(8,128)S(1)}, f32[48,128]{1,0:T(8,128)S(1)}, u32[]{:S(2)}, u32[]{:S(2)}) %collective-permute-start.4) | collective-permute-done | bytes 24608 | tf_op jit(solution)/shard_map/wide_far/ppermute | solution.py:427
  55.6 1.9 %collective-permute-start.6 = (f32[72,128]{1,0:T(8,128)S(1)}, f32[72,128]{1,0:T(8,128)S(1)}, u32[]{:S(2)}, u32[]{:S(2)}) collective-permute-start(f32[72,128]{1,0:T(8,128)S(1)} %get-tuple-element.37), channel_id=1, source_target_pairs={{0,3},{1,2},{2,1},{3,0},{4,7},{5,6},{6,5},{7,4},{8,11},{9,10},{10,... | collective-permute-start | bytes 110600 | tf_op jit(solution)/shard_map/narrow_far/ppermute | solution.py:427
  57.5 1.6 %collective-permute-done.6.low = f32[72,128]{1,0:T(8,128)S(1)} collective-permute-done((f32[72,128]{1,0:T(8,128)S(1)}, f32[72,128]{1,0:T(8,128)S(1)}, u32[]{:S(2)}, u32[]{:S(2)}) %collective-permute-start.6) | collective-permute-done | bytes 36896 | tf_op jit(solution)/shard_map/narrow_far/ppermute | solution.py:427
  59.1 4.9 %next_sweep.2 = (f32[768,128]{1,0:T(8,128)}, f32[3,4,8,128]{3,2,1,0:T(8,128)S(1)}, f32[48,128]{1,0:T(8,128)S(1)}, f32[48,128]{1,0:T(8,128)S(1)}) custom-call(f32[3,4,8,128]{3,2,1,0:T(8,128)S(1)} %get-tuple-element.34.current, f32[48,128]{1,0:T(8,128)S(1)} %collective-permute-done.4.far, f32[48,128]{1,0:T(8,128)S(1)} %collective-permute-done.5.near, ...), custom_call_target="tpu_custom_call" | custom-call | flops 1000000 | tf_op jit(solution)/shard_map/next_sweep/pallas_call | solution.py:409
  64.1 7.6 %all-to-all-start.1 = ((f32[256,1,384]{2,1,0:T(1,128)}), f32[256,1,384]{2,1,0:T(1,128)S(1)}, u32[]{:S(2)}, u32[]{:S(2)}) async-start(f32[256,1,384]{2,1,0:T(1,128)} %bitcast.14), calls=%async_computation.1 | async-start | bytes 786432 | tf_op jit(solution)/shard_map/all_to_all | solution.py:493
  71.7 9.3 %collective-permute-start.8 = (f32[48,128]{1,0:T(8,128)S(1)}, f32[48,128]{1,0:T(8,128)S(1)}, u32[]{:S(2)}, u32[]{:S(2)}) collective-permute-start(f32[48,128]{1,0:T(8,128)S(1)} %get-tuple-element.43), channel_id=1, source_target_pairs={{0,252},{4,8},{8,4},{12,16},{16,12},{20,24},{24,20},{28,32},{32,28... | collective-permute-start | bytes 73736 | tf_op jit(solution)/shard_map/wide_far/ppermute | solution.py:427
  81.0 6.6 %collective-permute-done.8.far = f32[48,128]{1,0:T(8,128)S(1)} collective-permute-done((f32[48,128]{1,0:T(8,128)S(1)}, f32[48,128]{1,0:T(8,128)S(1)}, u32[]{:S(2)}, u32[]{:S(2)}) %collective-permute-start.8) | collective-permute-done | bytes 24608 | tf_op jit(solution)/shard_map/wide_far/ppermute | solution.py:427
  87.7 1.9 %collective-permute-start.10 = (f32[72,128]{1,0:T(8,128)S(1)}, f32[72,128]{1,0:T(8,128)S(1)}, u32[]{:S(2)}, u32[]{:S(2)}) collective-permute-start(f32[72,128]{1,0:T(8,128)S(1)} %get-tuple-element.45), channel_id=1, source_target_pairs={{0,3},{1,2},{2,1},{3,0},{4,7},{5,6},{6,5},{7,4},{8,11},{9,10},{10,... | collective-permute-start | bytes 110600 | tf_op jit(solution)/shard_map/narrow_far/ppermute | solution.py:427
  89.5 1.6 %collective-permute-done.10.low = f32[72,128]{1,0:T(8,128)S(1)} collective-permute-done((f32[72,128]{1,0:T(8,128)S(1)}, f32[72,128]{1,0:T(8,128)S(1)}, u32[]{:S(2)}, u32[]{:S(2)}) %collective-permute-start.10) | collective-permute-done | bytes 36896 | tf_op jit(solution)/shard_map/narrow_far/ppermute | solution.py:427
  91.2 4.9 %next_sweep.3 = (f32[768,128]{1,0:T(8,128)}, f32[3,4,8,128]{3,2,1,0:T(8,128)S(1)}, f32[48,128]{1,0:T(8,128)S(1)}, f32[48,128]{1,0:T(8,128)S(1)}) custom-call(f32[3,4,8,128]{3,2,1,0:T(8,128)S(1)} %get-tuple-element.42.current, f32[48,128]{1,0:T(8,128)S(1)} %collective-permute-done.8.far, f32[48,128]{1,0:T(8,128)S(1)} %collective-permute-done.9.near, ...), custom_call_target="tpu_custom_call" | custom-call | flops 1000000 | tf_op jit(solution)/shard_map/next_sweep/pallas_call | solution.py:409
  96.1 7.6 %all-to-all-start.2 = ((f32[256,1,384]{2,1,0:T(1,128)}), f32[256,1,384]{2,1,0:T(1,128)S(1)}, u32[]{:S(2)}, u32[]{:S(2)}) async-start(f32[256,1,384]{2,1,0:T(1,128)} %bitcast.13), calls=%async_computation.2 | async-start | bytes 786432 | tf_op jit(solution)/shard_map/all_to_all | solution.py:493
  103.7 9.1 %collective-permute-start.12 = (f32[48,128]{1,0:T(8,128)S(1)}, f32[48,128]{1,0:T(8,128)S(1)}, u32[]{:S(2)}, u32[]{:S(2)}) collective-permute-start(f32[48,128]{1,0:T(8,128)S(1)} %get-tuple-element.49), channel_id=1, source_target_pairs={{0,252},{4,8},{8,4},{12,16},{16,12},{20,24},{24,20},{28,32},{32,28... | collective-permute-start | bytes 73736 | tf_op jit(solution)/shard_map/wide_far/ppermute | solution.py:427
  112.8 6.8 %collective-permute-done.12.far = f32[48,128]{1,0:T(8,128)S(1)} collective-permute-done((f32[48,128]{1,0:T(8,128)S(1)}, f32[48,128]{1,0:T(8,128)S(1)}, u32[]{:S(2)}, u32[]{:S(2)}) %collective-permute-start.12) | collective-permute-done | bytes 24608 | tf_op jit(solution)/shard_map/wide_far/ppermute | solution.py:427
  119.7 1.9 %collective-permute-start.14 = (f32[72,128]{1,0:T(8,128)S(1)}, f32[72,128]{1,0:T(8,128)S(1)}, u32[]{:S(2)}, u32[]{:S(2)}) collective-permute-start(f32[72,128]{1,0:T(8,128)S(1)} %get-tuple-element.51), channel_id=1, source_target_pairs={{0,3},{1,2},{2,1},{3,0},{4,7},{5,6},{6,5},{7,4},{8,11},{9,10},{10,... | collective-permute-start | bytes 110600 | tf_op jit(solution)/shard_map/narrow_far/ppermute | solution.py:427
  121.6 1.6 %collective-permute-done.14.low = f32[72,128]{1,0:T(8,128)S(1)} collective-permute-done((f32[72,128]{1,0:T(8,128)S(1)}, f32[72,128]{1,0:T(8,128)S(1)}, u32[]{:S(2)}, u32[]{:S(2)}) %collective-permute-start.14) | collective-permute-done | bytes 36896 | tf_op jit(solution)/shard_map/narrow_far/ppermute | solution.py:427
  (27 shorter events, 2.2 us)
Async XLA Ops:
  1.8 14.2 %collective-permute-start = (f32[216,128]{1,0:T(8,128)S(1)}, f32[216,128]{1,0:T(8,128)S(1)}, u32[]{:S(2)}, u32[]{:S(2)}) collective-permute-start(f32[216,128]{1,0:T(8,128)S(1)} %get-tuple-element.28), channel_id=1, source_target_pairs={{0,252},{4,8},{8,4},{12,16},{16,12},{20,24},{24,20},{28,32},{32,28... | collective-permute-start | bytes 331784 | tf_op jit(solution)/shard_map/wide_far/ppermute | solution.py:427
  13.2 5.1 %collective-permute-start.1 = (f32[216,128]{1,0:T(8,128)S(1)}, f32[216,128]{1,0:T(8,128)S(1)}, u32[]{:S(2)}, u32[]{:S(2)}) collective-permute-start(f32[216,128]{1,0:T(8,128)S(1)} %get-tuple-element.29), channel_id=1, source_target_pairs={{0,4},{4,0},{8,12},{12,8},{16,20},{20,16},{24,28},{28,24},{32,36},... | collective-permute-start | bytes 331784 | tf_op jit(solution)/shard_map/wide_near/ppermute | solution.py:429
  18.4 6.7 %collective-permute-start.2 = (f32[324,128]{1,0:T(8,128)S(1)}, f32[324,128]{1,0:T(8,128)S(1)}, u32[]{:S(2)}, u32[]{:S(2)}) collective-permute-start(f32[324,128]{1,0:T(8,128)S(1)} %get-tuple-element.31), channel_id=1, source_target_pairs={{0,3},{1,2},{2,1},{3,0},{4,7},{5,6},{6,5},{7,4},{8,11},{9,10},{10,... | collective-permute-start | bytes 497672 | tf_op jit(solution)/shard_map/narrow_far/ppermute | solution.py:427
  20.7 4.3 %collective-permute-start.3 = (f32[324,128]{1,0:T(8,128)S(1)}, f32[324,128]{1,0:T(8,128)S(1)}, u32[]{:S(2)}, u32[]{:S(2)}) collective-permute-start(f32[324,128]{1,0:T(8,128)S(1)} %get-tuple-element.32), channel_id=1, source_target_pairs={{0,1},{1,0},{2,3},{3,2},{4,5},{5,4},{6,7},{7,6},{8,9},{9,8},{10,11... | collective-permute-start | bytes 497672 | tf_op jit(solution)/shard_map/narrow_near/ppermute | solution.py:429
  25.0 1.2 copy-start
  26.3 32.8 %copy-start.1 = (f32[32,8192]{1,0:T(8,128)S(1)}, f32[32,8192]{1,0:T(8,128)}, u32[]{:S(2)}) copy-start(f32[32,8192]{1,0:T(8,128)} %coarse.5) | copy-start | bytes 3145732
  31.0 28.1 %all-to-all-start = ((f32[256,1,384]{2,1,0:T(1,128)}), f32[256,1,384]{2,1,0:T(1,128)S(1)}, u32[]{:S(2)}, u32[]{:S(2)}) async-start(f32[256,1,384]{2,1,0:T(1,128)} %bitcast.12), calls=%async_computation | async-start | bytes 786432 | tf_op jit(solution)/shard_map/all_to_all | solution.py:493
  39.6 16.0 %collective-permute-start.4 = (f32[48,128]{1,0:T(8,128)S(1)}, f32[48,128]{1,0:T(8,128)S(1)}, u32[]{:S(2)}, u32[]{:S(2)}) collective-permute-start(f32[48,128]{1,0:T(8,128)S(1)} %get-tuple-element.35), channel_id=1, source_target_pairs={{0,252},{4,8},{8,4},{12,16},{16,12},{20,24},{24,20},{28,32},{32,28... | collective-permute-start | bytes 73736 | tf_op jit(solution)/shard_map/wide_far/ppermute | solution.py:427
  48.7 6.8 %collective-permute-start.5 = (f32[48,128]{1,0:T(8,128)S(1)}, f32[48,128]{1,0:T(8,128)S(1)}, u32[]{:S(2)}, u32[]{:S(2)}) collective-permute-start(f32[48,128]{1,0:T(8,128)S(1)} %get-tuple-element.36), channel_id=1, source_target_pairs={{0,4},{4,0},{8,12},{12,8},{16,20},{20,16},{24,28},{28,24},{32,36},... | collective-permute-start | bytes 73736 | tf_op jit(solution)/shard_map/wide_near/ppermute | solution.py:429
  55.6 3.5 %collective-permute-start.6 = (f32[72,128]{1,0:T(8,128)S(1)}, f32[72,128]{1,0:T(8,128)S(1)}, u32[]{:S(2)}, u32[]{:S(2)}) collective-permute-start(f32[72,128]{1,0:T(8,128)S(1)} %get-tuple-element.37), channel_id=1, source_target_pairs={{0,3},{1,2},{2,1},{3,0},{4,7},{5,6},{6,5},{7,4},{8,11},{9,10},{10,... | collective-permute-start | bytes 110600 | tf_op jit(solution)/shard_map/narrow_far/ppermute | solution.py:427
  57.5 1.6 %collective-permute-start.7 = (f32[72,128]{1,0:T(8,128)S(1)}, f32[72,128]{1,0:T(8,128)S(1)}, u32[]{:S(2)}, u32[]{:S(2)}) collective-permute-start(f32[72,128]{1,0:T(8,128)S(1)} %get-tuple-element.38), channel_id=1, source_target_pairs={{0,1},{1,0},{2,3},{3,2},{4,5},{5,4},{6,7},{7,6},{8,9},{9,8},{10,11... | collective-permute-start | bytes 110600 | tf_op jit(solution)/shard_map/narrow_near/ppermute | solution.py:429
  64.1 27.1 %all-to-all-start.1 = ((f32[256,1,384]{2,1,0:T(1,128)}), f32[256,1,384]{2,1,0:T(1,128)S(1)}, u32[]{:S(2)}, u32[]{:S(2)}) async-start(f32[256,1,384]{2,1,0:T(1,128)} %bitcast.14), calls=%async_computation.1 | async-start | bytes 786432 | tf_op jit(solution)/shard_map/all_to_all | solution.py:493
  71.7 16.0 %collective-permute-start.8 = (f32[48,128]{1,0:T(8,128)S(1)}, f32[48,128]{1,0:T(8,128)S(1)}, u32[]{:S(2)}, u32[]{:S(2)}) collective-permute-start(f32[48,128]{1,0:T(8,128)S(1)} %get-tuple-element.43), channel_id=1, source_target_pairs={{0,252},{4,8},{8,4},{12,16},{16,12},{20,24},{24,20},{28,32},{32,28... | collective-permute-start | bytes 73736 | tf_op jit(solution)/shard_map/wide_far/ppermute | solution.py:427
  81.0 6.6 %collective-permute-start.9 = (f32[48,128]{1,0:T(8,128)S(1)}, f32[48,128]{1,0:T(8,128)S(1)}, u32[]{:S(2)}, u32[]{:S(2)}) collective-permute-start(f32[48,128]{1,0:T(8,128)S(1)} %get-tuple-element.44), channel_id=1, source_target_pairs={{0,4},{4,0},{8,12},{12,8},{16,20},{20,16},{24,28},{28,24},{32,36},... | collective-permute-start | bytes 73736 | tf_op jit(solution)/shard_map/wide_near/ppermute | solution.py:429
  87.7 3.5 %collective-permute-start.10 = (f32[72,128]{1,0:T(8,128)S(1)}, f32[72,128]{1,0:T(8,128)S(1)}, u32[]{:S(2)}, u32[]{:S(2)}) collective-permute-start(f32[72,128]{1,0:T(8,128)S(1)} %get-tuple-element.45), channel_id=1, source_target_pairs={{0,3},{1,2},{2,1},{3,0},{4,7},{5,6},{6,5},{7,4},{8,11},{9,10},{10,... | collective-permute-start | bytes 110600 | tf_op jit(solution)/shard_map/narrow_far/ppermute | solution.py:427
  89.5 1.6 %collective-permute-start.11 = (f32[72,128]{1,0:T(8,128)S(1)}, f32[72,128]{1,0:T(8,128)S(1)}, u32[]{:S(2)}, u32[]{:S(2)}) collective-permute-start(f32[72,128]{1,0:T(8,128)S(1)} %get-tuple-element.46), channel_id=1, source_target_pairs={{0,1},{1,0},{2,3},{3,2},{4,5},{5,4},{6,7},{7,6},{8,9},{9,8},{10,11... | collective-permute-start | bytes 110600 | tf_op jit(solution)/shard_map/narrow_near/ppermute | solution.py:429
  96.1 27.1 %all-to-all-start.2 = ((f32[256,1,384]{2,1,0:T(1,128)}), f32[256,1,384]{2,1,0:T(1,128)S(1)}, u32[]{:S(2)}, u32[]{:S(2)}) async-start(f32[256,1,384]{2,1,0:T(1,128)} %bitcast.13), calls=%async_computation.2 | async-start | bytes 786432 | tf_op jit(solution)/shard_map/all_to_all | solution.py:493
  103.7 16.0 %collective-permute-start.12 = (f32[48,128]{1,0:T(8,128)S(1)}, f32[48,128]{1,0:T(8,128)S(1)}, u32[]{:S(2)}, u32[]{:S(2)}) collective-permute-start(f32[48,128]{1,0:T(8,128)S(1)} %get-tuple-element.49), channel_id=1, source_target_pairs={{0,252},{4,8},{8,4},{12,16},{16,12},{20,24},{24,20},{28,32},{32,28... | collective-permute-start | bytes 73736 | tf_op jit(solution)/shard_map/wide_far/ppermute | solution.py:427
  112.8 6.8 %collective-permute-start.13 = (f32[48,128]{1,0:T(8,128)S(1)}, f32[48,128]{1,0:T(8,128)S(1)}, u32[]{:S(2)}, u32[]{:S(2)}) collective-permute-start(f32[48,128]{1,0:T(8,128)S(1)} %get-tuple-element.50), channel_id=1, source_target_pairs={{0,4},{4,0},{8,12},{12,8},{16,20},{20,16},{24,28},{28,24},{32,36},... | collective-permute-start | bytes 73736 | tf_op jit(solution)/shard_map/wide_near/ppermute | solution.py:429
  119.7 3.5 %collective-permute-start.14 = (f32[72,128]{1,0:T(8,128)S(1)}, f32[72,128]{1,0:T(8,128)S(1)}, u32[]{:S(2)}, u32[]{:S(2)}) collective-permute-start(f32[72,128]{1,0:T(8,128)S(1)} %get-tuple-element.51), channel_id=1, source_target_pairs={{0,3},{1,2},{2,1},{3,0},{4,7},{5,6},{6,5},{7,4},{8,11},{9,10},{10,... | collective-permute-start | bytes 110600 | tf_op jit(solution)/shard_map/narrow_far/ppermute | solution.py:427
  121.6 1.6 %collective-permute-start.15 = (f32[72,128]{1,0:T(8,128)S(1)}, f32[72,128]{1,0:T(8,128)S(1)}, u32[]{:S(2)}, u32[]{:S(2)}) collective-permute-start(f32[72,128]{1,0:T(8,128)S(1)} %get-tuple-element.52), channel_id=1, source_target_pairs={{0,1},{1,0},{2,3},{3,2},{4,5},{5,4},{6,7},{7,6},{8,9},{9,8},{10,11... | collective-permute-start | bytes 110600 | tf_op jit(solution)/shard_map/narrow_near/ppermute | solution.py:429

commit v3 on v2

--- a/solution.py
+++ b/solution.py
@@ -161,7 +161,15 @@
             high[at : at + 2] = pick(narrow_odd, v[0:2], v[6:8])
 
 
-def pack_current(current, far, near, low, high):
+def pack_current(current, far, near, received, low, high, part):
+    total = received[0:24]
+    for i in range(24, received.shape[0], 24):
+        total += received[i : i + 24]
+    block_of = lax.broadcasted_iota(jnp.int32, (24, LANES), 0) % 3
+    part[...] = jnp.zeros((8, LANES), f32)
+    for k in range(3):
+        part[k : k + 1, :] = jnp.sum(jnp.where(block_of == k, total, 0.0), axis=0, keepdims=True)
+    high[72:80] = part[...]
     odd = is_odd("wide")
     narrow_odd = is_odd("narrow")
     for c in range(3):
@@ -182,18 +190,14 @@
     count = coarse.shape[1] // LANES
     for w in range(count):
         row = jnp.sum(coarse[:, w * LANES : (w + 1) * LANES] * weight, axis=0, keepdims=True)
-        spread[1, w + 1 : w + 2, :] = row
-    middle = spread[1, 1 : count + 1, :]
-    for n in range(4):
-        turned = middle if n == 1 else shifted(middle, 32 * (n - 1), 1)
-        if n != 1:
-            spread[n, 1 : count + 1, :] = turned
-        spread[n, 0:1, :] = turned[count - 1 : count]
-        spread[n, count + 1 : count + 2, :] = turned[0:1]
+        spread[w + 1 : w + 2, :] = row
+    spread[0:1, :] = spread[count : count + 1, :]
+    spread[count + 1 : count + 2, :] = spread[1:2, :]
     for w in range(count):
-        for n in range(4):
-            at = 3 * (4 * w + n)
-            staged[at : at + 3, :] = spread[n, w : w + 3, :]
+        rows = spread[w : w + 3, :]
+        for half in range(2):
+            at = 3 * (2 * w + half)
+            staged[at : at + 3, :] = rows
 
 
 def solve_box(values, coef, agg, coarse, factors_hbm, payload, current, far, near, scratch):
@@ -221,7 +225,8 @@
 
 
 def fetch_tiles(factors_hbm, factors, sems):
-    return [pltpu.make_async_copy(factors_hbm.at[a], factors.at[a], sems.at[a]) for a in range(6)]
+    cols = [slice(1, 11) if a in (0, 5) else slice(0, 12) for a in range(6)]
+    return [pltpu.make_async_copy(factors_hbm.at[a, cols[a]], factors.at[a, cols[a]], sems.at[a]) for a in range(6)]
 
 
 def first_sweep(
@@ -269,7 +274,9 @@
     row = lax.broadcasted_iota(jnp.int32, (ROWS, LANES), 0)
     lane = lane_index((ROWS, LANES))
     low = lane < 64
-    offset = jnp.where(row < 8, 32, jnp.where(row < 12, 64, 0))
+    place_of = lax.axis_index("narrow")
+    below, here, above = (32 * ((place_of + i) % 4) for i in (3, 0, 1))
+    offset = jnp.where(row < 8, here, jnp.where(row < 12, above, below))
     inside = box_mask()
     for a in range(8):
         slots[a] = rim[3, a].astype(jnp.int32) + offset
@@ -293,18 +300,14 @@
     solve_box(values, coef, agg, coarse, factors_hbm, payload, current, far_out, near_out, scratch)
 
 
-def gather_values(current, far, near, low, high, received, slots, values):
+def gather_values(current, far, near, low, high, part, slots, values):
     odd = is_odd("wide")
     narrow_odd = is_odd("narrow")
-    total = received[0:24]
-    for i in range(24, received.shape[0], 24):
-        total += received[i : i + 24]
-    block_of = lax.broadcasted_iota(jnp.int32, (24, LANES), 0) % 3
-    totals = [jnp.sum(jnp.where(block_of == k, total, 0.0), axis=0, keepdims=True) for k in range(3)]
+    total = part[...] + high[72:80]
     blank = jnp.zeros((2, LANES), f32)
     for a in range(8):
         block = 0 if a < 2 else 2 if a >= 6 else 1
-        table = jnp.broadcast_to(totals[block], (8, LANES))
+        table = jnp.broadcast_to(total[block : block + 1], (8, LANES))
         for c in range(3):
             at = (c * 8 + a) * 3
             first, second = low[at : at + 3], high[at : at + 3]
@@ -324,7 +327,7 @@
     near,
     low,
     high,
-    received,
+    part,
     slots,
     coef,
     agg,
@@ -339,12 +342,12 @@
 ):
     for fetch in fetch_tiles(factors_hbm, scratch[-3], scratch[-2]):
         fetch.start()
-    gather_values(current, far, near, low, high, received, slots, values)
+    gather_values(current, far, near, low, high, part, slots, values)
     solve_box(values, coef, agg, coarse, factors_hbm, payload, moved, far_out, near_out, scratch)
 
 
-def last_misfit(current, far, near, low, high, received, slots, coef, iterate, residual, values):
-    gather_values(current, far, near, low, high, received, slots, values)
+def last_misfit(current, far, near, low, high, part, slots, coef, iterate, residual, values):
+    gather_values(current, far, near, low, high, part, slots, values)
     rolled = {}
     for a in range(2, 6):
         applied = operate_pair(values, coef, a, rolled)
@@ -434,17 +437,19 @@
     rhs, start, trans, accum, coupling, well_cells, well_index, agg_map, tile_factors, coarse_inverse
 ):
     devices = lax.axis_size("wide") * lax.axis_size("narrow")
+    members = devices // 2
+    groups = [[4 * w + n for w in range(devices // 4) for n in (parity, parity + 2)] for parity in range(2)]
     dma = pltpu.SemaphoreType.DMA
     own = ((3, 4, 8, LANES), f32)
     box = (3, PAIRS, ROWS, LANES)
     wide_type = ((48, LANES), f32)
     narrow_type = ((72, LANES), f32)
-    payload_type = ((devices * 3, LANES), f32)
+    payload_type = ((members * 3, LANES), f32)
     scratch = [
         pltpu.VMEM(box, f32),
         pltpu.VMEM(box, f32),
         pltpu.VMEM((AGG_LOC, LANES), f32),
-        pltpu.VMEM((4, devices // 4 + 8, LANES), f32),
+        pltpu.VMEM((devices // 4 + 8, LANES), f32),
         pltpu.VMEM(payload_type[0], f32),
         pltpu.VMEM(box, f32),
         pltpu.VMEM(box, f32),
@@ -489,12 +494,18 @@
         out_hbm=(2,),
     )
     for sweep in range(SWEEPS):
-        blocks = payload.reshape(devices, 1, 3 * LANES)
-        received = lax.all_to_all(blocks, ("wide", "narrow"), 0, 0).reshape(payload_type[0])
+        blocks = payload.reshape(members, 1, 3 * LANES)
+        received = lax.all_to_all(blocks, ("wide", "narrow"), 0, 0, axis_index_groups=groups).reshape(payload_type[0])
         far, near = swaps("wide", far, near)
-        low, high = call(pack_current, "pack_current", [narrow_type] * 2, [], [current, far, near])
+        low, high, part = call(
+            pack_current,
+            "pack_current",
+            [narrow_type, ((80, LANES), f32), ((8, LANES), f32)],
+            [],
+            [current, far, near, received],
+        )
         low, high = swaps("narrow", low, high)
-        known = [current, far, near, low, high, received, slots, coef]
+        known = [current, far, near, low, high, part, slots, coef]
         if sweep < SWEEPS - 1:
             payload, current, far, near = call(
                 next_sweep,

time: 124 us -> 118 us (0.952)
  starting transfers between devices: 70.7 us -> 66.3 us
  waiting for transfers between devices: 34.6 us -> 33.3 us
    ppermute x8, starting transfers between devices: 47 us -> 36.3 us  [swaps(): lax.ppermute(far, axis, [(i, (i + (1 if i % 2 else -1)) % count) for i in...]
    ppermute x8, starting transfers between devices: 0.02 us -> 7.5 us  [swaps(): near = lax.ppermute(near, axis, [(i, i ^ 1) for i in range(count)])]
    ppermute x8, waiting for transfers between devices: 32.2 us -> 25.3 us  [swaps(): lax.ppermute(far, axis, [(i, (i + (1 if i % 2 else -1)) % count) for i in...]
    ppermute x8, waiting for transfers between devices: 2.36 us -> 6.6 us  [swaps(): near = lax.ppermute(near, axis, [(i, i ^ 1) for i in range(count)])]
    all_to_all x3, waiting for transfers between devices: 0.01 us -> 1.4 us  [per_device(): lax.all_to_all(blocks, ('wide', 'narrow'), 0, 0, axis_index_groups=groups)]
    all_to_all x3, starting transfers between devices: 23.7 us -> 22.5 us  [per_device(): lax.all_to_all(blocks, ('wide', 'narrow'), 0, 0, axis_index_groups=groups)]
  transfers between devices with their start and end apart: 19 -> 19, of which waited for: 9 -> 15; matrix products, arithmetic and copies ran while one was open for 0% -> 0% of each run, Pallas kernels for 0% -> 0%
where the time goes in v3:
time: 118 us
  starting transfers between devices  66.3 us (56%)
  waiting for transfers between devices  33.3 us (28%)
  Pallas kernels  16.1 us (14%)
  local copies, waits for them, and re-layouts  1.23 us (1%)
    ppermute x8, starting transfers between devices, swaps(): lax.ppermute(far, axis, [(i, (i + (1 if i % 2 else -1)) % count) for i in...  36.3 us
    ppermute x8, waiting for transfers between devices, swaps(): lax.ppermute(far, axis, [(i, (i + (1 if i % 2 else -1)) % count) for i in...  25.3 us
    all_to_all x3, starting transfers between devices, per_device(): lax.all_to_all(blocks, ('wide', 'narrow'), 0, 0, axis_index_groups=groups)  22.5 us
    pallas_call x9, Pallas kernels, call(): pl.pallas_call(body, out_shape=[pltpu.HBM(shape, dtype) if i in out_hbm e...  16.1 us
    ppermute x8, starting transfers between devices, swaps(): near = lax.ppermute(near, axis, [(i, i ^ 1) for i in range(count)])  7.5 us
    ppermute x8, waiting for transfers between devices, swaps(): near = lax.ppermute(near, axis, [(i, i ^ 1) for i in range(count)])  6.6 us
  transfers between devices with their start and end apart: 19, of which 15 were waited for; matrix products, arithmetic and copies ran while one was open for 0% of the time, Pallas kernels for 0%

profile of v3, /device:TPU:1, one launch (start us, length us, event | category | flops | bytes accessed | tf_op | source)
XLA Modules:
  0.0 117.6 jit_solution(11512319432309261979)
XLA Ops:
  1.8 11.4 %collective-permute-start = (f32[216,128]{1,0:T(8,128)S(1)}, f32[216,128]{1,0:T(8,128)S(1)}, u32[]{:S(2)}, u32[]{:S(2)}) collective-permute-start(f32[216,128]{1,0:T(8,128)S(1)} %get-tuple-element.31), channel_id=1, source_target_pairs={{0,252},{4,8},{8,4},{12,16},{16,12},{20,24},{24,20},{28,32},{32,28... | collective-permute-start | bytes 331784 | tf_op jit(solution)/shard_map/wide_far/ppermute | solution.py:430
  13.2 2.8 %collective-permute-done.far = f32[216,128]{1,0:T(8,128)S(1)} collective-permute-done((f32[216,128]{1,0:T(8,128)S(1)}, f32[216,128]{1,0:T(8,128)S(1)}, u32[]{:S(2)}, u32[]{:S(2)}) %collective-permute-start) | collective-permute-done | bytes 110624 | tf_op jit(solution)/shard_map/wide_far/ppermute | solution.py:430
  15.9 2.3 %collective-permute-done.1.near = f32[216,128]{1,0:T(8,128)S(1)} collective-permute-done((f32[216,128]{1,0:T(8,128)S(1)}, f32[216,128]{1,0:T(8,128)S(1)}, u32[]{:S(2)}, u32[]{:S(2)}) %collective-permute-start.1) | collective-permute-done | bytes 110624 | tf_op jit(solution)/shard_map/wide_near/ppermute | solution.py:432
  18.4 2.4 %collective-permute-start.2 = (f32[324,128]{1,0:T(8,128)S(1)}, f32[324,128]{1,0:T(8,128)S(1)}, u32[]{:S(2)}, u32[]{:S(2)}) collective-permute-start(f32[324,128]{1,0:T(8,128)S(1)} %get-tuple-element.34), channel_id=1, source_target_pairs={{0,3},{1,2},{2,1},{3,0},{4,7},{5,6},{6,5},{7,4},{8,11},{9,10},{10,... | collective-permute-start | bytes 497672 | tf_op jit(solution)/shard_map/narrow_far/ppermute | solution.py:430
  20.8 4.3 %collective-permute-done.2.low = f32[324,128]{1,0:T(8,128)S(1)} collective-permute-done((f32[324,128]{1,0:T(8,128)S(1)}, f32[324,128]{1,0:T(8,128)S(1)}, u32[]{:S(2)}, u32[]{:S(2)}) %collective-permute-start.2) | collective-permute-done | bytes 165920 | tf_op jit(solution)/shard_map/narrow_far/ppermute | solution.py:430
  26.3 5.0 %first_sweep.1 = (f32[22,6,16,128]{3,2,1,0:T(8,128)S(1)}, s32[8,16,128]{2,1,0:T(8,128)S(1)}, f32[384,128]{1,0:T(8,128)}, f32[3,4,8,128]{3,2,1,0:T(8,128)S(1)}, f...) custom-call(f32[216,128]{1,0:T(8,128)S(1)} %collective-permute-done.far, f32[216,128]{1,0:T(8,128)S(1)} %collective-permute-done.1.near, ...), custom_call_target="tpu_custom_call" | custom-call | flops 1000000 | tf_op jit(solution)/shard_map/first_sweep/pallas_call | solution.py:412
  31.3 9.5 %all-to-all-start = ((f32[128,1,384]{2,1,0:T(1,128)}), f32[128,1,384]{2,1,0:T(1,128)S(1)}, u32[]{:S(2)}, u32[]{:S(2)}) async-start(f32[128,1,384]{2,1,0:T(1,128)} %bitcast.12), calls=%async_computation | async-start | bytes 393216 | tf_op jit(solution)/shard_map/all_to_all | solution.py:498
  40.8 7.1 %collective-permute-start.4 = (f32[48,128]{1,0:T(8,128)S(1)}, f32[48,128]{1,0:T(8,128)S(1)}, u32[]{:S(2)}, u32[]{:S(2)}) collective-permute-start(f32[48,128]{1,0:T(8,128)S(1)} %get-tuple-element.38), channel_id=1, source_target_pairs={{0,252},{4,8},{8,4},{12,16},{16,12},{20,24},{24,20},{28,32},{32,28... | collective-permute-start | bytes 73736 | tf_op jit(solution)/shard_map/wide_far/ppermute | solution.py:430
  47.9 2.9 %collective-permute-done.4.far = f32[48,128]{1,0:T(8,128)S(1)} collective-permute-done((f32[48,128]{1,0:T(8,128)S(1)}, f32[48,128]{1,0:T(8,128)S(1)}, u32[]{:S(2)}, u32[]{:S(2)}) %collective-permute-start.4) | collective-permute-done | bytes 24608 | tf_op jit(solution)/shard_map/wide_far/ppermute | solution.py:430
  50.8 1.6 %collective-permute-done.5.near = f32[48,128]{1,0:T(8,128)S(1)} collective-permute-done((f32[48,128]{1,0:T(8,128)S(1)}, f32[48,128]{1,0:T(8,128)S(1)}, u32[]{:S(2)}, u32[]{:S(2)}) %collective-permute-start.5) | collective-permute-done | bytes 24608 | tf_op jit(solution)/shard_map/wide_near/ppermute | solution.py:432
  52.7 2.9 %collective-permute-start.7 = (f32[80,128]{1,0:T(8,128)S(1)}, f32[80,128]{1,0:T(8,128)S(1)}, u32[]{:S(2)}, u32[]{:S(2)}) collective-permute-start(f32[80,128]{1,0:T(8,128)S(1)} %get-tuple-element.42), channel_id=1, source_target_pairs={{0,1},{1,0},{2,3},{3,2},{4,5},{5,4},{6,7},{7,6},{8,9},{9,8},{10,11... | collective-permute-start | bytes 122888 | tf_op jit(solution)/shard_map/narrow_near/ppermute | solution.py:432
  55.9 3.1 %collective-permute-done.6.low = f32[72,128]{1,0:T(8,128)S(1)} collective-permute-done((f32[72,128]{1,0:T(8,128)S(1)}, f32[72,128]{1,0:T(8,128)S(1)}, u32[]{:S(2)}, u32[]{:S(2)}) %collective-permute-start.6) | collective-permute-done | bytes 36896 | tf_op jit(solution)/shard_map/narrow_far/ppermute | solution.py:430
  59.0 4.5 %next_sweep.2 = (f32[384,128]{1,0:T(8,128)}, f32[3,4,8,128]{3,2,1,0:T(8,128)S(1)}, f32[48,128]{1,0:T(8,128)S(1)}, f32[48,128]{1,0:T(8,128)S(1)}) custom-call(f32[3,4,8,128]{3,2,1,0:T(8,128)S(1)} %get-tuple-element.37.current, f32[48,128]{1,0:T(8,128)S(1)} %collective-permute-done.4.far, f32[48,128]{1,0:T(8,128)S(1)} %collective-permute-done.5.near, ...), custom_call_target="tpu_custom_call" | custom-call | flops 1000000 | tf_op jit(solution)/shard_map/next_sweep/pallas_call | solution.py:412
  63.5 6.5 %all-to-all-start.1 = ((f32[128,1,384]{2,1,0:T(1,128)}), f32[128,1,384]{2,1,0:T(1,128)S(1)}, u32[]{:S(2)}, u32[]{:S(2)}) async-start(f32[128,1,384]{2,1,0:T(1,128)} %bitcast.14), calls=%async_computation.1 | async-start | bytes 393216 | tf_op jit(solution)/shard_map/all_to_all | solution.py:498
  70.0 7.1 %collective-permute-start.8 = (f32[48,128]{1,0:T(8,128)S(1)}, f32[48,128]{1,0:T(8,128)S(1)}, u32[]{:S(2)}, u32[]{:S(2)}) collective-permute-start(f32[48,128]{1,0:T(8,128)S(1)} %get-tuple-element.47), channel_id=1, source_target_pairs={{0,252},{4,8},{8,4},{12,16},{16,12},{20,24},{24,20},{28,32},{32,28... | collective-permute-start | bytes 73736 | tf_op jit(solution)/shard_map/wide_far/ppermute | solution.py:430
  77.1 3.2 %collective-permute-done.8.far = f32[48,128]{1,0:T(8,128)S(1)} collective-permute-done((f32[48,128]{1,0:T(8,128)S(1)}, f32[48,128]{1,0:T(8,128)S(1)}, u32[]{:S(2)}, u32[]{:S(2)}) %collective-permute-start.8) | collective-permute-done | bytes 24608 | tf_op jit(solution)/shard_map/wide_far/ppermute | solution.py:430
  82.2 2.3 %collective-permute-start.11 = (f32[80,128]{1,0:T(8,128)S(1)}, f32[80,128]{1,0:T(8,128)S(1)}, u32[]{:S(2)}, u32[]{:S(2)}) collective-permute-start(f32[80,128]{1,0:T(8,128)S(1)} %get-tuple-element.51), channel_id=1, source_target_pairs={{0,1},{1,0},{2,3},{3,2},{4,5},{5,4},{6,7},{7,6},{8,9},{9,8},{10,11... | collective-permute-start | bytes 122888 | tf_op jit(solution)/shard_map/narrow_near/ppermute | solution.py:432
  85.0 3.0 %collective-permute-done.10.low = f32[72,128]{1,0:T(8,128)S(1)} collective-permute-done((f32[72,128]{1,0:T(8,128)S(1)}, f32[72,128]{1,0:T(8,128)S(1)}, u32[]{:S(2)}, u32[]{:S(2)}) %collective-permute-start.10) | collective-permute-done | bytes 36896 | tf_op jit(solution)/shard_map/narrow_far/ppermute | solution.py:430
  87.9 4.5 %next_sweep.3 = (f32[384,128]{1,0:T(8,128)}, f32[3,4,8,128]{3,2,1,0:T(8,128)S(1)}, f32[48,128]{1,0:T(8,128)S(1)}, f32[48,128]{1,0:T(8,128)S(1)}) custom-call(f32[3,4,8,128]{3,2,1,0:T(8,128)S(1)} %get-tuple-element.46.current, f32[48,128]{1,0:T(8,128)S(1)} %collective-permute-done.8.far, f32[48,128]{1,0:T(8,128)S(1)} %collective-permute-done.9.near, ...), custom_call_target="tpu_custom_call" | custom-call | flops 1000000 | tf_op jit(solution)/shard_map/next_sweep/pallas_call | solution.py:412
  92.4 6.4 %all-to-all-start.2 = ((f32[128,1,384]{2,1,0:T(1,128)}), f32[128,1,384]{2,1,0:T(1,128)S(1)}, u32[]{:S(2)}, u32[]{:S(2)}) async-start(f32[128,1,384]{2,1,0:T(1,128)} %bitcast.13), calls=%async_computation.2 | async-start | bytes 393216 | tf_op jit(solution)/shard_map/all_to_all | solution.py:498
  98.9 7.1 %collective-permute-start.12 = (f32[48,128]{1,0:T(8,128)S(1)}, f32[48,128]{1,0:T(8,128)S(1)}, u32[]{:S(2)}, u32[]{:S(2)}) collective-permute-start(f32[48,128]{1,0:T(8,128)S(1)} %get-tuple-element.54), channel_id=1, source_target_pairs={{0,252},{4,8},{8,4},{12,16},{16,12},{20,24},{24,20},{28,32},{32,28... | collective-permute-start | bytes 73736 | tf_op jit(solution)/shard_map/wide_far/ppermute | solution.py:430
  106.0 3.2 %collective-permute-done.12.far = f32[48,128]{1,0:T(8,128)S(1)} collective-permute-done((f32[48,128]{1,0:T(8,128)S(1)}, f32[48,128]{1,0:T(8,128)S(1)}, u32[]{:S(2)}, u32[]{:S(2)}) %collective-permute-start.12) | collective-permute-done | bytes 24608 | tf_op jit(solution)/shard_map/wide_far/ppermute | solution.py:430
  111.1 2.3 %collective-permute-start.15 = (f32[80,128]{1,0:T(8,128)S(1)}, f32[80,128]{1,0:T(8,128)S(1)}, u32[]{:S(2)}, u32[]{:S(2)}) collective-permute-start(f32[80,128]{1,0:T(8,128)S(1)} %get-tuple-element.58), channel_id=1, source_target_pairs={{0,1},{1,0},{2,3},{3,2},{4,5},{5,4},{6,7},{7,6},{8,9},{9,8},{10,11... | collective-permute-start | bytes 122888 | tf_op jit(solution)/shard_map/narrow_near/ppermute | solution.py:432
  113.8 3.0 %collective-permute-done.14.low = f32[72,128]{1,0:T(8,128)S(1)} collective-permute-done((f32[72,128]{1,0:T(8,128)S(1)}, f32[72,128]{1,0:T(8,128)S(1)}, u32[]{:S(2)}, u32[]{:S(2)}) %collective-permute-start.14) | collective-permute-done | bytes 36896 | tf_op jit(solution)/shard_map/narrow_far/ppermute | solution.py:430
  (27 shorter events, 8.6 us)
Async XLA Ops:
  1.8 14.2 %collective-permute-start = (f32[216,128]{1,0:T(8,128)S(1)}, f32[216,128]{1,0:T(8,128)S(1)}, u32[]{:S(2)}, u32[]{:S(2)}) collective-permute-start(f32[216,128]{1,0:T(8,128)S(1)} %get-tuple-element.31), channel_id=1, source_target_pairs={{0,252},{4,8},{8,4},{12,16},{16,12},{20,24},{24,20},{28,32},{32,28... | collective-permute-start | bytes 331784 | tf_op jit(solution)/shard_map/wide_far/ppermute | solution.py:430
  13.2 5.1 %collective-permute-start.1 = (f32[216,128]{1,0:T(8,128)S(1)}, f32[216,128]{1,0:T(8,128)S(1)}, u32[]{:S(2)}, u32[]{:S(2)}) collective-permute-start(f32[216,128]{1,0:T(8,128)S(1)} %get-tuple-element.32), channel_id=1, source_target_pairs={{0,4},{4,0},{8,12},{12,8},{16,20},{20,16},{24,28},{28,24},{32,36},... | collective-permute-start | bytes 331784 | tf_op jit(solution)/shard_map/wide_near/ppermute | solution.py:432
  18.4 6.7 %collective-permute-start.2 = (f32[324,128]{1,0:T(8,128)S(1)}, f32[324,128]{1,0:T(8,128)S(1)}, u32[]{:S(2)}, u32[]{:S(2)}) collective-permute-start(f32[324,128]{1,0:T(8,128)S(1)} %get-tuple-element.34), channel_id=1, source_target_pairs={{0,3},{1,2},{2,1},{3,0},{4,7},{5,6},{6,5},{7,4},{8,11},{9,10},{10,... | collective-permute-start | bytes 497672 | tf_op jit(solution)/shard_map/narrow_far/ppermute | solution.py:430
  20.7 4.3 %collective-permute-start.3 = (f32[324,128]{1,0:T(8,128)S(1)}, f32[324,128]{1,0:T(8,128)S(1)}, u32[]{:S(2)}, u32[]{:S(2)}) collective-permute-start(f32[324,128]{1,0:T(8,128)S(1)} %get-tuple-element.35), channel_id=1, source_target_pairs={{0,1},{1,0},{2,3},{3,2},{4,5},{5,4},{6,7},{7,6},{8,9},{9,8},{10,11... | collective-permute-start | bytes 497672 | tf_op jit(solution)/shard_map/narrow_near/ppermute | solution.py:432
  25.0 1.2 %copy-start = (f32[32,8192]{1,0:T(8,128)S(1)}, f32[32,8192]{1,0:T(8,128)}, u32[]{:S(2)}) copy-start(f32[32,8192]{1,0:T(8,128)} %coarse.5) | copy-start | bytes 3145732
  26.3 32.7 %copy-start.1 = (f32[32,8192]{1,0:T(8,128)S(1)}, f32[32,8192]{1,0:T(8,128)}, u32[]{:S(2)}) copy-start(f32[32,8192]{1,0:T(8,128)} %coarse.5) | copy-start | bytes 3145732
  31.3 21.4 %all-to-all-start = ((f32[128,1,384]{2,1,0:T(1,128)}), f32[128,1,384]{2,1,0:T(1,128)S(1)}, u32[]{:S(2)}, u32[]{:S(2)}) async-start(f32[128,1,384]{2,1,0:T(1,128)} %bitcast.12), calls=%async_computation | async-start | bytes 393216 | tf_op jit(solution)/shard_map/all_to_all | solution.py:498
  40.8 10.0 %collective-permute-start.4 = (f32[48,128]{1,0:T(8,128)S(1)}, f32[48,128]{1,0:T(8,128)S(1)}, u32[]{:S(2)}, u32[]{:S(2)}) collective-permute-start(f32[48,128]{1,0:T(8,128)S(1)} %get-tuple-element.38), channel_id=1, source_target_pairs={{0,252},{4,8},{8,4},{12,16},{16,12},{20,24},{24,20},{28,32},{32,28... | collective-permute-start | bytes 73736 | tf_op jit(solution)/shard_map/wide_far/ppermute | solution.py:430
  47.9 4.5 %collective-permute-start.5 = (f32[48,128]{1,0:T(8,128)S(1)}, f32[48,128]{1,0:T(8,128)S(1)}, u32[]{:S(2)}, u32[]{:S(2)}) collective-permute-start(f32[48,128]{1,0:T(8,128)S(1)} %get-tuple-element.39), channel_id=1, source_target_pairs={{0,4},{4,0},{8,12},{12,8},{16,20},{20,16},{24,28},{28,24},{32,36},... | collective-permute-start | bytes 73736 | tf_op jit(solution)/shard_map/wide_near/ppermute | solution.py:432
  52.7 6.2 %collective-permute-start.7 = (f32[80,128]{1,0:T(8,128)S(1)}, f32[80,128]{1,0:T(8,128)S(1)}, u32[]{:S(2)}, u32[]{:S(2)}) collective-permute-start(f32[80,128]{1,0:T(8,128)S(1)} %get-tuple-element.42), channel_id=1, source_target_pairs={{0,1},{1,0},{2,3},{3,2},{4,5},{5,4},{6,7},{7,6},{8,9},{9,8},{10,11... | collective-permute-start | bytes 122888 | tf_op jit(solution)/shard_map/narrow_near/ppermute | solution.py:432
  55.6 3.4 %collective-permute-start.6 = (f32[72,128]{1,0:T(8,128)S(1)}, f32[72,128]{1,0:T(8,128)S(1)}, u32[]{:S(2)}, u32[]{:S(2)}) collective-permute-start(f32[72,128]{1,0:T(8,128)S(1)} %get-tuple-element.41), channel_id=1, source_target_pairs={{0,3},{1,2},{2,1},{3,0},{4,7},{5,6},{6,5},{7,4},{8,11},{9,10},{10,... | collective-permute-start | bytes 110600 | tf_op jit(solution)/shard_map/narrow_far/ppermute | solution.py:430
  63.5 18.7 %all-to-all-start.1 = ((f32[128,1,384]{2,1,0:T(1,128)}), f32[128,1,384]{2,1,0:T(1,128)S(1)}, u32[]{:S(2)}, u32[]{:S(2)}) async-start(f32[128,1,384]{2,1,0:T(1,128)} %bitcast.14), calls=%async_computation.1 | async-start | bytes 393216 | tf_op jit(solution)/shard_map/all_to_all | solution.py:498
  70.0 10.3 %collective-permute-start.8 = (f32[48,128]{1,0:T(8,128)S(1)}, f32[48,128]{1,0:T(8,128)S(1)}, u32[]{:S(2)}, u32[]{:S(2)}) collective-permute-start(f32[48,128]{1,0:T(8,128)S(1)} %get-tuple-element.47), channel_id=1, source_target_pairs={{0,252},{4,8},{8,4},{12,16},{16,12},{20,24},{24,20},{28,32},{32,28... | collective-permute-start | bytes 73736 | tf_op jit(solution)/shard_map/wide_far/ppermute | solution.py:430
  77.1 4.5 %collective-permute-start.9 = (f32[48,128]{1,0:T(8,128)S(1)}, f32[48,128]{1,0:T(8,128)S(1)}, u32[]{:S(2)}, u32[]{:S(2)}) collective-permute-start(f32[48,128]{1,0:T(8,128)S(1)} %get-tuple-element.48), channel_id=1, source_target_pairs={{0,4},{4,0},{8,12},{12,8},{16,20},{20,16},{24,28},{28,24},{32,36},... | collective-permute-start | bytes 73736 | tf_op jit(solution)/shard_map/wide_near/ppermute | solution.py:432
  82.2 5.7 %collective-permute-start.11 = (f32[80,128]{1,0:T(8,128)S(1)}, f32[80,128]{1,0:T(8,128)S(1)}, u32[]{:S(2)}, u32[]{:S(2)}) collective-permute-start(f32[80,128]{1,0:T(8,128)S(1)} %get-tuple-element.51), channel_id=1, source_target_pairs={{0,1},{1,0},{2,3},{3,2},{4,5},{5,4},{6,7},{7,6},{8,9},{9,8},{10,11... | collective-permute-start | bytes 122888 | tf_op jit(solution)/shard_map/narrow_near/ppermute | solution.py:432
  84.5 3.4 %collective-permute-start.10 = (f32[72,128]{1,0:T(8,128)S(1)}, f32[72,128]{1,0:T(8,128)S(1)}, u32[]{:S(2)}, u32[]{:S(2)}) collective-permute-start(f32[72,128]{1,0:T(8,128)S(1)} %get-tuple-element.50), channel_id=1, source_target_pairs={{0,3},{1,2},{2,1},{3,0},{4,7},{5,6},{6,5},{7,4},{8,11},{9,10},{10,... | collective-permute-start | bytes 110600 | tf_op jit(solution)/shard_map/narrow_far/ppermute | solution.py:430
  92.4 18.6 %all-to-all-start.2 = ((f32[128,1,384]{2,1,0:T(1,128)}), f32[128,1,384]{2,1,0:T(1,128)S(1)}, u32[]{:S(2)}, u32[]{:S(2)}) async-start(f32[128,1,384]{2,1,0:T(1,128)} %bitcast.13), calls=%async_computation.2 | async-start | bytes 393216 | tf_op jit(solution)/shard_map/all_to_all | solution.py:498
  98.9 10.3 %collective-permute-start.12 = (f32[48,128]{1,0:T(8,128)S(1)}, f32[48,128]{1,0:T(8,128)S(1)}, u32[]{:S(2)}, u32[]{:S(2)}) collective-permute-start(f32[48,128]{1,0:T(8,128)S(1)} %get-tuple-element.54), channel_id=1, source_target_pairs={{0,252},{4,8},{8,4},{12,16},{16,12},{20,24},{24,20},{28,32},{32,28... | collective-permute-start | bytes 73736 | tf_op jit(solution)/shard_map/wide_far/ppermute | solution.py:430
  106.0 4.5 %collective-permute-start.13 = (f32[48,128]{1,0:T(8,128)S(1)}, f32[48,128]{1,0:T(8,128)S(1)}, u32[]{:S(2)}, u32[]{:S(2)}) collective-permute-start(f32[48,128]{1,0:T(8,128)S(1)} %get-tuple-element.55), channel_id=1, source_target_pairs={{0,4},{4,0},{8,12},{12,8},{16,20},{20,16},{24,28},{28,24},{32,36},... | collective-permute-start | bytes 73736 | tf_op jit(solution)/shard_map/wide_near/ppermute | solution.py:432
  111.1 5.7 %collective-permute-start.15 = (f32[80,128]{1,0:T(8,128)S(1)}, f32[80,128]{1,0:T(8,128)S(1)}, u32[]{:S(2)}, u32[]{:S(2)}) collective-permute-start(f32[80,128]{1,0:T(8,128)S(1)} %get-tuple-element.58), channel_id=1, source_target_pairs={{0,1},{1,0},{2,3},{3,2},{4,5},{5,4},{6,7},{7,6},{8,9},{9,8},{10,11... | collective-permute-start | bytes 122888 | tf_op jit(solution)/shard_map/narrow_near/ppermute | solution.py:432
  113.4 3.4 %collective-permute-start.14 = (f32[72,128]{1,0:T(8,128)S(1)}, f32[72,128]{1,0:T(8,128)S(1)}, u32[]{:S(2)}, u32[]{:S(2)}) collective-permute-start(f32[72,128]{1,0:T(8,128)S(1)} %get-tuple-element.57), channel_id=1, source_target_pairs={{0,3},{1,2},{2,1},{3,0},{4,7},{5,6},{6,5},{7,4},{8,11},{9,10},{10,... | collective-permute-start | bytes 110600 | tf_op jit(solution)/shard_map/narrow_far/ppermute | solution.py:430

commit v4 on v3

--- a/solution.py
+++ b/solution.py
@@ -180,7 +180,7 @@
             high[at : at + 3] = pick(narrow_odd, v[0:3], v[5:8])
 
 
-def coarse_part(misfit0, agg, coarse, sums, spread, staged):
+def coarse_part(misfit0, agg, coarse, sums, spread, staged, payload, sems):
     for g in range(AGG_LOC):
         picked = jnp.where(agg[0] == float(g), misfit0[0], 0.0)
         for p in range(1, 4):
@@ -193,15 +193,22 @@
         spread[w + 1 : w + 2, :] = row
     spread[0:1, :] = spread[count : count + 1, :]
     spread[count + 1 : count + 2, :] = spread[1:2, :]
+    pieces = [slice(0, 3 * count), slice(3 * count, 6 * count)]
+    writes = [pltpu.make_async_copy(staged.at[piece], payload.at[piece], sems.at[i]) for i, piece in enumerate(pieces)]
     for w in range(count):
         rows = spread[w : w + 3, :]
         for half in range(2):
             at = 3 * (2 * w + half)
             staged[at : at + 3, :] = rows
-
-
-def solve_box(values, coef, agg, coarse, factors_hbm, payload, current, far, near, scratch):
-    misfit, sums, spread, staged, one, two, factors, tile_sems, sem = scratch
+        if w == count // 2 - 1:
+            writes[0].start()
+    writes[1].start()
+    for write in writes:
+        write.wait()
+
+
+def misfit_part(values, coef, agg, coarse, misfit, payload, scratch, fetch=None):
+    sums, spread, staged, write_sems = scratch
     inside = box_mask()
     rolled = {}
     for c in range(3):
@@ -211,17 +218,9 @@
         applied = operate_pair(values, coef, a, rolled)
         for c in range(3):
             misfit[c, a] = jnp.where(inside, coef[RHS + c, a - 1] - applied[c], 0.0)
-    coarse_part([misfit[0, a, 0:8] for a in range(2, 6)], agg, coarse, sums, spread, staged)
-    write = pltpu.make_async_copy(staged, payload, sem)
-    write.start()
-    local_solve(misfit, coef, values, factors_hbm, factors, tile_sems, current, one, two)
-    odd = is_odd("wide")
-    for c in range(3):
-        for p in range(2):
-            at = c * 16 + p * 8
-            far[at : at + 8] = pick(odd, current[c, 2 + p], current[c, p])
-            near[at : at + 8] = pick(odd, current[c, p], current[c, 2 + p])
-    write.wait()
+    if fetch is not None:
+        fetch.wait()
+    coarse_part([misfit[0, a, 0:8] for a in range(2, 6)], agg, coarse, sums, spread, staged, payload, write_sems)
 
 
 def fetch_tiles(factors_hbm, factors, sems):
@@ -229,27 +228,27 @@
     return [pltpu.make_async_copy(factors_hbm.at[a, cols[a]], factors.at[a, cols[a]], sems.at[a]) for a in range(6)]
 
 
-def first_sweep(
+def first_misfit(
     far,
     near,
     low,
     high,
     mine,
     agg,
-    coarse,
-    factors_hbm,
+    coarse_hbm,
     coef,
     slots,
+    moved,
+    misfit,
     payload,
-    current,
-    far_out,
-    near_out,
     rim,
+    coarse,
+    sem,
     values,
     *scratch,
 ):
-    for fetch in fetch_tiles(factors_hbm, scratch[-3], scratch[-2]):
-        fetch.start()
+    fetch = pltpu.make_async_copy(coarse_hbm, coarse, sem)
+    fetch.start()
     odd = is_odd("wide")
     narrow_odd = is_odd("narrow")
     blank = jnp.zeros((ROWS, LANES), f32)
@@ -297,7 +296,10 @@
         for c in range(3):
             diagonal = jnp.where(inside, centre + coef[COUP + 4 * c, a - 1], 1.0)
             coef[INV + c, a - 1] = jnp.where(inside, 1.0 / diagonal, 0.0)
-    solve_box(values, coef, agg, coarse, factors_hbm, payload, current, far_out, near_out, scratch)
+    for c in range(3):
+        for p in range(4):
+            moved[c, p] = mine[3 + c, p]
+    misfit_part(values, coef, agg, coarse, misfit, payload, scratch, fetch)
 
 
 def gather_values(current, far, near, low, high, part, slots, values):
@@ -321,29 +323,14 @@
             values[0, a, 8 * half : 8 * half + 8] += lifted
 
 
-def next_sweep(
-    current,
-    far,
-    near,
-    low,
-    high,
-    part,
-    slots,
-    coef,
-    agg,
-    coarse,
-    factors_hbm,
-    payload,
-    moved,
-    far_out,
-    near_out,
-    values,
-    *scratch,
+def next_misfit(
+    current, far, near, low, high, part, slots, coef, agg, coarse, moved, misfit, payload, values, *scratch
 ):
-    for fetch in fetch_tiles(factors_hbm, scratch[-3], scratch[-2]):
-        fetch.start()
     gather_values(current, far, near, low, high, part, slots, values)
-    solve_box(values, coef, agg, coarse, factors_hbm, payload, moved, far_out, near_out, scratch)
+    for c in range(3):
+        for p in range(4):
+            moved[c, p] = values[c, p + 2, 0:8]
+    misfit_part(values, coef, agg, coarse, misfit, payload, scratch)
 
 
 def last_misfit(current, far, near, low, high, part, slots, coef, iterate, residual, values):
@@ -356,8 +343,10 @@
             residual[c, a - 2] = (coef[RHS + c, a - 1] - applied[c])[0:8]
 
 
-def local_solve(misfit, coef, values, factors_hbm, factors, sems, moved, one, two):
+def local_solve(misfit, coef, current, factors_hbm, moved, far, near, one, two, factors, sems):
     fetches = fetch_tiles(factors_hbm, factors, sems)
+    for fetch in fetches:
+        fetch.start()
     own_cols = list(range(8))
     row8 = lax.broadcasted_iota(jnp.int32, (24, LANES), 0) % 8
 
@@ -377,19 +366,19 @@
         for ref in (one, two):
             ref[c, 0] = blank
             ref[c, 7] = blank
-    for a in range(1, 7):
-        edge = a in (1, 6)
+    rolled_one, rolled_two = {}, {}
+
+    def first(a):
         fetches[a - 1].wait()
-        for half, cols in ((0, own_cols), (1, [8, -1] if edge else [8, 9, -2, -1])):
+        for half, cols in ((0, own_cols), (1, [8, -1] if a in (1, 6) else [8, 9, -2, -1])):
             part = tiles([misfit[c, a, 8 * half : 8 * half + 8] for c in range(3)], a, cols, half)
             for c in range(3):
                 one[c, a, 8 * half : 8 * half + 8] = part[c]
-    rolled = {}
-    for a in range(1, 7):
-        edge = a in (1, 6)
-        applied = operate_pair(one, coef, a, rolled)
+
+    def second(a):
+        applied = operate_pair(one, coef, a, rolled_one)
         left = [misfit[c, a] - applied[c] for c in range(3)]
-        for half, cols in ((0, own_cols), (1, [] if edge else [8, -1])):
+        for half, cols in ((0, own_cols), (1, [] if a in (1, 6) else [8, -1])):
             if not cols:
                 for c in range(3):
                     two[c, a, 8:16] = one[c, a, 8:16]
@@ -397,12 +386,26 @@
             part = tiles([v[8 * half : 8 * half + 8] for v in left], a, cols, half)
             for c in range(3):
                 two[c, a, 8 * half : 8 * half + 8] = one[c, a, 8 * half : 8 * half + 8] + part[c]
-    rolled = {}
-    for a in range(2, 6):
-        applied = operate_pair(two, coef, a, rolled)
+
+    def third(a):
+        applied = operate_pair(two, coef, a, rolled_two)
         part = tiles([(misfit[c, a] - applied[c])[0:8] for c in range(3)], a, own_cols, 0)
         for c in range(3):
-            moved[c, a - 2] = values[c, a, 0:8] + (two[c, a, 0:8] + part[c])
+            moved[c, a - 2] = current[c, a - 2] + (two[c, a, 0:8] + part[c])
+
+    for a in range(1, 8):
+        if a <= 6:
+            first(a)
+        if a >= 2:
+            second(a - 1)
+        if a >= 4:
+            third(a - 2)
+    odd = is_odd("wide")
+    for c in range(3):
+        for p in range(2):
+            at = c * 16 + p * 8
+            far[at : at + 8] = pick(odd, moved[c, 2 + p], moved[c, p])
+            near[at : at + 8] = pick(odd, moved[c, p], moved[c, 2 + p])
 
 
 def call(body, name, outs, scratch, operands, in_hbm=(), out_hbm=(), flops=1000000):
@@ -447,15 +450,16 @@
     payload_type = ((members * 3, LANES), f32)
     scratch = [
         pltpu.VMEM(box, f32),
-        pltpu.VMEM(box, f32),
         pltpu.VMEM((AGG_LOC, LANES), f32),
         pltpu.VMEM((devices // 4 + 8, LANES), f32),
         pltpu.VMEM(payload_type[0], f32),
+        dma((2,)),
+    ]
+    solve_scratch = [
         pltpu.VMEM(box, f32),
         pltpu.VMEM(box, f32),
         pltpu.VMEM(tile_factors.shape, tile_factors.dtype),
         dma((6,)),
-        dma,
     ]
 
     mine, agg, far, near = call(
@@ -484,18 +488,33 @@
     far, near = swaps("wide", far, near)
     low, high = call(pack_narrow, "pack_narrow", [((NARROW_ROWS, LANES), f32)] * 2, [], [far, near, mine])
     low, high = swaps("narrow", low, high)
-    coef, slots, payload, current, far, near = call(
-        first_sweep,
-        "first_sweep",
-        [((N_COEF, 6, ROWS, LANES), f32), ((PAIRS, ROWS, LANES), jnp.int32), payload_type, own, wide_type, wide_type],
-        [pltpu.VMEM((4, PAIRS, ROWS, LANES), f32)] + scratch,
-        [far, near, low, high, mine, agg, coarse_inverse, tile_factors],
-        in_hbm=(7,),
-        out_hbm=(2,),
+    coef, slots, current, misfit, payload = call(
+        first_misfit,
+        "first_misfit",
+        [
+            ((N_COEF, 6, ROWS, LANES), f32),
+            ((PAIRS, ROWS, LANES), jnp.int32),
+            own,
+            (box, f32),
+            payload_type,
+        ],
+        [pltpu.VMEM((4, PAIRS, ROWS, LANES), f32), pltpu.VMEM(coarse_inverse.shape, f32), dma] + scratch,
+        [far, near, low, high, mine, agg, coarse_inverse],
+        in_hbm=(6,),
+        out_hbm=(4,),
     )
     for sweep in range(SWEEPS):
         blocks = payload.reshape(members, 1, 3 * LANES)
         received = lax.all_to_all(blocks, ("wide", "narrow"), 0, 0, axis_index_groups=groups).reshape(payload_type[0])
+        current, far, near = call(
+            local_solve,
+            "local_solve",
+            [own, wide_type, wide_type],
+            solve_scratch,
+            [misfit, coef, current, tile_factors],
+            in_hbm=(3,),
+            flops=30000000,
+        )
         far, near = swaps("wide", far, near)
         low, high, part = call(
             pack_current,
@@ -507,14 +526,13 @@
         low, high = swaps("narrow", low, high)
         known = [current, far, near, low, high, part, slots, coef]
         if sweep < SWEEPS - 1:
-            payload, current, far, near = call(
-                next_sweep,
-                "next_sweep",
-                [payload_type, own, wide_type, wide_type],
+            current, misfit, payload = call(
+                next_misfit,
+                "next_misfit",
+                [own, (box, f32), payload_type],
                 scratch,
-                known + [agg, coarse_inverse, tile_factors],
-                in_hbm=(10,),
-                out_hbm=(0,),
+                known + [agg, coarse_inverse],
+                out_hbm=(2,),
             )
         else:
             iterate, residual = call(last_misfit, "last_misfit", [own, own], [pltpu.VMEM(box, f32)], known)

time: 118 us -> 123 us (1.042)
  Pallas kernels: 16.1 us -> 23.2 us
  waiting for transfers between devices: 33.3 us -> 31.3 us
    pallas_call x9 -> x12, Pallas kernels: 16.1 us -> 23.2 us  [call(): pl.pallas_call(body, out_shape=[pltpu.HBM(shape, dtype) if i in out_hbm e...]
    ppermute x8, waiting for transfers between devices: 25.3 us -> 20.8 us  [swaps(): lax.ppermute(far, axis, [(i, (i + (1 if i % 2 else -1)) % count) for i in...]
    ppermute x8, waiting for transfers between devices: 6.6 us -> 10.5 us  [swaps(): near = lax.ppermute(near, axis, [(i, i ^ 1) for i in range(count)])]
    all_to_all x3, starting transfers between devices: 22.5 us -> 24.7 us  [per_device(): lax.all_to_all(blocks, ('wide', 'narrow'), 0, 0, axis_index_groups=groups)]
    all_to_all x3, waiting for transfers between devices: 1.4 us -> 0.01 us  [per_device(): lax.all_to_all(blocks, ('wide', 'narrow'), 0, 0, axis_index_groups=groups)]
  transfers between devices with their start and end apart: 19 -> 19, of which waited for: 15 -> 12; matrix products, arithmetic and copies ran while one was open for 0% -> 0% of each run, Pallas kernels for 0% -> 13%
where the time goes in v4:
time: 123 us
  starting transfers between devices  67.4 us (55%)
  waiting for transfers between devices  31.3 us (25%)
  Pallas kernels  23.2 us (19%)
    ppermute x8, starting transfers between devices, swaps(): lax.ppermute(far, axis, [(i, (i + (1 if i % 2 else -1)) % count) for i in...  35.8 us
    all_to_all x3, starting transfers between devices, per_device(): lax.all_to_all(blocks, ('wide', 'narrow'), 0, 0, axis_index_groups=groups)  24.7 us
    pallas_call x12, Pallas kernels, call(): pl.pallas_call(body, out_shape=[pltpu.HBM(shape, dtype) if i in out_hbm e...  23.2 us
    ppermute x8, waiting for transfers between devices, swaps(): lax.ppermute(far, axis, [(i, (i + (1 if i % 2 else -1)) % count) for i in...  20.8 us
    ppermute x8, waiting for transfers between devices, swaps(): near = lax.ppermute(near, axis, [(i, i ^ 1) for i in range(count)])  10.5 us
    ppermute x8, starting transfers between devices, swaps(): near = lax.ppermute(near, axis, [(i, i ^ 1) for i in range(count)])  6.86 us
  transfers between devices with their start and end apart: 19, of which 12 were waited for; matrix products, arithmetic and copies ran while one was open for 0% of the time, Pallas kernels for 13%

profile of v4, /device:TPU:1, one launch (start us, length us, event | category | flops | bytes accessed | tf_op | source)
XLA Modules:
  0.0 122.7 jit_solution(17964614169231343873)
XLA Ops:
  1.8 11.4 %collective-permute-start = (f32[216,128]{1,0:T(8,128)S(1)}, f32[216,128]{1,0:T(8,128)S(1)}, u32[]{:S(2)}, u32[]{:S(2)}) collective-permute-start(f32[216,128]{1,0:T(8,128)S(1)} %get-tuple-element.37), channel_id=1, source_target_pairs={{0,252},{4,8},{8,4},{12,16},{16,12},{20,24},{24,20},{28,32},{32,28... | collective-permute-start | bytes 331784 | tf_op jit(solution)/shard_map/wide_far/ppermute | solution.py:433
  13.2 2.8 %collective-permute-done.far = f32[216,128]{1,0:T(8,128)S(1)} collective-permute-done((f32[216,128]{1,0:T(8,128)S(1)}, f32[216,128]{1,0:T(8,128)S(1)}, u32[]{:S(2)}, u32[]{:S(2)}) %collective-permute-start) | collective-permute-done | bytes 110624 | tf_op jit(solution)/shard_map/wide_far/ppermute | solution.py:433
  15.9 2.3 %collective-permute-done.1.near = f32[216,128]{1,0:T(8,128)S(1)} collective-permute-done((f32[216,128]{1,0:T(8,128)S(1)}, f32[216,128]{1,0:T(8,128)S(1)}, u32[]{:S(2)}, u32[]{:S(2)}) %collective-permute-start.1) | collective-permute-done | bytes 110624 | tf_op jit(solution)/shard_map/wide_near/ppermute | solution.py:435
  18.4 2.4 %collective-permute-start.2 = (f32[324,128]{1,0:T(8,128)S(1)}, f32[324,128]{1,0:T(8,128)S(1)}, u32[]{:S(2)}, u32[]{:S(2)}) collective-permute-start(f32[324,128]{1,0:T(8,128)S(1)} %get-tuple-element.40), channel_id=1, source_target_pairs={{0,3},{1,2},{2,1},{3,0},{4,7},{5,6},{6,5},{7,4},{8,11},{9,10},{10,... | collective-permute-start | bytes 497672 | tf_op jit(solution)/shard_map/narrow_far/ppermute | solution.py:433
  20.8 4.3 %collective-permute-done.2.low = f32[324,128]{1,0:T(8,128)S(1)} collective-permute-done((f32[324,128]{1,0:T(8,128)S(1)}, f32[324,128]{1,0:T(8,128)S(1)}, u32[]{:S(2)}, u32[]{:S(2)}) %collective-permute-start.2) | collective-permute-done | bytes 165920 | tf_op jit(solution)/shard_map/narrow_far/ppermute | solution.py:433
  25.0 2.5 %first_misfit.1 = (f32[22,6,16,128]{3,2,1,0:T(8,128)S(1)}, s32[8,16,128]{2,1,0:T(8,128)S(1)}, f32[3,4,8,128]{3,2,1,0:T(8,128)S(1)}, f32[3,8,16,128]{3,2,1,0:T(8,128)S(1)}, f32[384,128]{1,0:T(8,128)}) custom-call(f32[216,128]{1,0:T(8,128)S(1)} %collective-permute-done.far, f32[216,128]{1,0:T(8,128)S(1)} %collective-permute-done.1.near, ...), custom_call_target="tpu_custom_call" | custom-call | flops 1000000 | tf_op jit(solution)/shard_map/first_misfit/pallas_call | solution.py:415
  27.5 9.6 %all-to-all-start = ((f32[128,1,384]{2,1,0:T(1,128)}), f32[128,1,384]{2,1,0:T(1,128)S(1)}, u32[]{:S(2)}, u32[]{:S(2)}) async-start(f32[128,1,384]{2,1,0:T(1,128)} %bitcast.12), calls=%async_computation | async-start | bytes 393216 | tf_op jit(solution)/shard_map/all_to_all | solution.py:508
  37.2 5.5 %local_solve.3 = (f32[3,4,8,128]{3,2,1,0:T(8,128)S(1)}, f32[48,128]{1,0:T(8,128)S(1)}, f32[48,128]{1,0:T(8,128)S(1)}) custom-call(f32[3,8,16,128]{3,2,1,0:T(8,128)S(1)} %get-tuple-element.43.misfit, f32[22,6,16,128]{3,2,1,0:T(8,128)S(1)} %get-tuple-element.44.coef, f32[3,4,8,128]{3,2,1,0:T(8,128)S(1)} %get-tuple-element.45.current, ...), custom_call_target="tpu_custom_call" | custom-call | flops 30000000 | tf_op jit(solution)/shard_map/local_solve/pallas_call | solution.py:415
  42.6 7.1 %collective-permute-start.4 = (f32[48,128]{1,0:T(8,128)S(1)}, f32[48,128]{1,0:T(8,128)S(1)}, u32[]{:S(2)}, u32[]{:S(2)}) collective-permute-start(f32[48,128]{1,0:T(8,128)S(1)} %get-tuple-element.47), channel_id=1, source_target_pairs={{0,252},{4,8},{8,4},{12,16},{16,12},{20,24},{24,20},{28,32},{32,28... | collective-permute-start | bytes 73736 | tf_op jit(solution)/shard_map/wide_far/ppermute | solution.py:433
  51.2 2.8 %collective-permute-done.5.near = f32[48,128]{1,0:T(8,128)S(1)} collective-permute-done((f32[48,128]{1,0:T(8,128)S(1)}, f32[48,128]{1,0:T(8,128)S(1)}, u32[]{:S(2)}, u32[]{:S(2)}) %collective-permute-start.5) | collective-permute-done | bytes 24608 | tf_op jit(solution)/shard_map/wide_near/ppermute | solution.py:435
  54.0 2.5 %collective-permute-start.7 = (f32[80,128]{1,0:T(8,128)S(1)}, f32[80,128]{1,0:T(8,128)S(1)}, u32[]{:S(2)}, u32[]{:S(2)}) collective-permute-start(f32[80,128]{1,0:T(8,128)S(1)} %get-tuple-element.51), channel_id=1, source_target_pairs={{0,1},{1,0},{2,3},{3,2},{4,5},{5,4},{6,7},{7,6},{8,9},{9,8},{10,11... | collective-permute-start | bytes 122888 | tf_op jit(solution)/shard_map/narrow_near/ppermute | solution.py:435
  56.8 3.1 %collective-permute-done.6.low = f32[72,128]{1,0:T(8,128)S(1)} collective-permute-done((f32[72,128]{1,0:T(8,128)S(1)}, f32[72,128]{1,0:T(8,128)S(1)}, u32[]{:S(2)}, u32[]{:S(2)}) %collective-permute-start.6) | collective-permute-done | bytes 36896 | tf_op jit(solution)/shard_map/narrow_far/ppermute | solution.py:433
  61.0 7.6 %all-to-all-start.1 = ((f32[128,1,384]{2,1,0:T(1,128)}), f32[128,1,384]{2,1,0:T(1,128)S(1)}, u32[]{:S(2)}, u32[]{:S(2)}) async-start(f32[128,1,384]{2,1,0:T(1,128)} %bitcast.14), calls=%async_computation.1 | async-start | bytes 393216 | tf_op jit(solution)/shard_map/all_to_all | solution.py:508
  68.7 5.5 %local_solve.4 = (f32[3,4,8,128]{3,2,1,0:T(8,128)S(1)}, f32[48,128]{1,0:T(8,128)S(1)}, f32[48,128]{1,0:T(8,128)S(1)}) custom-call(f32[3,8,16,128]{3,2,1,0:T(8,128)S(1)} %get-tuple-element.54.misfit, f32[22,6,16,128]{3,2,1,0:T(8,128)S(1)} %get-tuple-element.44.coef, f32[3,4,8,128]{3,2,1,0:T(8,128)S(1)} %get-tuple-element.55.current, ...), custom_call_target="tpu_custom_call" | custom-call | flops 30000000 | tf_op jit(solution)/shard_map/local_solve/pallas_call | solution.py:415
  74.1 7.0 %collective-permute-start.8 = (f32[48,128]{1,0:T(8,128)S(1)}, f32[48,128]{1,0:T(8,128)S(1)}, u32[]{:S(2)}, u32[]{:S(2)}) collective-permute-start(f32[48,128]{1,0:T(8,128)S(1)} %get-tuple-element.57), channel_id=1, source_target_pairs={{0,252},{4,8},{8,4},{12,16},{16,12},{20,24},{24,20},{28,32},{32,28... | collective-permute-start | bytes 73736 | tf_op jit(solution)/shard_map/wide_far/ppermute | solution.py:433
  82.7 2.6 %collective-permute-done.9.near = f32[48,128]{1,0:T(8,128)S(1)} collective-permute-done((f32[48,128]{1,0:T(8,128)S(1)}, f32[48,128]{1,0:T(8,128)S(1)}, u32[]{:S(2)}, u32[]{:S(2)}) %collective-permute-start.9) | collective-permute-done | bytes 24608 | tf_op jit(solution)/shard_map/wide_near/ppermute | solution.py:435
  85.3 2.2 %collective-permute-start.11 = (f32[80,128]{1,0:T(8,128)S(1)}, f32[80,128]{1,0:T(8,128)S(1)}, u32[]{:S(2)}, u32[]{:S(2)}) collective-permute-start(f32[80,128]{1,0:T(8,128)S(1)} %get-tuple-element.61), channel_id=1, source_target_pairs={{0,1},{1,0},{2,3},{3,2},{4,5},{5,4},{6,7},{7,6},{8,9},{9,8},{10,11... | collective-permute-start | bytes 122888 | tf_op jit(solution)/shard_map/narrow_near/ppermute | solution.py:435
  87.8 3.1 %collective-permute-done.10.low = f32[72,128]{1,0:T(8,128)S(1)} collective-permute-done((f32[72,128]{1,0:T(8,128)S(1)}, f32[72,128]{1,0:T(8,128)S(1)}, u32[]{:S(2)}, u32[]{:S(2)}) %collective-permute-start.10) | collective-permute-done | bytes 36896 | tf_op jit(solution)/shard_map/narrow_far/ppermute | solution.py:433
  92.1 7.5 %all-to-all-start.2 = ((f32[128,1,384]{2,1,0:T(1,128)}), f32[128,1,384]{2,1,0:T(1,128)S(1)}, u32[]{:S(2)}, u32[]{:S(2)}) async-start(f32[128,1,384]{2,1,0:T(1,128)} %bitcast.13), calls=%async_computation.2 | async-start | bytes 393216 | tf_op jit(solution)/shard_map/all_to_all | solution.py:508
  99.5 5.5 %local_solve.5 = (f32[3,4,8,128]{3,2,1,0:T(8,128)S(1)}, f32[48,128]{1,0:T(8,128)S(1)}, f32[48,128]{1,0:T(8,128)S(1)}) custom-call(f32[3,8,16,128]{3,2,1,0:T(8,128)S(1)} %get-tuple-element.63.misfit, f32[22,6,16,128]{3,2,1,0:T(8,128)S(1)} %get-tuple-element.44.coef, f32[3,4,8,128]{3,2,1,0:T(8,128)S(1)} %get-tuple-element.64.current, ...), custom_call_target="tpu_custom_call" | custom-call | flops 30000000 | tf_op jit(solution)/shard_map/local_solve/pallas_call | solution.py:415
  105.0 7.1 %collective-permute-start.12 = (f32[48,128]{1,0:T(8,128)S(1)}, f32[48,128]{1,0:T(8,128)S(1)}, u32[]{:S(2)}, u32[]{:S(2)}) collective-permute-start(f32[48,128]{1,0:T(8,128)S(1)} %get-tuple-element.66), channel_id=1, source_target_pairs={{0,252},{4,8},{8,4},{12,16},{16,12},{20,24},{24,20},{28,32},{32,28... | collective-permute-start | bytes 73736 | tf_op jit(solution)/shard_map/wide_far/ppermute | solution.py:433
  113.5 2.8 %collective-permute-done.13.near = f32[48,128]{1,0:T(8,128)S(1)} collective-permute-done((f32[48,128]{1,0:T(8,128)S(1)}, f32[48,128]{1,0:T(8,128)S(1)}, u32[]{:S(2)}, u32[]{:S(2)}) %collective-permute-start.13) | collective-permute-done | bytes 24608 | tf_op jit(solution)/shard_map/wide_near/ppermute | solution.py:435
  116.3 2.2 %collective-permute-start.15 = (f32[80,128]{1,0:T(8,128)S(1)}, f32[80,128]{1,0:T(8,128)S(1)}, u32[]{:S(2)}, u32[]{:S(2)}) collective-permute-start(f32[80,128]{1,0:T(8,128)S(1)} %get-tuple-element.70), channel_id=1, source_target_pairs={{0,1},{1,0},{2,3},{3,2},{4,5},{5,4},{6,7},{7,6},{8,9},{9,8},{10,11... | collective-permute-start | bytes 122888 | tf_op jit(solution)/shard_map/narrow_near/ppermute | solution.py:435
  118.8 3.1 %collective-permute-done.14.low = f32[72,128]{1,0:T(8,128)S(1)} collective-permute-done((f32[72,128]{1,0:T(8,128)S(1)}, f32[72,128]{1,0:T(8,128)S(1)}, u32[]{:S(2)}, u32[]{:S(2)}) %collective-permute-start.14) | collective-permute-done | bytes 36896 | tf_op jit(solution)/shard_map/narrow_far/ppermute | solution.py:433
  (28 shorter events, 9.7 us)
Async XLA Ops:
  1.8 14.2 %collective-permute-start = (f32[216,128]{1,0:T(8,128)S(1)}, f32[216,128]{1,0:T(8,128)S(1)}, u32[]{:S(2)}, u32[]{:S(2)}) collective-permute-start(f32[216,128]{1,0:T(8,128)S(1)} %get-tuple-element.37), channel_id=1, source_target_pairs={{0,252},{4,8},{8,4},{12,16},{16,12},{20,24},{24,20},{28,32},{32,28... | collective-permute-start | bytes 331784 | tf_op jit(solution)/shard_map/wide_far/ppermute | solution.py:433
  13.2 5.1 %collective-permute-start.1 = (f32[216,128]{1,0:T(8,128)S(1)}, f32[216,128]{1,0:T(8,128)S(1)}, u32[]{:S(2)}, u32[]{:S(2)}) collective-permute-start(f32[216,128]{1,0:T(8,128)S(1)} %get-tuple-element.38), channel_id=1, source_target_pairs={{0,4},{4,0},{8,12},{12,8},{16,20},{20,16},{24,28},{28,24},{32,36},... | collective-permute-start | bytes 331784 | tf_op jit(solution)/shard_map/wide_near/ppermute | solution.py:435
  18.4 6.7 %collective-permute-start.2 = (f32[324,128]{1,0:T(8,128)S(1)}, f32[324,128]{1,0:T(8,128)S(1)}, u32[]{:S(2)}, u32[]{:S(2)}) collective-permute-start(f32[324,128]{1,0:T(8,128)S(1)} %get-tuple-element.40), channel_id=1, source_target_pairs={{0,3},{1,2},{2,1},{3,0},{4,7},{5,6},{6,5},{7,4},{8,11},{9,10},{10,... | collective-permute-start | bytes 497672 | tf_op jit(solution)/shard_map/narrow_far/ppermute | solution.py:433
  20.7 4.3 %collective-permute-start.3 = (f32[324,128]{1,0:T(8,128)S(1)}, f32[324,128]{1,0:T(8,128)S(1)}, u32[]{:S(2)}, u32[]{:S(2)}) collective-permute-start(f32[324,128]{1,0:T(8,128)S(1)} %get-tuple-element.41), channel_id=1, source_target_pairs={{0,1},{1,0},{2,3},{3,2},{4,5},{5,4},{6,7},{7,6},{8,9},{9,8},{10,11... | collective-permute-start | bytes 497672 | tf_op jit(solution)/shard_map/narrow_near/ppermute | solution.py:435
  27.5 32.4 %copy-start = (f32[32,8192]{1,0:T(8,128)S(1)}, f32[32,8192]{1,0:T(8,128)}, u32[]{:S(2)}) copy-start(f32[32,8192]{1,0:T(8,128)} %coarse.3) | copy-start | bytes 3145732
  27.5 26.4 %all-to-all-start = ((f32[128,1,384]{2,1,0:T(1,128)}), f32[128,1,384]{2,1,0:T(1,128)S(1)}, u32[]{:S(2)}, u32[]{:S(2)}) async-start(f32[128,1,384]{2,1,0:T(1,128)} %bitcast.12), calls=%async_computation | async-start | bytes 393216 | tf_op jit(solution)/shard_map/all_to_all | solution.py:508
  42.6 8.5 %collective-permute-start.4 = (f32[48,128]{1,0:T(8,128)S(1)}, f32[48,128]{1,0:T(8,128)S(1)}, u32[]{:S(2)}, u32[]{:S(2)}) collective-permute-start(f32[48,128]{1,0:T(8,128)S(1)} %get-tuple-element.47), channel_id=1, source_target_pairs={{0,252},{4,8},{8,4},{12,16},{16,12},{20,24},{24,20},{28,32},{32,28... | collective-permute-start | bytes 73736 | tf_op jit(solution)/shard_map/wide_far/ppermute | solution.py:433
  49.8 4.2 %collective-permute-start.5 = (f32[48,128]{1,0:T(8,128)S(1)}, f32[48,128]{1,0:T(8,128)S(1)}, u32[]{:S(2)}, u32[]{:S(2)}) collective-permute-start(f32[48,128]{1,0:T(8,128)S(1)} %get-tuple-element.48), channel_id=1, source_target_pairs={{0,4},{4,0},{8,12},{12,8},{16,20},{20,16},{24,28},{28,24},{32,36},... | collective-permute-start | bytes 73736 | tf_op jit(solution)/shard_map/wide_near/ppermute | solution.py:435
  54.0 5.9 %collective-permute-start.7 = (f32[80,128]{1,0:T(8,128)S(1)}, f32[80,128]{1,0:T(8,128)S(1)}, u32[]{:S(2)}, u32[]{:S(2)}) collective-permute-start(f32[80,128]{1,0:T(8,128)S(1)} %get-tuple-element.51), channel_id=1, source_target_pairs={{0,1},{1,0},{2,3},{3,2},{4,5},{5,4},{6,7},{7,6},{8,9},{9,8},{10,11... | collective-permute-start | bytes 122888 | tf_op jit(solution)/shard_map/narrow_near/ppermute | solution.py:435
  56.5 3.4 %collective-permute-start.6 = (f32[72,128]{1,0:T(8,128)S(1)}, f32[72,128]{1,0:T(8,128)S(1)}, u32[]{:S(2)}, u32[]{:S(2)}) collective-permute-start(f32[72,128]{1,0:T(8,128)S(1)} %get-tuple-element.50), channel_id=1, source_target_pairs={{0,3},{1,2},{2,1},{3,0},{4,7},{5,6},{6,5},{7,4},{8,11},{9,10},{10,... | collective-permute-start | bytes 110600 | tf_op jit(solution)/shard_map/narrow_far/ppermute | solution.py:433
  61.0 24.2 %all-to-all-start.1 = ((f32[128,1,384]{2,1,0:T(1,128)}), f32[128,1,384]{2,1,0:T(1,128)S(1)}, u32[]{:S(2)}, u32[]{:S(2)}) async-start(f32[128,1,384]{2,1,0:T(1,128)} %bitcast.14), calls=%async_computation.1 | async-start | bytes 393216 | tf_op jit(solution)/shard_map/all_to_all | solution.py:508
  74.1 8.5 %collective-permute-start.8 = (f32[48,128]{1,0:T(8,128)S(1)}, f32[48,128]{1,0:T(8,128)S(1)}, u32[]{:S(2)}, u32[]{:S(2)}) collective-permute-start(f32[48,128]{1,0:T(8,128)S(1)} %get-tuple-element.57), channel_id=1, source_target_pairs={{0,252},{4,8},{8,4},{12,16},{16,12},{20,24},{24,20},{28,32},{32,28... | collective-permute-start | bytes 73736 | tf_op jit(solution)/shard_map/wide_far/ppermute | solution.py:433
  81.1 4.2 %collective-permute-start.9 = (f32[48,128]{1,0:T(8,128)S(1)}, f32[48,128]{1,0:T(8,128)S(1)}, u32[]{:S(2)}, u32[]{:S(2)}) collective-permute-start(f32[48,128]{1,0:T(8,128)S(1)} %get-tuple-element.58), channel_id=1, source_target_pairs={{0,4},{4,0},{8,12},{12,8},{16,20},{20,16},{24,28},{28,24},{32,36},... | collective-permute-start | bytes 73736 | tf_op jit(solution)/shard_map/wide_near/ppermute | solution.py:435
  85.3 5.6 %collective-permute-start.11 = (f32[80,128]{1,0:T(8,128)S(1)}, f32[80,128]{1,0:T(8,128)S(1)}, u32[]{:S(2)}, u32[]{:S(2)}) collective-permute-start(f32[80,128]{1,0:T(8,128)S(1)} %get-tuple-element.61), channel_id=1, source_target_pairs={{0,1},{1,0},{2,3},{3,2},{4,5},{5,4},{6,7},{7,6},{8,9},{9,8},{10,11... | collective-permute-start | bytes 122888 | tf_op jit(solution)/shard_map/narrow_near/ppermute | solution.py:435
  87.5 3.4 %collective-permute-start.10 = (f32[72,128]{1,0:T(8,128)S(1)}, f32[72,128]{1,0:T(8,128)S(1)}, u32[]{:S(2)}, u32[]{:S(2)}) collective-permute-start(f32[72,128]{1,0:T(8,128)S(1)} %get-tuple-element.60), channel_id=1, source_target_pairs={{0,3},{1,2},{2,1},{3,0},{4,7},{5,6},{6,5},{7,4},{8,11},{9,10},{10,... | collective-permute-start | bytes 110600 | tf_op jit(solution)/shard_map/narrow_far/ppermute | solution.py:433
  92.1 24.2 %all-to-all-start.2 = ((f32[128,1,384]{2,1,0:T(1,128)}), f32[128,1,384]{2,1,0:T(1,128)S(1)}, u32[]{:S(2)}, u32[]{:S(2)}) async-start(f32[128,1,384]{2,1,0:T(1,128)} %bitcast.13), calls=%async_computation.2 | async-start | bytes 393216 | tf_op jit(solution)/shard_map/all_to_all | solution.py:508
  105.0 8.5 %collective-permute-start.12 = (f32[48,128]{1,0:T(8,128)S(1)}, f32[48,128]{1,0:T(8,128)S(1)}, u32[]{:S(2)}, u32[]{:S(2)}) collective-permute-start(f32[48,128]{1,0:T(8,128)S(1)} %get-tuple-element.66), channel_id=1, source_target_pairs={{0,252},{4,8},{8,4},{12,16},{16,12},{20,24},{24,20},{28,32},{32,28... | collective-permute-start | bytes 73736 | tf_op jit(solution)/shard_map/wide_far/ppermute | solution.py:433
  112.1 4.2 %collective-permute-start.13 = (f32[48,128]{1,0:T(8,128)S(1)}, f32[48,128]{1,0:T(8,128)S(1)}, u32[]{:S(2)}, u32[]{:S(2)}) collective-permute-start(f32[48,128]{1,0:T(8,128)S(1)} %get-tuple-element.67), channel_id=1, source_target_pairs={{0,4},{4,0},{8,12},{12,8},{16,20},{20,16},{24,28},{28,24},{32,36},... | collective-permute-start | bytes 73736 | tf_op jit(solution)/shard_map/wide_near/ppermute | solution.py:435
  116.3 5.6 %collective-permute-start.15 = (f32[80,128]{1,0:T(8,128)S(1)}, f32[80,128]{1,0:T(8,128)S(1)}, u32[]{:S(2)}, u32[]{:S(2)}) collective-permute-start(f32[80,128]{1,0:T(8,128)S(1)} %get-tuple-element.70), channel_id=1, source_target_pairs={{0,1},{1,0},{2,3},{3,2},{4,5},{5,4},{6,7},{7,6},{8,9},{9,8},{10,11... | collective-permute-start | bytes 122888 | tf_op jit(solution)/shard_map/narrow_near/ppermute | solution.py:435
  118.5 3.4 %collective-permute-start.14 = (f32[72,128]{1,0:T(8,128)S(1)}, f32[72,128]{1,0:T(8,128)S(1)}, u32[]{:S(2)}, u32[]{:S(2)}) collective-permute-start(f32[72,128]{1,0:T(8,128)S(1)} %get-tuple-element.69), channel_id=1, source_target_pairs={{0,3},{1,2},{2,1},{3,0},{4,7},{5,6},{6,5},{7,4},{8,11},{9,10},{10,... | collective-permute-start | bytes 110600 | tf_op jit(solution)/shard_map/narrow_far/ppermute | solution.py:433

commit v5 on v3

--- a/solution.py
+++ b/solution.py
@@ -1,11 +1,10 @@
-import functools
-
 import jax
 import jax.numpy as jnp
 from jax import lax
 from jax.experimental import pallas as pl
 from jax.experimental.pallas import tpu as pltpu
 from jax.sharding import PartitionSpec as P
+
 
 AGG_LOC = 32
 SWEEPS = 3
@@ -162,13 +161,11 @@
 
 
 def pack_current(current, far, near, received, low, high, part):
-    total = received[0:24]
-    for i in range(24, received.shape[0], 24):
-        total += received[i : i + 24]
-    block_of = lax.broadcasted_iota(jnp.int32, (24, LANES), 0) % 3
-    part[...] = jnp.zeros((8, LANES), f32)
-    for k in range(3):
-        part[k : k + 1, :] = jnp.sum(jnp.where(block_of == k, total, 0.0), axis=0, keepdims=True)
+    total = received[0:8]
+    for i in range(8, received.shape[0], 8):
+        total += received[i : i + 8]
+    part[...] = jnp.broadcast_to(jnp.sum(total, axis=0, keepdims=True), (8, LANES))
+    low[72:80] = part[...]
     high[72:80] = part[...]
     odd = is_odd("wide")
     narrow_odd = is_odd("narrow")
@@ -190,17 +187,21 @@
     count = coarse.shape[1] // LANES
     for w in range(count):
         row = jnp.sum(coarse[:, w * LANES : (w + 1) * LANES] * weight, axis=0, keepdims=True)
-        spread[w + 1 : w + 2, :] = row
-    spread[0:1, :] = spread[count : count + 1, :]
-    spread[count + 1 : count + 2, :] = spread[1:2, :]
-    for w in range(count):
-        rows = spread[w : w + 3, :]
-        for half in range(2):
-            at = 3 * (2 * w + half)
-            staged[at : at + 3, :] = rows
-
-
-def solve_box(values, coef, agg, coarse, factors_hbm, payload, current, far, near, scratch):
+        spread[0, w + 1 : w + 2, :] = row
+    middle = spread[0, 1 : count + 1, :]
+    for turn in range(4):
+        turned = shifted(middle, -32 * turn, 1) if turn else middle
+        if turn:
+            spread[turn, 1 : count + 1, :] = turned
+        spread[turn, 0:1, :] = turned[count - 1 : count]
+        spread[turn, count + 1 : count + 2, :] = turned[0:1]
+    lane = lane_index((count, LANES))
+    for n in range(4):
+        before, own, after = (spread[(k - n) % 4, k : k + count, :] for k in range(3))
+        staged[pl.ds(n, count, stride=4), :] = jnp.where(lane < 32, before, jnp.where(lane < 64, own, after))
+
+
+def solve_box(values, coef, agg, coarse, factors_hbm, payload, current, far, near, scratch, coarse_fetch=None):
     misfit, sums, spread, staged, one, two, factors, tile_sems, sem = scratch
     inside = box_mask()
     rolled = {}
@@ -211,6 +212,8 @@
         applied = operate_pair(values, coef, a, rolled)
         for c in range(3):
             misfit[c, a] = jnp.where(inside, coef[RHS + c, a - 1] - applied[c], 0.0)
+    if coarse_fetch is not None:
+        coarse_fetch.wait()
     coarse_part([misfit[0, a, 0:8] for a in range(2, 6)], agg, coarse, sums, spread, staged)
     write = pltpu.make_async_copy(staged, payload, sem)
     write.start()
@@ -236,7 +239,7 @@
     high,
     mine,
     agg,
-    coarse,
+    coarse_hbm,
     factors_hbm,
     coef,
     slots,
@@ -245,9 +248,13 @@
     far_out,
     near_out,
     rim,
+    coarse,
+    coarse_sem,
     values,
     *scratch,
 ):
+    coarse_fetch = pltpu.make_async_copy(coarse_hbm, coarse, coarse_sem)
+    coarse_fetch.start()
     for fetch in fetch_tiles(factors_hbm, scratch[-3], scratch[-2]):
         fetch.start()
     odd = is_odd("wide")
@@ -274,12 +281,9 @@
     row = lax.broadcasted_iota(jnp.int32, (ROWS, LANES), 0)
     lane = lane_index((ROWS, LANES))
     low = lane < 64
-    place_of = lax.axis_index("narrow")
-    below, here, above = (32 * ((place_of + i) % 4) for i in (3, 0, 1))
-    offset = jnp.where(row < 8, here, jnp.where(row < 12, above, below))
     inside = box_mask()
     for a in range(8):
-        slots[a] = rim[3, a].astype(jnp.int32) + offset
+        slots[a] = rim[3, a].astype(jnp.int32) + (0 if a < 2 else 64 if a >= 6 else 32)
     for a in range(1, 7):
         tx, ty = rim[0, a], rim[1, a]
         tz = jnp.where((lane % 64) < 63, rim[2, a], 0.0)
@@ -297,17 +301,18 @@
         for c in range(3):
             diagonal = jnp.where(inside, centre + coef[COUP + 4 * c, a - 1], 1.0)
             coef[INV + c, a - 1] = jnp.where(inside, 1.0 / diagonal, 0.0)
-    solve_box(values, coef, agg, coarse, factors_hbm, payload, current, far_out, near_out, scratch)
+    solve_box(values, coef, agg, coarse, factors_hbm, payload, current, far_out, near_out, scratch, coarse_fetch)
 
 
 def gather_values(current, far, near, low, high, part, slots, values):
     odd = is_odd("wide")
     narrow_odd = is_odd("narrow")
-    total = part[...] + high[72:80]
+    a_part, b_part = low[72:80], high[72:80]
+    upper_rows = lax.broadcasted_iota(jnp.int32, (8, LANES), 0) < 4
+    from_above, from_below = pick(narrow_odd, a_part, b_part), pick(narrow_odd, b_part, a_part)
+    tables = (part[...], jnp.where(upper_rows, from_above, from_below))
     blank = jnp.zeros((2, LANES), f32)
     for a in range(8):
-        block = 0 if a < 2 else 2 if a >= 6 else 1
-        table = jnp.broadcast_to(total[block : block + 1], (8, LANES))
         for c in range(3):
             at = (c * 8 + a) * 3
             first, second = low[at : at + 3], high[at : at + 3]
@@ -317,7 +322,7 @@
             values[c, a, 13:16] = pick(narrow_odd, second, first)
         for half in range(2):
             where = slots[a, 8 * half : 8 * half + 8]
-            lifted = jnp.take_along_axis(table, where, axis=1, mode="promise_in_bounds")
+            lifted = jnp.take_along_axis(tables[half], where, axis=1, mode="promise_in_bounds")
             values[0, a, 8 * half : 8 * half + 8] += lifted
 
 
@@ -379,7 +384,9 @@
             ref[c, 7] = blank
     for a in range(1, 7):
         edge = a in (1, 6)
-        fetches[a - 1].wait()
+        if a in (1, 4):
+            for fetch in fetches[a - 1 : a + 2]:
+                fetch.wait()
         for half, cols in ((0, own_cols), (1, [8, -1] if edge else [8, 9, -2, -1])):
             part = tiles([misfit[c, a, 8 * half : 8 * half + 8] for c in range(3)], a, cols, half)
             for c in range(3):
@@ -405,7 +412,7 @@
             moved[c, a - 2] = values[c, a, 0:8] + (two[c, a, 0:8] + part[c])
 
 
-def call(body, name, outs, scratch, operands, in_hbm=(), out_hbm=(), flops=1000000):
+def call(body, outs, scratch, operands, in_hbm=(), out_hbm=(), flops=1000000):
     vmem = pl.BlockSpec(memory_space=pltpu.VMEM)
     hbm = pl.BlockSpec(memory_space=pltpu.HBM)
     operands = [pltpu.with_memory_space_constraint(x, pltpu.HBM) if i in in_hbm else x for i, x in enumerate(operands)]
@@ -420,16 +427,13 @@
         scratch_shapes=scratch,
         compiler_params=pltpu.CompilerParams(vmem_limit_bytes=VMEM_LIMIT),
         cost_estimate=pl.CostEstimate(flops=flops, bytes_accessed=0, transcendentals=0),
-        name=name,
     )(*operands)
 
 
 def swaps(axis, far, near):
     count = lax.axis_size(axis)
-    with jax.named_scope(axis + "_far"):
-        far = lax.ppermute(far, axis, [(i, (i + (1 if i % 2 else -1)) % count) for i in range(count)])
-    with jax.named_scope(axis + "_near"):
-        near = lax.ppermute(near, axis, [(i, i ^ 1) for i in range(count)])
+    far = lax.ppermute(far, axis, [(i, (i + (1 if i % 2 else -1)) % count) for i in range(count)])
+    near = lax.ppermute(near, axis, [(i, i ^ 1) for i in range(count)])
     return far, near
 
 
@@ -437,19 +441,17 @@
     rhs, start, trans, accum, coupling, well_cells, well_index, agg_map, tile_factors, coarse_inverse
 ):
     devices = lax.axis_size("wide") * lax.axis_size("narrow")
-    members = devices // 2
-    groups = [[4 * w + n for w in range(devices // 4) for n in (parity, parity + 2)] for parity in range(2)]
     dma = pltpu.SemaphoreType.DMA
     own = ((3, 4, 8, LANES), f32)
     box = (3, PAIRS, ROWS, LANES)
     wide_type = ((48, LANES), f32)
-    narrow_type = ((72, LANES), f32)
-    payload_type = ((members * 3, LANES), f32)
+    narrow_type = ((80, LANES), f32)
+    payload_type = ((devices, LANES), f32)
     scratch = [
         pltpu.VMEM(box, f32),
         pltpu.VMEM(box, f32),
         pltpu.VMEM((AGG_LOC, LANES), f32),
-        pltpu.VMEM((devices // 4 + 8, LANES), f32),
+        pltpu.VMEM((4, devices // 4 + 8, LANES), f32),
         pltpu.VMEM(payload_type[0], f32),
         pltpu.VMEM(box, f32),
         pltpu.VMEM(box, f32),
@@ -460,7 +462,6 @@
 
     mine, agg, far, near = call(
         add_wells_and_pack,
-        "pack_wide",
         [((FULL + THIN, 4, 8, LANES), f32), ((4, 8, LANES), f32)] + [((WIDE_ROWS, LANES), f32)] * 2,
         [
             pltpu.VMEM((1, 64), jnp.int32),
@@ -482,34 +483,28 @@
         in_hbm=range(8),
     )
     far, near = swaps("wide", far, near)
-    low, high = call(pack_narrow, "pack_narrow", [((NARROW_ROWS, LANES), f32)] * 2, [], [far, near, mine])
+    low, high = call(pack_narrow, [((NARROW_ROWS, LANES), f32)] * 2, [], [far, near, mine])
     low, high = swaps("narrow", low, high)
     coef, slots, payload, current, far, near = call(
         first_sweep,
-        "first_sweep",
         [((N_COEF, 6, ROWS, LANES), f32), ((PAIRS, ROWS, LANES), jnp.int32), payload_type, own, wide_type, wide_type],
-        [pltpu.VMEM((4, PAIRS, ROWS, LANES), f32)] + scratch,
+        [pltpu.VMEM((4, PAIRS, ROWS, LANES), f32), pltpu.VMEM(coarse_inverse.shape, f32), dma] + scratch,
         [far, near, low, high, mine, agg, coarse_inverse, tile_factors],
-        in_hbm=(7,),
+        in_hbm=(6, 7),
         out_hbm=(2,),
     )
     for sweep in range(SWEEPS):
-        blocks = payload.reshape(members, 1, 3 * LANES)
-        received = lax.all_to_all(blocks, ("wide", "narrow"), 0, 0, axis_index_groups=groups).reshape(payload_type[0])
+        blocks = payload.reshape(devices, 1, LANES)
+        received = lax.all_to_all(blocks, ("wide", "narrow"), 0, 0).reshape(payload_type[0])
         far, near = swaps("wide", far, near)
         low, high, part = call(
-            pack_current,
-            "pack_current",
-            [narrow_type, ((80, LANES), f32), ((8, LANES), f32)],
-            [],
-            [current, far, near, received],
+            pack_current, [narrow_type, narrow_type, ((8, LANES), f32)], [], [current, far, near, received]
         )
         low, high = swaps("narrow", low, high)
         known = [current, far, near, low, high, part, slots, coef]
         if sweep < SWEEPS - 1:
             payload, current, far, near = call(
                 next_sweep,
-                "next_sweep",
                 [payload_type, own, wide_type, wide_type],
                 scratch,
                 known + [agg, coarse_inverse, tile_factors],
@@ -517,7 +512,7 @@
                 out_hbm=(0,),
             )
         else:
-            iterate, residual = call(last_misfit, "last_misfit", [own, own], [pltpu.VMEM(box, f32)], known)
+            iterate, residual = call(last_misfit, [own, own], [pltpu.VMEM(box, f32)], known)
     return iterate, residual
 
 

time: 118 us -> 116 us (0.983)
  waiting for transfers between devices: 33.3 us -> 27 us
  starting transfers between devices: 66.3 us -> 71.9 us
  local copies, waits for them, and re-layouts: 1.23 us -> 0.01 us
    ppermute x8, starting transfers between devices: 36.3 us -> 47.7 us  [swaps(): lax.ppermute(far, axis, [(i, (i + (1 if i % 2 else -1)) % count) for i in...]
    ppermute x8, starting transfers between devices: 7.5 us -> 0.02 us  [swaps(): near = lax.ppermute(near, axis, [(i, i ^ 1) for i in range(count)])]
    ppermute x8, waiting for transfers between devices: 25.3 us -> 20.7 us  [swaps(): lax.ppermute(far, axis, [(i, (i + (1 if i % 2 else -1)) % count) for i in...]
    all_to_all x3, starting transfers between devices: 22.5 us -> 24.2 us  [per_device(): lax.all_to_all(blocks, ('wide', 'narrow'), 0, 0).reshape(payload_type[0])]
    all_to_all x3, waiting for transfers between devices: 1.4 us -> 0.01 us  [per_device(): lax.all_to_all(blocks, ('wide', 'narrow'), 0, 0).reshape(payload_type[0])]
    unnamed x4 -> x2, local copies, waits for them, and re-layouts: 1.23 us -> 0.01 us
  transfers between devices with their start and end apart: 19 -> 19, of which waited for: 15 -> 12; matrix products, arithmetic and copies ran while one was open for 0% -> 0% of each run, Pallas kernels for 0% -> 0%
where the time goes in v5:
time: 116 us; the launch traced here: 115 us
  starting transfers between devices  71.9 us (62%)
  waiting for transfers between devices  27 us (23%)
  Pallas kernels  15.7 us (14%)
    ppermute x8, starting transfers between devices, swaps(): lax.ppermute(far, axis, [(i, (i + (1 if i % 2 else -1)) % count) for i in...  47.7 us
    all_to_all x3, starting transfers between devices, per_device(): lax.all_to_all(blocks, ('wide', 'narrow'), 0, 0).reshape(payload_type[0])  24.2 us
    ppermute x8, waiting for transfers between devices, swaps(): lax.ppermute(far, axis, [(i, (i + (1 if i % 2 else -1)) % count) for i in...  20.7 us
    pallas_call x9, Pallas kernels, call(): pl.pallas_call(body, out_shape=[pltpu.HBM(shape, dtype) if i in out_hbm e...  15.7 us
    ppermute x8, waiting for transfers between devices, swaps(): near = lax.ppermute(near, axis, [(i, i ^ 1) for i in range(count)])  6.32 us
  transfers between devices with their start and end apart: 19, of which 12 were waited for; matrix products, arithmetic and copies ran while one was open for 0% of the time, Pallas kernels for 0%

profile of v5, /device:TPU:1, one launch (start us, length us, event | category | flops | bytes accessed | tf_op | source)
XLA Modules:
  0.0 115.4 jit_solution(9893895403874703768)
XLA Ops:
  1.8 11.4 %collective-permute-start = (f32[216,128]{1,0:T(8,128)S(1)}, f32[216,128]{1,0:T(8,128)S(1)}, u32[]{:S(2)}, u32[]{:S(2)}) collective-permute-start(f32[216,128]{1,0:T(8,128)S(1)} %get-tuple-element.31), channel_id=1, source_target_pairs={{0,252},{4,8},{8,4},{12,16},{16,12},{20,24},{24,20},{28,32},{32,28... | collective-permute-start | bytes 331784 | tf_op jit(solution)/shard_map/ppermute | solution.py:435
  13.2 2.8 %collective-permute-done.far = f32[216,128]{1,0:T(8,128)S(1)} collective-permute-done((f32[216,128]{1,0:T(8,128)S(1)}, f32[216,128]{1,0:T(8,128)S(1)}, u32[]{:S(2)}, u32[]{:S(2)}) %collective-permute-start) | collective-permute-done | bytes 110624 | tf_op jit(solution)/shard_map/ppermute | solution.py:435
  15.9 2.3 %collective-permute-done.1.near = f32[216,128]{1,0:T(8,128)S(1)} collective-permute-done((f32[216,128]{1,0:T(8,128)S(1)}, f32[216,128]{1,0:T(8,128)S(1)}, u32[]{:S(2)}, u32[]{:S(2)}) %collective-permute-start.1) | collective-permute-done | bytes 110624 | tf_op jit(solution)/shard_map/ppermute | solution.py:436
  18.4 2.4 %collective-permute-start.2 = (f32[324,128]{1,0:T(8,128)S(1)}, f32[324,128]{1,0:T(8,128)S(1)}, u32[]{:S(2)}, u32[]{:S(2)}) collective-permute-start(f32[324,128]{1,0:T(8,128)S(1)} %get-tuple-element.34), channel_id=1, source_target_pairs={{0,3},{1,2},{2,1},{3,0},{4,7},{5,6},{6,5},{7,4},{8,11},{9,10},{10,... | collective-permute-start | bytes 497672 | tf_op jit(solution)/shard_map/ppermute | solution.py:435
  20.8 4.3 %collective-permute-done.2.low = f32[324,128]{1,0:T(8,128)S(1)} collective-permute-done((f32[324,128]{1,0:T(8,128)S(1)}, f32[324,128]{1,0:T(8,128)S(1)}, u32[]{:S(2)}, u32[]{:S(2)}) %collective-permute-start.2) | collective-permute-done | bytes 165920 | tf_op jit(solution)/shard_map/ppermute | solution.py:435
  25.0 5.1 %shard_map.115 = (f32[22,6,16,128]{3,2,1,0:T(8,128)S(1)}, s32[8,16,128]{2,1,0:T(8,128)S(1)}, f32[256,128]{1,0:T(8,128)}, f32[3,4,8,128]{3,2,1,0:T(8,128)S(1)}, f...) custom-call(f32[216,128]{1,0:T(8,128)S(1)} %collective-permute-done.far, f32[216,128]{1,0:T(8,128)S(1)} %collective-permute-done.1.near, ...), custom_call_target="tpu_custom_call" | custom-call | flops 1000000 | tf_op jit(solution)/shard_map/pallas_call | solution.py:419
  30.2 8.6 %all-to-all-start = ((f32[256,1,128]{2,1,0:T(1,128)}), f32[256,1,128]{2,1,0:T(1,128)S(1)}, u32[]{:S(2)}, u32[]{:S(2)}) async-start(f32[256,1,128]{2,1,0:T(1,128)} %bitcast.19), calls=%async_computation | async-start | bytes 262144 | tf_op jit(solution)/shard_map/all_to_all | solution.py:498
  38.8 9.1 %collective-permute-start.4 = (f32[48,128]{1,0:T(8,128)S(1)}, f32[48,128]{1,0:T(8,128)S(1)}, u32[]{:S(2)}, u32[]{:S(2)}) collective-permute-start(f32[48,128]{1,0:T(8,128)S(1)} %get-tuple-element.38), channel_id=1, source_target_pairs={{0,252},{4,8},{8,4},{12,16},{16,12},{20,24},{24,20},{28,32},{32,28... | collective-permute-start | bytes 73736 | tf_op jit(solution)/shard_map/ppermute | solution.py:435
  47.9 2.9 %collective-permute-done.4.far = f32[48,128]{1,0:T(8,128)S(1)} collective-permute-done((f32[48,128]{1,0:T(8,128)S(1)}, f32[48,128]{1,0:T(8,128)S(1)}, u32[]{:S(2)}, u32[]{:S(2)}) %collective-permute-start.4) | collective-permute-done | bytes 24608 | tf_op jit(solution)/shard_map/ppermute | solution.py:435
  52.1 2.1 %collective-permute-start.6 = (f32[80,128]{1,0:T(8,128)S(1)}, f32[80,128]{1,0:T(8,128)S(1)}, u32[]{:S(2)}, u32[]{:S(2)}) collective-permute-start(f32[80,128]{1,0:T(8,128)S(1)} %get-tuple-element.41), channel_id=1, source_target_pairs={{0,3},{1,2},{2,1},{3,0},{4,7},{5,6},{6,5},{7,4},{8,11},{9,10},{10,... | collective-permute-start | bytes 122888 | tf_op jit(solution)/shard_map/ppermute | solution.py:435
  54.2 1.7 %collective-permute-done.6.low = f32[80,128]{1,0:T(8,128)S(1)} collective-permute-done((f32[80,128]{1,0:T(8,128)S(1)}, f32[80,128]{1,0:T(8,128)S(1)}, u32[]{:S(2)}, u32[]{:S(2)}) %collective-permute-start.6) | collective-permute-done | bytes 40992 | tf_op jit(solution)/shard_map/ppermute | solution.py:435
  55.9 4.2 %shard_map.117 = (f32[256,128]{1,0:T(8,128)}, f32[3,4,8,128]{3,2,1,0:T(8,128)S(1)}, f32[48,128]{1,0:T(8,128)S(1)}, f32[48,128]{1,0:T(8,128)S(1)}) custom-call(f32[3,4,8,128]{3,2,1,0:T(8,128)S(1)} %get-tuple-element.37.current, f32[48,128]{1,0:T(8,128)S(1)} %collective-permute-done.4.far, f32[48,128]{1,0:T(8,128)S(1)} %collective-permute-done.5.near, ...), custom_call_target="tpu_custom_call" | custom-call | flops 1000000 | tf_op jit(solution)/shard_map/pallas_call | solution.py:419
  60.2 7.8 %all-to-all-start.1 = ((f32[256,1,128]{2,1,0:T(1,128)}), f32[256,1,128]{2,1,0:T(1,128)S(1)}, u32[]{:S(2)}, u32[]{:S(2)}) async-start(f32[256,1,128]{2,1,0:T(1,128)} %bitcast.21), calls=%async_computation.1 | async-start | bytes 262144 | tf_op jit(solution)/shard_map/all_to_all | solution.py:498
  68.0 9.3 %collective-permute-start.8 = (f32[48,128]{1,0:T(8,128)S(1)}, f32[48,128]{1,0:T(8,128)S(1)}, u32[]{:S(2)}, u32[]{:S(2)}) collective-permute-start(f32[48,128]{1,0:T(8,128)S(1)} %get-tuple-element.47), channel_id=1, source_target_pairs={{0,252},{4,8},{8,4},{12,16},{16,12},{20,24},{24,20},{28,32},{32,28... | collective-permute-start | bytes 73736 | tf_op jit(solution)/shard_map/ppermute | solution.py:435
  77.3 2.8 %collective-permute-done.8.far = f32[48,128]{1,0:T(8,128)S(1)} collective-permute-done((f32[48,128]{1,0:T(8,128)S(1)}, f32[48,128]{1,0:T(8,128)S(1)}, u32[]{:S(2)}, u32[]{:S(2)}) %collective-permute-start.8) | collective-permute-done | bytes 24608 | tf_op jit(solution)/shard_map/ppermute | solution.py:435
  80.1 1.4 %collective-permute-done.9.near = f32[48,128]{1,0:T(8,128)S(1)} collective-permute-done((f32[48,128]{1,0:T(8,128)S(1)}, f32[48,128]{1,0:T(8,128)S(1)}, u32[]{:S(2)}, u32[]{:S(2)}) %collective-permute-start.9) | collective-permute-done | bytes 24608 | tf_op jit(solution)/shard_map/ppermute | solution.py:436
  81.6 2.1 %collective-permute-start.10 = (f32[80,128]{1,0:T(8,128)S(1)}, f32[80,128]{1,0:T(8,128)S(1)}, u32[]{:S(2)}, u32[]{:S(2)}) collective-permute-start(f32[80,128]{1,0:T(8,128)S(1)} %get-tuple-element.50), channel_id=1, source_target_pairs={{0,3},{1,2},{2,1},{3,0},{4,7},{5,6},{6,5},{7,4},{8,11},{9,10},{10,... | collective-permute-start | bytes 122888 | tf_op jit(solution)/shard_map/ppermute | solution.py:435
  83.7 1.7 %collective-permute-done.10.low = f32[80,128]{1,0:T(8,128)S(1)} collective-permute-done((f32[80,128]{1,0:T(8,128)S(1)}, f32[80,128]{1,0:T(8,128)S(1)}, u32[]{:S(2)}, u32[]{:S(2)}) %collective-permute-start.10) | collective-permute-done | bytes 40992 | tf_op jit(solution)/shard_map/ppermute | solution.py:435
  85.3 4.2 %shard_map.119 = (f32[256,128]{1,0:T(8,128)}, f32[3,4,8,128]{3,2,1,0:T(8,128)S(1)}, f32[48,128]{1,0:T(8,128)S(1)}, f32[48,128]{1,0:T(8,128)S(1)}) custom-call(f32[3,4,8,128]{3,2,1,0:T(8,128)S(1)} %get-tuple-element.46.current, f32[48,128]{1,0:T(8,128)S(1)} %collective-permute-done.8.far, f32[48,128]{1,0:T(8,128)S(1)} %collective-permute-done.9.near, ...), custom_call_target="tpu_custom_call" | custom-call | flops 1000000 | tf_op jit(solution)/shard_map/pallas_call | solution.py:419
  89.6 7.8 %all-to-all-start.2 = ((f32[256,1,128]{2,1,0:T(1,128)}), f32[256,1,128]{2,1,0:T(1,128)S(1)}, u32[]{:S(2)}, u32[]{:S(2)}) async-start(f32[256,1,128]{2,1,0:T(1,128)} %bitcast.20), calls=%async_computation.2 | async-start | bytes 262144 | tf_op jit(solution)/shard_map/all_to_all | solution.py:498
  97.4 9.1 %collective-permute-start.12 = (f32[48,128]{1,0:T(8,128)S(1)}, f32[48,128]{1,0:T(8,128)S(1)}, u32[]{:S(2)}, u32[]{:S(2)}) collective-permute-start(f32[48,128]{1,0:T(8,128)S(1)} %get-tuple-element.54), channel_id=1, source_target_pairs={{0,252},{4,8},{8,4},{12,16},{16,12},{20,24},{24,20},{28,32},{32,28... | collective-permute-start | bytes 73736 | tf_op jit(solution)/shard_map/ppermute | solution.py:435
  106.6 2.9 %collective-permute-done.12.far = f32[48,128]{1,0:T(8,128)S(1)} collective-permute-done((f32[48,128]{1,0:T(8,128)S(1)}, f32[48,128]{1,0:T(8,128)S(1)}, u32[]{:S(2)}, u32[]{:S(2)}) %collective-permute-start.12) | collective-permute-done | bytes 24608 | tf_op jit(solution)/shard_map/ppermute | solution.py:435
  110.8 2.1 %collective-permute-start.14 = (f32[80,128]{1,0:T(8,128)S(1)}, f32[80,128]{1,0:T(8,128)S(1)}, u32[]{:S(2)}, u32[]{:S(2)}) collective-permute-start(f32[80,128]{1,0:T(8,128)S(1)} %get-tuple-element.57), channel_id=1, source_target_pairs={{0,3},{1,2},{2,1},{3,0},{4,7},{5,6},{6,5},{7,4},{8,11},{9,10},{10,... | collective-permute-start | bytes 122888 | tf_op jit(solution)/shard_map/ppermute | solution.py:435
  112.9 1.7 %collective-permute-done.14.low = f32[80,128]{1,0:T(8,128)S(1)} collective-permute-done((f32[80,128]{1,0:T(8,128)S(1)}, f32[80,128]{1,0:T(8,128)S(1)}, u32[]{:S(2)}, u32[]{:S(2)}) %collective-permute-start.14) | collective-permute-done | bytes 40992 | tf_op jit(solution)/shard_map/ppermute | solution.py:435
  (25 shorter events, 4.7 us)
Async XLA Ops:
  1.8 14.2 %collective-permute-start = (f32[216,128]{1,0:T(8,128)S(1)}, f32[216,128]{1,0:T(8,128)S(1)}, u32[]{:S(2)}, u32[]{:S(2)}) collective-permute-start(f32[216,128]{1,0:T(8,128)S(1)} %get-tuple-element.31), channel_id=1, source_target_pairs={{0,252},{4,8},{8,4},{12,16},{16,12},{20,24},{24,20},{28,32},{32,28... | collective-permute-start | bytes 331784 | tf_op jit(solution)/shard_map/ppermute | solution.py:435
  13.2 5.1 %collective-permute-start.1 = (f32[216,128]{1,0:T(8,128)S(1)}, f32[216,128]{1,0:T(8,128)S(1)}, u32[]{:S(2)}, u32[]{:S(2)}) collective-permute-start(f32[216,128]{1,0:T(8,128)S(1)} %get-tuple-element.32), channel_id=1, source_target_pairs={{0,4},{4,0},{8,12},{12,8},{16,20},{20,16},{24,28},{28,24},{32,36},... | collective-permute-start | bytes 331784 | tf_op jit(solution)/shard_map/ppermute | solution.py:436
  18.4 6.7 %collective-permute-start.2 = (f32[324,128]{1,0:T(8,128)S(1)}, f32[324,128]{1,0:T(8,128)S(1)}, u32[]{:S(2)}, u32[]{:S(2)}) collective-permute-start(f32[324,128]{1,0:T(8,128)S(1)} %get-tuple-element.34), channel_id=1, source_target_pairs={{0,3},{1,2},{2,1},{3,0},{4,7},{5,6},{6,5},{7,4},{8,11},{9,10},{10,... | collective-permute-start | bytes 497672 | tf_op jit(solution)/shard_map/ppermute | solution.py:435
  20.7 4.3 %collective-permute-start.3 = (f32[324,128]{1,0:T(8,128)S(1)}, f32[324,128]{1,0:T(8,128)S(1)}, u32[]{:S(2)}, u32[]{:S(2)}) collective-permute-start(f32[324,128]{1,0:T(8,128)S(1)} %get-tuple-element.35), channel_id=1, source_target_pairs={{0,1},{1,0},{2,3},{3,2},{4,5},{5,4},{6,7},{7,6},{8,9},{9,8},{10,11... | collective-permute-start | bytes 497672 | tf_op jit(solution)/shard_map/ppermute | solution.py:436
  25.0 30.9 %copy-start = (f32[32,8192]{1,0:T(8,128)S(1)}, f32[32,8192]{1,0:T(8,128)}, u32[]{:S(2)}) copy-start(f32[32,8192]{1,0:T(8,128)} %coarse.3) | copy-start | bytes 3145732
  30.2 21.9 %all-to-all-start = ((f32[256,1,128]{2,1,0:T(1,128)}), f32[256,1,128]{2,1,0:T(1,128)S(1)}, u32[]{:S(2)}, u32[]{:S(2)}) async-start(f32[256,1,128]{2,1,0:T(1,128)} %bitcast.19), calls=%async_computation | async-start | bytes 262144 | tf_op jit(solution)/shard_map/all_to_all | solution.py:498
  38.8 12.0 %collective-permute-start.4 = (f32[48,128]{1,0:T(8,128)S(1)}, f32[48,128]{1,0:T(8,128)S(1)}, u32[]{:S(2)}, u32[]{:S(2)}) collective-permute-start(f32[48,128]{1,0:T(8,128)S(1)} %get-tuple-element.38), channel_id=1, source_target_pairs={{0,252},{4,8},{8,4},{12,16},{16,12},{20,24},{24,20},{28,32},{32,28... | collective-permute-start | bytes 73736 | tf_op jit(solution)/shard_map/ppermute | solution.py:435
  47.9 4.2 %collective-permute-start.5 = (f32[48,128]{1,0:T(8,128)S(1)}, f32[48,128]{1,0:T(8,128)S(1)}, u32[]{:S(2)}, u32[]{:S(2)}) collective-permute-start(f32[48,128]{1,0:T(8,128)S(1)} %get-tuple-element.39), channel_id=1, source_target_pairs={{0,4},{4,0},{8,12},{12,8},{16,20},{20,16},{24,28},{28,24},{32,36},... | collective-permute-start | bytes 73736 | tf_op jit(solution)/shard_map/ppermute | solution.py:436
  52.1 3.8 %collective-permute-start.6 = (f32[80,128]{1,0:T(8,128)S(1)}, f32[80,128]{1,0:T(8,128)S(1)}, u32[]{:S(2)}, u32[]{:S(2)}) collective-permute-start(f32[80,128]{1,0:T(8,128)S(1)} %get-tuple-element.41), channel_id=1, source_target_pairs={{0,3},{1,2},{2,1},{3,0},{4,7},{5,6},{6,5},{7,4},{8,11},{9,10},{10,... | collective-permute-start | bytes 122888 | tf_op jit(solution)/shard_map/ppermute | solution.py:435
  54.2 1.7 %collective-permute-start.7 = (f32[80,128]{1,0:T(8,128)S(1)}, f32[80,128]{1,0:T(8,128)S(1)}, u32[]{:S(2)}, u32[]{:S(2)}) collective-permute-start(f32[80,128]{1,0:T(8,128)S(1)} %get-tuple-element.42), channel_id=1, source_target_pairs={{0,1},{1,0},{2,3},{3,2},{4,5},{5,4},{6,7},{7,6},{8,9},{9,8},{10,11... | collective-permute-start | bytes 122888 | tf_op jit(solution)/shard_map/ppermute | solution.py:436
  60.2 21.4 %all-to-all-start.1 = ((f32[256,1,128]{2,1,0:T(1,128)}), f32[256,1,128]{2,1,0:T(1,128)S(1)}, u32[]{:S(2)}, u32[]{:S(2)}) async-start(f32[256,1,128]{2,1,0:T(1,128)} %bitcast.21), calls=%async_computation.1 | async-start | bytes 262144 | tf_op jit(solution)/shard_map/all_to_all | solution.py:498
  68.0 12.1 %collective-permute-start.8 = (f32[48,128]{1,0:T(8,128)S(1)}, f32[48,128]{1,0:T(8,128)S(1)}, u32[]{:S(2)}, u32[]{:S(2)}) collective-permute-start(f32[48,128]{1,0:T(8,128)S(1)} %get-tuple-element.47), channel_id=1, source_target_pairs={{0,252},{4,8},{8,4},{12,16},{16,12},{20,24},{24,20},{28,32},{32,28... | collective-permute-start | bytes 73736 | tf_op jit(solution)/shard_map/ppermute | solution.py:435
  77.3 4.2 %collective-permute-start.9 = (f32[48,128]{1,0:T(8,128)S(1)}, f32[48,128]{1,0:T(8,128)S(1)}, u32[]{:S(2)}, u32[]{:S(2)}) collective-permute-start(f32[48,128]{1,0:T(8,128)S(1)} %get-tuple-element.48), channel_id=1, source_target_pairs={{0,4},{4,0},{8,12},{12,8},{16,20},{20,16},{24,28},{28,24},{32,36},... | collective-permute-start | bytes 73736 | tf_op jit(solution)/shard_map/ppermute | solution.py:436
  81.6 3.8 %collective-permute-start.10 = (f32[80,128]{1,0:T(8,128)S(1)}, f32[80,128]{1,0:T(8,128)S(1)}, u32[]{:S(2)}, u32[]{:S(2)}) collective-permute-start(f32[80,128]{1,0:T(8,128)S(1)} %get-tuple-element.50), channel_id=1, source_target_pairs={{0,3},{1,2},{2,1},{3,0},{4,7},{5,6},{6,5},{7,4},{8,11},{9,10},{10,... | collective-permute-start | bytes 122888 | tf_op jit(solution)/shard_map/ppermute | solution.py:435
  83.6 1.7 %collective-permute-start.11 = (f32[80,128]{1,0:T(8,128)S(1)}, f32[80,128]{1,0:T(8,128)S(1)}, u32[]{:S(2)}, u32[]{:S(2)}) collective-permute-start(f32[80,128]{1,0:T(8,128)S(1)} %get-tuple-element.51), channel_id=1, source_target_pairs={{0,1},{1,0},{2,3},{3,2},{4,5},{5,4},{6,7},{7,6},{8,9},{9,8},{10,11... | collective-permute-start | bytes 122888 | tf_op jit(solution)/shard_map/ppermute | solution.py:436
  89.6 21.2 %all-to-all-start.2 = ((f32[256,1,128]{2,1,0:T(1,128)}), f32[256,1,128]{2,1,0:T(1,128)S(1)}, u32[]{:S(2)}, u32[]{:S(2)}) async-start(f32[256,1,128]{2,1,0:T(1,128)} %bitcast.20), calls=%async_computation.2 | async-start | bytes 262144 | tf_op jit(solution)/shard_map/all_to_all | solution.py:498
  97.4 12.0 %collective-permute-start.12 = (f32[48,128]{1,0:T(8,128)S(1)}, f32[48,128]{1,0:T(8,128)S(1)}, u32[]{:S(2)}, u32[]{:S(2)}) collective-permute-start(f32[48,128]{1,0:T(8,128)S(1)} %get-tuple-element.54), channel_id=1, source_target_pairs={{0,252},{4,8},{8,4},{12,16},{16,12},{20,24},{24,20},{28,32},{32,28... | collective-permute-start | bytes 73736 | tf_op jit(solution)/shard_map/ppermute | solution.py:435
  106.6 4.2 %collective-permute-start.13 = (f32[48,128]{1,0:T(8,128)S(1)}, f32[48,128]{1,0:T(8,128)S(1)}, u32[]{:S(2)}, u32[]{:S(2)}) collective-permute-start(f32[48,128]{1,0:T(8,128)S(1)} %get-tuple-element.55), channel_id=1, source_target_pairs={{0,4},{4,0},{8,12},{12,8},{16,20},{20,16},{24,28},{28,24},{32,36},... | collective-permute-start | bytes 73736 | tf_op jit(solution)/shard_map/ppermute | solution.py:436
  110.8 3.8 %collective-permute-start.14 = (f32[80,128]{1,0:T(8,128)S(1)}, f32[80,128]{1,0:T(8,128)S(1)}, u32[]{:S(2)}, u32[]{:S(2)}) collective-permute-start(f32[80,128]{1,0:T(8,128)S(1)} %get-tuple-element.57), channel_id=1, source_target_pairs={{0,3},{1,2},{2,1},{3,0},{4,7},{5,6},{6,5},{7,4},{8,11},{9,10},{10,... | collective-permute-start | bytes 122888 | tf_op jit(solution)/shard_map/ppermute | solution.py:435
  112.9 1.7 %collective-permute-start.15 = (f32[80,128]{1,0:T(8,128)S(1)}, f32[80,128]{1,0:T(8,128)S(1)}, u32[]{:S(2)}, u32[]{:S(2)}) collective-permute-start(f32[80,128]{1,0:T(8,128)S(1)} %get-tuple-element.58), channel_id=1, source_target_pairs={{0,1},{1,0},{2,3},{3,2},{4,5},{5,4},{6,7},{7,6},{8,9},{9,8},{10,11... | collective-permute-start | bytes 122888 | tf_op jit(solution)/shard_map/ppermute | solution.py:436

commit v6 on v3

--- a/solution.py
+++ b/solution.py
@@ -1,11 +1,10 @@
-import functools
-
 import jax
 import jax.numpy as jnp
 from jax import lax
 from jax.experimental import pallas as pl
 from jax.experimental.pallas import tpu as pltpu
 from jax.sharding import PartitionSpec as P
+
 
 AGG_LOC = 32
 SWEEPS = 3
@@ -200,7 +199,7 @@
             staged[at : at + 3, :] = rows
 
 
-def solve_box(values, coef, agg, coarse, factors_hbm, payload, current, far, near, scratch):
+def solve_box(values, coef, agg, coarse, factors_hbm, payload, current, far, near, scratch, coarse_fetch=None):
     misfit, sums, spread, staged, one, two, factors, tile_sems, sem = scratch
     inside = box_mask()
     rolled = {}
@@ -211,6 +210,8 @@
         applied = operate_pair(values, coef, a, rolled)
         for c in range(3):
             misfit[c, a] = jnp.where(inside, coef[RHS + c, a - 1] - applied[c], 0.0)
+    if coarse_fetch is not None:
+        coarse_fetch.wait()
     coarse_part([misfit[0, a, 0:8] for a in range(2, 6)], agg, coarse, sums, spread, staged)
     write = pltpu.make_async_copy(staged, payload, sem)
     write.start()
@@ -236,7 +237,7 @@
     high,
     mine,
     agg,
-    coarse,
+    coarse_hbm,
     factors_hbm,
     coef,
     slots,
@@ -245,9 +246,13 @@
     far_out,
     near_out,
     rim,
+    coarse,
+    coarse_sem,
     values,
     *scratch,
 ):
+    coarse_fetch = pltpu.make_async_copy(coarse_hbm, coarse, coarse_sem)
+    coarse_fetch.start()
     for fetch in fetch_tiles(factors_hbm, scratch[-3], scratch[-2]):
         fetch.start()
     odd = is_odd("wide")
@@ -297,7 +302,7 @@
         for c in range(3):
             diagonal = jnp.where(inside, centre + coef[COUP + 4 * c, a - 1], 1.0)
             coef[INV + c, a - 1] = jnp.where(inside, 1.0 / diagonal, 0.0)
-    solve_box(values, coef, agg, coarse, factors_hbm, payload, current, far_out, near_out, scratch)
+    solve_box(values, coef, agg, coarse, factors_hbm, payload, current, far_out, near_out, scratch, coarse_fetch)
 
 
 def gather_values(current, far, near, low, high, part, slots, values):
@@ -379,7 +384,9 @@
             ref[c, 7] = blank
     for a in range(1, 7):
         edge = a in (1, 6)
-        fetches[a - 1].wait()
+        if a in (1, 4):
+            for fetch in fetches[a - 1 : a + 2]:
+                fetch.wait()
         for half, cols in ((0, own_cols), (1, [8, -1] if edge else [8, 9, -2, -1])):
             part = tiles([misfit[c, a, 8 * half : 8 * half + 8] for c in range(3)], a, cols, half)
             for c in range(3):
@@ -405,7 +412,7 @@
             moved[c, a - 2] = values[c, a, 0:8] + (two[c, a, 0:8] + part[c])
 
 
-def call(body, name, outs, scratch, operands, in_hbm=(), out_hbm=(), flops=1000000):
+def call(body, outs, scratch, operands, in_hbm=(), out_hbm=(), flops=1000000):
     vmem = pl.BlockSpec(memory_space=pltpu.VMEM)
     hbm = pl.BlockSpec(memory_space=pltpu.HBM)
     operands = [pltpu.with_memory_space_constraint(x, pltpu.HBM) if i in in_hbm else x for i, x in enumerate(operands)]
@@ -420,16 +427,13 @@
         scratch_shapes=scratch,
         compiler_params=pltpu.CompilerParams(vmem_limit_bytes=VMEM_LIMIT),
         cost_estimate=pl.CostEstimate(flops=flops, bytes_accessed=0, transcendentals=0),
-        name=name,
     )(*operands)
 
 
 def swaps(axis, far, near):
     count = lax.axis_size(axis)
-    with jax.named_scope(axis + "_far"):
-        far = lax.ppermute(far, axis, [(i, (i + (1 if i % 2 else -1)) % count) for i in range(count)])
-    with jax.named_scope(axis + "_near"):
-        near = lax.ppermute(near, axis, [(i, i ^ 1) for i in range(count)])
+    far = lax.ppermute(far, axis, [(i, (i + (1 if i % 2 else -1)) % count) for i in range(count)])
+    near = lax.ppermute(near, axis, [(i, i ^ 1) for i in range(count)])
     return far, near
 
 
@@ -460,7 +464,6 @@
 
     mine, agg, far, near = call(
         add_wells_and_pack,
-        "pack_wide",
         [((FULL + THIN, 4, 8, LANES), f32), ((4, 8, LANES), f32)] + [((WIDE_ROWS, LANES), f32)] * 2,
         [
             pltpu.VMEM((1, 64), jnp.int32),
@@ -482,15 +485,14 @@
         in_hbm=range(8),
     )
     far, near = swaps("wide", far, near)
-    low, high = call(pack_narrow, "pack_narrow", [((NARROW_ROWS, LANES), f32)] * 2, [], [far, near, mine])
+    low, high = call(pack_narrow, [((NARROW_ROWS, LANES), f32)] * 2, [], [far, near, mine])
     low, high = swaps("narrow", low, high)
     coef, slots, payload, current, far, near = call(
         first_sweep,
-        "first_sweep",
         [((N_COEF, 6, ROWS, LANES), f32), ((PAIRS, ROWS, LANES), jnp.int32), payload_type, own, wide_type, wide_type],
-        [pltpu.VMEM((4, PAIRS, ROWS, LANES), f32)] + scratch,
+        [pltpu.VMEM((4, PAIRS, ROWS, LANES), f32), pltpu.VMEM(coarse_inverse.shape, f32), dma] + scratch,
         [far, near, low, high, mine, agg, coarse_inverse, tile_factors],
-        in_hbm=(7,),
+        in_hbm=(6, 7),
         out_hbm=(2,),
     )
     for sweep in range(SWEEPS):
@@ -498,18 +500,13 @@
         received = lax.all_to_all(blocks, ("wide", "narrow"), 0, 0, axis_index_groups=groups).reshape(payload_type[0])
         far, near = swaps("wide", far, near)
         low, high, part = call(
-            pack_current,
-            "pack_current",
-            [narrow_type, ((80, LANES), f32), ((8, LANES), f32)],
-            [],
-            [current, far, near, received],
+            pack_current, [narrow_type, ((80, LANES), f32), ((8, LANES), f32)], [], [current, far, near, received]
         )
         low, high = swaps("narrow", low, high)
         known = [current, far, near, low, high, part, slots, coef]
         if sweep < SWEEPS - 1:
             payload, current, far, near = call(
                 next_sweep,
-                "next_sweep",
                 [payload_type, own, wide_type, wide_type],
                 scratch,
                 known + [agg, coarse_inverse, tile_factors],
@@ -517,7 +514,7 @@
                 out_hbm=(0,),
             )
         else:
-            iterate, residual = call(last_misfit, "last_misfit", [own, own], [pltpu.VMEM(box, f32)], known)
+            iterate, residual = call(last_misfit, [own, own], [pltpu.VMEM(box, f32)], known)
     return iterate, residual
 
 

time: 118 us -> 116 us (0.983)
  local copies, waits for them, and re-layouts: 1.23 us -> 0.01 us
    unnamed x4 -> x2, local copies, waits for them, and re-layouts: 1.23 us -> 0.01 us
where the time goes in v6:
time: 116 us
  starting transfers between devices  66.3 us (57%)
  waiting for transfers between devices  33.4 us (29%)
  Pallas kernels  15.7 us (14%)
    ppermute x8, starting transfers between devices, swaps(): lax.ppermute(far, axis, [(i, (i + (1 if i % 2 else -1)) % count) for i in...  36.2 us
    ppermute x8, waiting for transfers between devices, swaps(): lax.ppermute(far, axis, [(i, (i + (1 if i % 2 else -1)) % count) for i in...  25.4 us
    all_to_all x3, starting transfers between devices, per_device(): lax.all_to_all(blocks, ('wide', 'narrow'), 0, 0, axis_index_groups=groups)  22.4 us
    pallas_call x9, Pallas kernels, call(): pl.pallas_call(body, out_shape=[pltpu.HBM(shape, dtype) if i in out_hbm e...  15.7 us
    ppermute x8, starting transfers between devices, swaps(): near = lax.ppermute(near, axis, [(i, i ^ 1) for i in range(count)])  7.67 us
    ppermute x8, waiting for transfers between devices, swaps(): near = lax.ppermute(near, axis, [(i, i ^ 1) for i in range(count)])  6.58 us
  transfers between devices with their start and end apart: 19, of which 15 were waited for; matrix products, arithmetic and copies ran while one was open for 0% of the time, Pallas kernels for 0%

profile of v6, /device:TPU:1, one launch (start us, length us, event | category | flops | bytes accessed | tf_op | source)
XLA Modules:
  0.0 116.1 jit_solution(3103404409076354306)
XLA Ops:
  1.8 11.4 %collective-permute-start = (f32[216,128]{1,0:T(8,128)S(1)}, f32[216,128]{1,0:T(8,128)S(1)}, u32[]{:S(2)}, u32[]{:S(2)}) collective-permute-start(f32[216,128]{1,0:T(8,128)S(1)} %get-tuple-element.31), channel_id=1, source_target_pairs={{0,252},{4,8},{8,4},{12,16},{16,12},{20,24},{24,20},{28,32},{32,28... | collective-permute-start | bytes 331784 | tf_op jit(solution)/shard_map/ppermute | solution.py:435
  13.2 2.8 %collective-permute-done.far = f32[216,128]{1,0:T(8,128)S(1)} collective-permute-done((f32[216,128]{1,0:T(8,128)S(1)}, f32[216,128]{1,0:T(8,128)S(1)}, u32[]{:S(2)}, u32[]{:S(2)}) %collective-permute-start) | collective-permute-done | bytes 110624 | tf_op jit(solution)/shard_map/ppermute | solution.py:435
  15.9 2.3 %collective-permute-done.1.near = f32[216,128]{1,0:T(8,128)S(1)} collective-permute-done((f32[216,128]{1,0:T(8,128)S(1)}, f32[216,128]{1,0:T(8,128)S(1)}, u32[]{:S(2)}, u32[]{:S(2)}) %collective-permute-start.1) | collective-permute-done | bytes 110624 | tf_op jit(solution)/shard_map/ppermute | solution.py:436
  18.4 2.4 %collective-permute-start.2 = (f32[324,128]{1,0:T(8,128)S(1)}, f32[324,128]{1,0:T(8,128)S(1)}, u32[]{:S(2)}, u32[]{:S(2)}) collective-permute-start(f32[324,128]{1,0:T(8,128)S(1)} %get-tuple-element.34), channel_id=1, source_target_pairs={{0,3},{1,2},{2,1},{3,0},{4,7},{5,6},{6,5},{7,4},{8,11},{9,10},{10,... | collective-permute-start | bytes 497672 | tf_op jit(solution)/shard_map/ppermute | solution.py:435
  20.8 4.3 %collective-permute-done.2.low = f32[324,128]{1,0:T(8,128)S(1)} collective-permute-done((f32[324,128]{1,0:T(8,128)S(1)}, f32[324,128]{1,0:T(8,128)S(1)}, u32[]{:S(2)}, u32[]{:S(2)}) %collective-permute-start.2) | collective-permute-done | bytes 165920 | tf_op jit(solution)/shard_map/ppermute | solution.py:435
  25.0 5.1 %shard_map.115 = (f32[22,6,16,128]{3,2,1,0:T(8,128)S(1)}, s32[8,16,128]{2,1,0:T(8,128)S(1)}, f32[384,128]{1,0:T(8,128)}, f32[3,4,8,128]{3,2,1,0:T(8,128)S(1)}, f...) custom-call(f32[216,128]{1,0:T(8,128)S(1)} %collective-permute-done.far, f32[216,128]{1,0:T(8,128)S(1)} %collective-permute-done.1.near, ...), custom_call_target="tpu_custom_call" | custom-call | flops 1000000 | tf_op jit(solution)/shard_map/pallas_call | solution.py:419
  30.1 9.5 %all-to-all-start = ((f32[128,1,384]{2,1,0:T(1,128)}), f32[128,1,384]{2,1,0:T(1,128)S(1)}, u32[]{:S(2)}, u32[]{:S(2)}) async-start(f32[128,1,384]{2,1,0:T(1,128)} %bitcast.12), calls=%async_computation | async-start | bytes 393216 | tf_op jit(solution)/shard_map/all_to_all | solution.py:500
  39.6 7.1 %collective-permute-start.4 = (f32[48,128]{1,0:T(8,128)S(1)}, f32[48,128]{1,0:T(8,128)S(1)}, u32[]{:S(2)}, u32[]{:S(2)}) collective-permute-start(f32[48,128]{1,0:T(8,128)S(1)} %get-tuple-element.38), channel_id=1, source_target_pairs={{0,252},{4,8},{8,4},{12,16},{16,12},{20,24},{24,20},{28,32},{32,28... | collective-permute-start | bytes 73736 | tf_op jit(solution)/shard_map/ppermute | solution.py:435
  46.8 2.9 %collective-permute-done.4.far = f32[48,128]{1,0:T(8,128)S(1)} collective-permute-done((f32[48,128]{1,0:T(8,128)S(1)}, f32[48,128]{1,0:T(8,128)S(1)}, u32[]{:S(2)}, u32[]{:S(2)}) %collective-permute-start.4) | collective-permute-done | bytes 24608 | tf_op jit(solution)/shard_map/ppermute | solution.py:435
  49.7 1.6 %collective-permute-done.5.near = f32[48,128]{1,0:T(8,128)S(1)} collective-permute-done((f32[48,128]{1,0:T(8,128)S(1)}, f32[48,128]{1,0:T(8,128)S(1)}, u32[]{:S(2)}, u32[]{:S(2)}) %collective-permute-start.5) | collective-permute-done | bytes 24608 | tf_op jit(solution)/shard_map/ppermute | solution.py:436
  51.5 2.9 %collective-permute-start.7 = (f32[80,128]{1,0:T(8,128)S(1)}, f32[80,128]{1,0:T(8,128)S(1)}, u32[]{:S(2)}, u32[]{:S(2)}) collective-permute-start(f32[80,128]{1,0:T(8,128)S(1)} %get-tuple-element.42), channel_id=1, source_target_pairs={{0,1},{1,0},{2,3},{3,2},{4,5},{5,4},{6,7},{7,6},{8,9},{9,8},{10,11... | collective-permute-start | bytes 122888 | tf_op jit(solution)/shard_map/ppermute | solution.py:436
  54.7 3.1 %collective-permute-done.6.low = f32[72,128]{1,0:T(8,128)S(1)} collective-permute-done((f32[72,128]{1,0:T(8,128)S(1)}, f32[72,128]{1,0:T(8,128)S(1)}, u32[]{:S(2)}, u32[]{:S(2)}) %collective-permute-start.6) | collective-permute-done | bytes 36896 | tf_op jit(solution)/shard_map/ppermute | solution.py:435
  57.8 4.3 %shard_map.117 = (f32[384,128]{1,0:T(8,128)}, f32[3,4,8,128]{3,2,1,0:T(8,128)S(1)}, f32[48,128]{1,0:T(8,128)S(1)}, f32[48,128]{1,0:T(8,128)S(1)}) custom-call(f32[3,4,8,128]{3,2,1,0:T(8,128)S(1)} %get-tuple-element.37.current, f32[48,128]{1,0:T(8,128)S(1)} %collective-permute-done.4.far, f32[48,128]{1,0:T(8,128)S(1)} %collective-permute-done.5.near, ...), custom_call_target="tpu_custom_call" | custom-call | flops 1000000 | tf_op jit(solution)/shard_map/pallas_call | solution.py:419
  62.1 6.6 %all-to-all-start.1 = ((f32[128,1,384]{2,1,0:T(1,128)}), f32[128,1,384]{2,1,0:T(1,128)S(1)}, u32[]{:S(2)}, u32[]{:S(2)}) async-start(f32[128,1,384]{2,1,0:T(1,128)} %bitcast.14), calls=%async_computation.1 | async-start | bytes 393216 | tf_op jit(solution)/shard_map/all_to_all | solution.py:500
  68.6 7.1 %collective-permute-start.8 = (f32[48,128]{1,0:T(8,128)S(1)}, f32[48,128]{1,0:T(8,128)S(1)}, u32[]{:S(2)}, u32[]{:S(2)}) collective-permute-start(f32[48,128]{1,0:T(8,128)S(1)} %get-tuple-element.47), channel_id=1, source_target_pairs={{0,252},{4,8},{8,4},{12,16},{16,12},{20,24},{24,20},{28,32},{32,28... | collective-permute-start | bytes 73736 | tf_op jit(solution)/shard_map/ppermute | solution.py:435
  75.8 3.2 %collective-permute-done.8.far = f32[48,128]{1,0:T(8,128)S(1)} collective-permute-done((f32[48,128]{1,0:T(8,128)S(1)}, f32[48,128]{1,0:T(8,128)S(1)}, u32[]{:S(2)}, u32[]{:S(2)}) %collective-permute-start.8) | collective-permute-done | bytes 24608 | tf_op jit(solution)/shard_map/ppermute | solution.py:435
  80.9 2.4 %collective-permute-start.11 = (f32[80,128]{1,0:T(8,128)S(1)}, f32[80,128]{1,0:T(8,128)S(1)}, u32[]{:S(2)}, u32[]{:S(2)}) collective-permute-start(f32[80,128]{1,0:T(8,128)S(1)} %get-tuple-element.51), channel_id=1, source_target_pairs={{0,1},{1,0},{2,3},{3,2},{4,5},{5,4},{6,7},{7,6},{8,9},{9,8},{10,11... | collective-permute-start | bytes 122888 | tf_op jit(solution)/shard_map/ppermute | solution.py:436
  83.6 3.0 %collective-permute-done.10.low = f32[72,128]{1,0:T(8,128)S(1)} collective-permute-done((f32[72,128]{1,0:T(8,128)S(1)}, f32[72,128]{1,0:T(8,128)S(1)}, u32[]{:S(2)}, u32[]{:S(2)}) %collective-permute-start.10) | collective-permute-done | bytes 36896 | tf_op jit(solution)/shard_map/ppermute | solution.py:435
  86.6 4.3 %shard_map.119 = (f32[384,128]{1,0:T(8,128)}, f32[3,4,8,128]{3,2,1,0:T(8,128)S(1)}, f32[48,128]{1,0:T(8,128)S(1)}, f32[48,128]{1,0:T(8,128)S(1)}) custom-call(f32[3,4,8,128]{3,2,1,0:T(8,128)S(1)} %get-tuple-element.46.current, f32[48,128]{1,0:T(8,128)S(1)} %collective-permute-done.8.far, f32[48,128]{1,0:T(8,128)S(1)} %collective-permute-done.9.near, ...), custom_call_target="tpu_custom_call" | custom-call | flops 1000000 | tf_op jit(solution)/shard_map/pallas_call | solution.py:419
  90.9 6.4 %all-to-all-start.2 = ((f32[128,1,384]{2,1,0:T(1,128)}), f32[128,1,384]{2,1,0:T(1,128)S(1)}, u32[]{:S(2)}, u32[]{:S(2)}) async-start(f32[128,1,384]{2,1,0:T(1,128)} %bitcast.13), calls=%async_computation.2 | async-start | bytes 393216 | tf_op jit(solution)/shard_map/all_to_all | solution.py:500
  97.3 7.1 %collective-permute-start.12 = (f32[48,128]{1,0:T(8,128)S(1)}, f32[48,128]{1,0:T(8,128)S(1)}, u32[]{:S(2)}, u32[]{:S(2)}) collective-permute-start(f32[48,128]{1,0:T(8,128)S(1)} %get-tuple-element.54), channel_id=1, source_target_pairs={{0,252},{4,8},{8,4},{12,16},{16,12},{20,24},{24,20},{28,32},{32,28... | collective-permute-start | bytes 73736 | tf_op jit(solution)/shard_map/ppermute | solution.py:435
  104.4 3.2 %collective-permute-done.12.far = f32[48,128]{1,0:T(8,128)S(1)} collective-permute-done((f32[48,128]{1,0:T(8,128)S(1)}, f32[48,128]{1,0:T(8,128)S(1)}, u32[]{:S(2)}, u32[]{:S(2)}) %collective-permute-start.12) | collective-permute-done | bytes 24608 | tf_op jit(solution)/shard_map/ppermute | solution.py:435
  109.5 2.4 %collective-permute-start.15 = (f32[80,128]{1,0:T(8,128)S(1)}, f32[80,128]{1,0:T(8,128)S(1)}, u32[]{:S(2)}, u32[]{:S(2)}) collective-permute-start(f32[80,128]{1,0:T(8,128)S(1)} %get-tuple-element.58), channel_id=1, source_target_pairs={{0,1},{1,0},{2,3},{3,2},{4,5},{5,4},{6,7},{7,6},{8,9},{9,8},{10,11... | collective-permute-start | bytes 122888 | tf_op jit(solution)/shard_map/ppermute | solution.py:436
  112.3 3.0 %collective-permute-done.14.low = f32[72,128]{1,0:T(8,128)S(1)} collective-permute-done((f32[72,128]{1,0:T(8,128)S(1)}, f32[72,128]{1,0:T(8,128)S(1)}, u32[]{:S(2)}, u32[]{:S(2)}) %collective-permute-start.14) | collective-permute-done | bytes 36896 | tf_op jit(solution)/shard_map/ppermute | solution.py:435
  (25 shorter events, 7.2 us)
Async XLA Ops:
  1.8 14.2 %collective-permute-start = (f32[216,128]{1,0:T(8,128)S(1)}, f32[216,128]{1,0:T(8,128)S(1)}, u32[]{:S(2)}, u32[]{:S(2)}) collective-permute-start(f32[216,128]{1,0:T(8,128)S(1)} %get-tuple-element.31), channel_id=1, source_target_pairs={{0,252},{4,8},{8,4},{12,16},{16,12},{20,24},{24,20},{28,32},{32,28... | collective-permute-start | bytes 331784 | tf_op jit(solution)/shard_map/ppermute | solution.py:435
  13.2 5.1 %collective-permute-start.1 = (f32[216,128]{1,0:T(8,128)S(1)}, f32[216,128]{1,0:T(8,128)S(1)}, u32[]{:S(2)}, u32[]{:S(2)}) collective-permute-start(f32[216,128]{1,0:T(8,128)S(1)} %get-tuple-element.32), channel_id=1, source_target_pairs={{0,4},{4,0},{8,12},{12,8},{16,20},{20,16},{24,28},{28,24},{32,36},... | collective-permute-start | bytes 331784 | tf_op jit(solution)/shard_map/ppermute | solution.py:436
  18.4 6.7 %collective-permute-start.2 = (f32[324,128]{1,0:T(8,128)S(1)}, f32[324,128]{1,0:T(8,128)S(1)}, u32[]{:S(2)}, u32[]{:S(2)}) collective-permute-start(f32[324,128]{1,0:T(8,128)S(1)} %get-tuple-element.34), channel_id=1, source_target_pairs={{0,3},{1,2},{2,1},{3,0},{4,7},{5,6},{6,5},{7,4},{8,11},{9,10},{10,... | collective-permute-start | bytes 497672 | tf_op jit(solution)/shard_map/ppermute | solution.py:435
  20.7 4.3 %collective-permute-start.3 = (f32[324,128]{1,0:T(8,128)S(1)}, f32[324,128]{1,0:T(8,128)S(1)}, u32[]{:S(2)}, u32[]{:S(2)}) collective-permute-start(f32[324,128]{1,0:T(8,128)S(1)} %get-tuple-element.35), channel_id=1, source_target_pairs={{0,1},{1,0},{2,3},{3,2},{4,5},{5,4},{6,7},{7,6},{8,9},{9,8},{10,11... | collective-permute-start | bytes 497672 | tf_op jit(solution)/shard_map/ppermute | solution.py:436
  25.0 32.7 %copy-start = (f32[32,8192]{1,0:T(8,128)S(1)}, f32[32,8192]{1,0:T(8,128)}, u32[]{:S(2)}) copy-start(f32[32,8192]{1,0:T(8,128)} %coarse.3) | copy-start | bytes 3145732
  30.1 21.4 %all-to-all-start = ((f32[128,1,384]{2,1,0:T(1,128)}), f32[128,1,384]{2,1,0:T(1,128)S(1)}, u32[]{:S(2)}, u32[]{:S(2)}) async-start(f32[128,1,384]{2,1,0:T(1,128)} %bitcast.12), calls=%async_computation | async-start | bytes 393216 | tf_op jit(solution)/shard_map/all_to_all | solution.py:500
  39.6 10.0 %collective-permute-start.4 = (f32[48,128]{1,0:T(8,128)S(1)}, f32[48,128]{1,0:T(8,128)S(1)}, u32[]{:S(2)}, u32[]{:S(2)}) collective-permute-start(f32[48,128]{1,0:T(8,128)S(1)} %get-tuple-element.38), channel_id=1, source_target_pairs={{0,252},{4,8},{8,4},{12,16},{16,12},{20,24},{24,20},{28,32},{32,28... | collective-permute-start | bytes 73736 | tf_op jit(solution)/shard_map/ppermute | solution.py:435
  46.8 4.5 %collective-permute-start.5 = (f32[48,128]{1,0:T(8,128)S(1)}, f32[48,128]{1,0:T(8,128)S(1)}, u32[]{:S(2)}, u32[]{:S(2)}) collective-permute-start(f32[48,128]{1,0:T(8,128)S(1)} %get-tuple-element.39), channel_id=1, source_target_pairs={{0,4},{4,0},{8,12},{12,8},{16,20},{20,16},{24,28},{28,24},{32,36},... | collective-permute-start | bytes 73736 | tf_op jit(solution)/shard_map/ppermute | solution.py:436
  51.5 6.2 %collective-permute-start.7 = (f32[80,128]{1,0:T(8,128)S(1)}, f32[80,128]{1,0:T(8,128)S(1)}, u32[]{:S(2)}, u32[]{:S(2)}) collective-permute-start(f32[80,128]{1,0:T(8,128)S(1)} %get-tuple-element.42), channel_id=1, source_target_pairs={{0,1},{1,0},{2,3},{3,2},{4,5},{5,4},{6,7},{7,6},{8,9},{9,8},{10,11... | collective-permute-start | bytes 122888 | tf_op jit(solution)/shard_map/ppermute | solution.py:436
  54.4 3.4 %collective-permute-start.6 = (f32[72,128]{1,0:T(8,128)S(1)}, f32[72,128]{1,0:T(8,128)S(1)}, u32[]{:S(2)}, u32[]{:S(2)}) collective-permute-start(f32[72,128]{1,0:T(8,128)S(1)} %get-tuple-element.41), channel_id=1, source_target_pairs={{0,3},{1,2},{2,1},{3,0},{4,7},{5,6},{6,5},{7,4},{8,11},{9,10},{10,... | collective-permute-start | bytes 110600 | tf_op jit(solution)/shard_map/ppermute | solution.py:435
  62.1 18.8 %all-to-all-start.1 = ((f32[128,1,384]{2,1,0:T(1,128)}), f32[128,1,384]{2,1,0:T(1,128)S(1)}, u32[]{:S(2)}, u32[]{:S(2)}) async-start(f32[128,1,384]{2,1,0:T(1,128)} %bitcast.14), calls=%async_computation.1 | async-start | bytes 393216 | tf_op jit(solution)/shard_map/all_to_all | solution.py:500
  68.6 10.3 %collective-permute-start.8 = (f32[48,128]{1,0:T(8,128)S(1)}, f32[48,128]{1,0:T(8,128)S(1)}, u32[]{:S(2)}, u32[]{:S(2)}) collective-permute-start(f32[48,128]{1,0:T(8,128)S(1)} %get-tuple-element.47), channel_id=1, source_target_pairs={{0,252},{4,8},{8,4},{12,16},{16,12},{20,24},{24,20},{28,32},{32,28... | collective-permute-start | bytes 73736 | tf_op jit(solution)/shard_map/ppermute | solution.py:435
  75.7 4.5 %collective-permute-start.9 = (f32[48,128]{1,0:T(8,128)S(1)}, f32[48,128]{1,0:T(8,128)S(1)}, u32[]{:S(2)}, u32[]{:S(2)}) collective-permute-start(f32[48,128]{1,0:T(8,128)S(1)} %get-tuple-element.48), channel_id=1, source_target_pairs={{0,4},{4,0},{8,12},{12,8},{16,20},{20,16},{24,28},{28,24},{32,36},... | collective-permute-start | bytes 73736 | tf_op jit(solution)/shard_map/ppermute | solution.py:436
  80.9 5.8 %collective-permute-start.11 = (f32[80,128]{1,0:T(8,128)S(1)}, f32[80,128]{1,0:T(8,128)S(1)}, u32[]{:S(2)}, u32[]{:S(2)}) collective-permute-start(f32[80,128]{1,0:T(8,128)S(1)} %get-tuple-element.51), channel_id=1, source_target_pairs={{0,1},{1,0},{2,3},{3,2},{4,5},{5,4},{6,7},{7,6},{8,9},{9,8},{10,11... | collective-permute-start | bytes 122888 | tf_op jit(solution)/shard_map/ppermute | solution.py:436
  83.3 3.4 %collective-permute-start.10 = (f32[72,128]{1,0:T(8,128)S(1)}, f32[72,128]{1,0:T(8,128)S(1)}, u32[]{:S(2)}, u32[]{:S(2)}) collective-permute-start(f32[72,128]{1,0:T(8,128)S(1)} %get-tuple-element.50), channel_id=1, source_target_pairs={{0,3},{1,2},{2,1},{3,0},{4,7},{5,6},{6,5},{7,4},{8,11},{9,10},{10,... | collective-permute-start | bytes 110600 | tf_op jit(solution)/shard_map/ppermute | solution.py:435
  90.9 18.6 %all-to-all-start.2 = ((f32[128,1,384]{2,1,0:T(1,128)}), f32[128,1,384]{2,1,0:T(1,128)S(1)}, u32[]{:S(2)}, u32[]{:S(2)}) async-start(f32[128,1,384]{2,1,0:T(1,128)} %bitcast.13), calls=%async_computation.2 | async-start | bytes 393216 | tf_op jit(solution)/shard_map/all_to_all | solution.py:500
  97.3 10.3 %collective-permute-start.12 = (f32[48,128]{1,0:T(8,128)S(1)}, f32[48,128]{1,0:T(8,128)S(1)}, u32[]{:S(2)}, u32[]{:S(2)}) collective-permute-start(f32[48,128]{1,0:T(8,128)S(1)} %get-tuple-element.54), channel_id=1, source_target_pairs={{0,252},{4,8},{8,4},{12,16},{16,12},{20,24},{24,20},{28,32},{32,28... | collective-permute-start | bytes 73736 | tf_op jit(solution)/shard_map/ppermute | solution.py:435
  104.4 4.5 %collective-permute-start.13 = (f32[48,128]{1,0:T(8,128)S(1)}, f32[48,128]{1,0:T(8,128)S(1)}, u32[]{:S(2)}, u32[]{:S(2)}) collective-permute-start(f32[48,128]{1,0:T(8,128)S(1)} %get-tuple-element.55), channel_id=1, source_target_pairs={{0,4},{4,0},{8,12},{12,8},{16,20},{20,16},{24,28},{28,24},{32,36},... | collective-permute-start | bytes 73736 | tf_op jit(solution)/shard_map/ppermute | solution.py:436
  109.5 5.8 %collective-permute-start.15 = (f32[80,128]{1,0:T(8,128)S(1)}, f32[80,128]{1,0:T(8,128)S(1)}, u32[]{:S(2)}, u32[]{:S(2)}) collective-permute-start(f32[80,128]{1,0:T(8,128)S(1)} %get-tuple-element.58), channel_id=1, source_target_pairs={{0,1},{1,0},{2,3},{3,2},{4,5},{5,4},{6,7},{7,6},{8,9},{9,8},{10,11... | collective-permute-start | bytes 122888 | tf_op jit(solution)/shard_map/ppermute | solution.py:436
  111.9 3.4 %collective-permute-start.14 = (f32[72,128]{1,0:T(8,128)S(1)}, f32[72,128]{1,0:T(8,128)S(1)}, u32[]{:S(2)}, u32[]{:S(2)}) collective-permute-start(f32[72,128]{1,0:T(8,128)S(1)} %get-tuple-element.57), channel_id=1, source_target_pairs={{0,3},{1,2},{2,1},{3,0},{4,7},{5,6},{6,5},{7,4},{8,11},{9,10},{10,... | collective-permute-start | bytes 110600 | tf_op jit(solution)/shard_map/ppermute | solution.py:435

commit v7 on v6

--- a/solution.py
+++ b/solution.py
@@ -210,12 +210,15 @@
         applied = operate_pair(values, coef, a, rolled)
         for c in range(3):
             misfit[c, a] = jnp.where(inside, coef[RHS + c, a - 1] - applied[c], 0.0)
+    write = pltpu.make_async_copy(staged, payload, sem)
+
+    def coarse_stretch():
+        coarse_part([misfit[0, a, 0:8] for a in range(2, 6)], agg, coarse, sums, spread, staged)
+        write.start()
+
     if coarse_fetch is not None:
         coarse_fetch.wait()
-    coarse_part([misfit[0, a, 0:8] for a in range(2, 6)], agg, coarse, sums, spread, staged)
-    write = pltpu.make_async_copy(staged, payload, sem)
-    write.start()
-    local_solve(misfit, coef, values, factors_hbm, factors, tile_sems, current, one, two)
+    local_solve(misfit, coef, values, factors_hbm, factors, tile_sems, current, one, two, coarse_stretch)
     odd = is_odd("wide")
     for c in range(3):
         for p in range(2):
@@ -361,7 +364,7 @@
             residual[c, a - 2] = (coef[RHS + c, a - 1] - applied[c])[0:8]
 
 
-def local_solve(misfit, coef, values, factors_hbm, factors, sems, moved, one, two):
+def local_solve(misfit, coef, values, factors_hbm, factors, sems, moved, one, two, beside):
     fetches = fetch_tiles(factors_hbm, factors, sems)
     own_cols = list(range(8))
     row8 = lax.broadcasted_iota(jnp.int32, (24, LANES), 0) % 8
@@ -391,6 +394,8 @@
             part = tiles([misfit[c, a, 8 * half : 8 * half + 8] for c in range(3)], a, cols, half)
             for c in range(3):
                 one[c, a, 8 * half : 8 * half + 8] = part[c]
+        if a == 3:
+            beside()
     rolled = {}
     for a in range(1, 7):
         edge = a in (1, 6)

time: 116 us -> 116 us (level)
  no operation moved by 1% of the time
where the time goes in v7:
time: 116 us
  starting transfers between devices  66.3 us (57%)
  waiting for transfers between devices  33.4 us (29%)
  Pallas kernels  15.7 us (14%)
    ppermute x8, starting transfers between devices, swaps(): lax.ppermute(far, axis, [(i, (i + (1 if i % 2 else -1)) % count) for i in...  36.2 us
    ppermute x8, waiting for transfers between devices, swaps(): lax.ppermute(far, axis, [(i, (i + (1 if i % 2 else -1)) % count) for i in...  25.4 us
    all_to_all x3, starting transfers between devices, per_device(): lax.all_to_all(blocks, ('wide', 'narrow'), 0, 0, axis_index_groups=groups)  22.4 us
    pallas_call x9, Pallas kernels, call(): pl.pallas_call(body, out_shape=[pltpu.HBM(shape, dtype) if i in out_hbm e...  15.7 us
    ppermute x8, starting transfers between devices, swaps(): near = lax.ppermute(near, axis, [(i, i ^ 1) for i in range(count)])  7.67 us
    ppermute x8, waiting for transfers between devices, swaps(): near = lax.ppermute(near, axis, [(i, i ^ 1) for i in range(count)])  6.58 us
  transfers between devices with their start and end apart: 19, of which 15 were waited for; matrix products, arithmetic and copies ran while one was open for 0% of the time, Pallas kernels for 0%

profile of v7, /device:TPU:1, one launch (start us, length us, event | category | flops | bytes accessed | tf_op | source)
XLA Modules:
  0.0 116.1 jit_solution(2961336510453034507)
XLA Ops:
  1.8 11.4 %collective-permute-start = (f32[216,128]{1,0:T(8,128)S(1)}, f32[216,128]{1,0:T(8,128)S(1)}, u32[]{:S(2)}, u32[]{:S(2)}) collective-permute-start(f32[216,128]{1,0:T(8,128)S(1)} %get-tuple-element.31), channel_id=1, source_target_pairs={{0,252},{4,8},{8,4},{12,16},{16,12},{20,24},{24,20},{28,32},{32,28... | collective-permute-start | bytes 331784 | tf_op jit(solution)/shard_map/ppermute | solution.py:440
  13.2 2.8 %collective-permute-done.far = f32[216,128]{1,0:T(8,128)S(1)} collective-permute-done((f32[216,128]{1,0:T(8,128)S(1)}, f32[216,128]{1,0:T(8,128)S(1)}, u32[]{:S(2)}, u32[]{:S(2)}) %collective-permute-start) | collective-permute-done | bytes 110624 | tf_op jit(solution)/shard_map/ppermute | solution.py:440
  15.9 2.3 %collective-permute-done.1.near = f32[216,128]{1,0:T(8,128)S(1)} collective-permute-done((f32[216,128]{1,0:T(8,128)S(1)}, f32[216,128]{1,0:T(8,128)S(1)}, u32[]{:S(2)}, u32[]{:S(2)}) %collective-permute-start.1) | collective-permute-done | bytes 110624 | tf_op jit(solution)/shard_map/ppermute | solution.py:441
  18.4 2.4 %collective-permute-start.2 = (f32[324,128]{1,0:T(8,128)S(1)}, f32[324,128]{1,0:T(8,128)S(1)}, u32[]{:S(2)}, u32[]{:S(2)}) collective-permute-start(f32[324,128]{1,0:T(8,128)S(1)} %get-tuple-element.34), channel_id=1, source_target_pairs={{0,3},{1,2},{2,1},{3,0},{4,7},{5,6},{6,5},{7,4},{8,11},{9,10},{10,... | collective-permute-start | bytes 497672 | tf_op jit(solution)/shard_map/ppermute | solution.py:440
  20.8 4.3 %collective-permute-done.2.low = f32[324,128]{1,0:T(8,128)S(1)} collective-permute-done((f32[324,128]{1,0:T(8,128)S(1)}, f32[324,128]{1,0:T(8,128)S(1)}, u32[]{:S(2)}, u32[]{:S(2)}) %collective-permute-start.2) | collective-permute-done | bytes 165920 | tf_op jit(solution)/shard_map/ppermute | solution.py:440
  25.0 4.9 %shard_map.115 = (f32[22,6,16,128]{3,2,1,0:T(8,128)S(1)}, s32[8,16,128]{2,1,0:T(8,128)S(1)}, f32[384,128]{1,0:T(8,128)}, f32[3,4,8,128]{3,2,1,0:T(8,128)S(1)}, f...) custom-call(f32[216,128]{1,0:T(8,128)S(1)} %collective-permute-done.far, f32[216,128]{1,0:T(8,128)S(1)} %collective-permute-done.1.near, ...), custom_call_target="tpu_custom_call" | custom-call | flops 1000000 | tf_op jit(solution)/shard_map/pallas_call | solution.py:424
  29.9 9.5 %all-to-all-start = ((f32[128,1,384]{2,1,0:T(1,128)}), f32[128,1,384]{2,1,0:T(1,128)S(1)}, u32[]{:S(2)}, u32[]{:S(2)}) async-start(f32[128,1,384]{2,1,0:T(1,128)} %bitcast.12), calls=%async_computation | async-start | bytes 393216 | tf_op jit(solution)/shard_map/all_to_all | solution.py:505
  39.5 7.1 %collective-permute-start.4 = (f32[48,128]{1,0:T(8,128)S(1)}, f32[48,128]{1,0:T(8,128)S(1)}, u32[]{:S(2)}, u32[]{:S(2)}) collective-permute-start(f32[48,128]{1,0:T(8,128)S(1)} %get-tuple-element.38), channel_id=1, source_target_pairs={{0,252},{4,8},{8,4},{12,16},{16,12},{20,24},{24,20},{28,32},{32,28... | collective-permute-start | bytes 73736 | tf_op jit(solution)/shard_map/ppermute | solution.py:440
  46.6 2.9 %collective-permute-done.4.far = f32[48,128]{1,0:T(8,128)S(1)} collective-permute-done((f32[48,128]{1,0:T(8,128)S(1)}, f32[48,128]{1,0:T(8,128)S(1)}, u32[]{:S(2)}, u32[]{:S(2)}) %collective-permute-start.4) | collective-permute-done | bytes 24608 | tf_op jit(solution)/shard_map/ppermute | solution.py:440
  49.5 1.6 %collective-permute-done.5.near = f32[48,128]{1,0:T(8,128)S(1)} collective-permute-done((f32[48,128]{1,0:T(8,128)S(1)}, f32[48,128]{1,0:T(8,128)S(1)}, u32[]{:S(2)}, u32[]{:S(2)}) %collective-permute-start.5) | collective-permute-done | bytes 24608 | tf_op jit(solution)/shard_map/ppermute | solution.py:441
  51.4 2.9 %collective-permute-start.7 = (f32[80,128]{1,0:T(8,128)S(1)}, f32[80,128]{1,0:T(8,128)S(1)}, u32[]{:S(2)}, u32[]{:S(2)}) collective-permute-start(f32[80,128]{1,0:T(8,128)S(1)} %get-tuple-element.42), channel_id=1, source_target_pairs={{0,1},{1,0},{2,3},{3,2},{4,5},{5,4},{6,7},{7,6},{8,9},{9,8},{10,11... | collective-permute-start | bytes 122888 | tf_op jit(solution)/shard_map/ppermute | solution.py:441
  54.5 3.1 %collective-permute-done.6.low = f32[72,128]{1,0:T(8,128)S(1)} collective-permute-done((f32[72,128]{1,0:T(8,128)S(1)}, f32[72,128]{1,0:T(8,128)S(1)}, u32[]{:S(2)}, u32[]{:S(2)}) %collective-permute-start.6) | collective-permute-done | bytes 36896 | tf_op jit(solution)/shard_map/ppermute | solution.py:440
  57.6 4.4 %shard_map.117 = (f32[384,128]{1,0:T(8,128)}, f32[3,4,8,128]{3,2,1,0:T(8,128)S(1)}, f32[48,128]{1,0:T(8,128)S(1)}, f32[48,128]{1,0:T(8,128)S(1)}) custom-call(f32[3,4,8,128]{3,2,1,0:T(8,128)S(1)} %get-tuple-element.37.current, f32[48,128]{1,0:T(8,128)S(1)} %collective-permute-done.4.far, f32[48,128]{1,0:T(8,128)S(1)} %collective-permute-done.5.near, ...), custom_call_target="tpu_custom_call" | custom-call | flops 1000000 | tf_op jit(solution)/shard_map/pallas_call | solution.py:424
  62.0 6.6 %all-to-all-start.1 = ((f32[128,1,384]{2,1,0:T(1,128)}), f32[128,1,384]{2,1,0:T(1,128)S(1)}, u32[]{:S(2)}, u32[]{:S(2)}) async-start(f32[128,1,384]{2,1,0:T(1,128)} %bitcast.14), calls=%async_computation.1 | async-start | bytes 393216 | tf_op jit(solution)/shard_map/all_to_all | solution.py:505
  68.5 7.1 %collective-permute-start.8 = (f32[48,128]{1,0:T(8,128)S(1)}, f32[48,128]{1,0:T(8,128)S(1)}, u32[]{:S(2)}, u32[]{:S(2)}) collective-permute-start(f32[48,128]{1,0:T(8,128)S(1)} %get-tuple-element.47), channel_id=1, source_target_pairs={{0,252},{4,8},{8,4},{12,16},{16,12},{20,24},{24,20},{28,32},{32,28... | collective-permute-start | bytes 73736 | tf_op jit(solution)/shard_map/ppermute | solution.py:440
  75.7 3.2 %collective-permute-done.8.far = f32[48,128]{1,0:T(8,128)S(1)} collective-permute-done((f32[48,128]{1,0:T(8,128)S(1)}, f32[48,128]{1,0:T(8,128)S(1)}, u32[]{:S(2)}, u32[]{:S(2)}) %collective-permute-start.8) | collective-permute-done | bytes 24608 | tf_op jit(solution)/shard_map/ppermute | solution.py:440
  80.8 2.4 %collective-permute-start.11 = (f32[80,128]{1,0:T(8,128)S(1)}, f32[80,128]{1,0:T(8,128)S(1)}, u32[]{:S(2)}, u32[]{:S(2)}) collective-permute-start(f32[80,128]{1,0:T(8,128)S(1)} %get-tuple-element.51), channel_id=1, source_target_pairs={{0,1},{1,0},{2,3},{3,2},{4,5},{5,4},{6,7},{7,6},{8,9},{9,8},{10,11... | collective-permute-start | bytes 122888 | tf_op jit(solution)/shard_map/ppermute | solution.py:441
  83.5 3.0 %collective-permute-done.10.low = f32[72,128]{1,0:T(8,128)S(1)} collective-permute-done((f32[72,128]{1,0:T(8,128)S(1)}, f32[72,128]{1,0:T(8,128)S(1)}, u32[]{:S(2)}, u32[]{:S(2)}) %collective-permute-start.10) | collective-permute-done | bytes 36896 | tf_op jit(solution)/shard_map/ppermute | solution.py:440
  86.6 4.4 %shard_map.119 = (f32[384,128]{1,0:T(8,128)}, f32[3,4,8,128]{3,2,1,0:T(8,128)S(1)}, f32[48,128]{1,0:T(8,128)S(1)}, f32[48,128]{1,0:T(8,128)S(1)}) custom-call(f32[3,4,8,128]{3,2,1,0:T(8,128)S(1)} %get-tuple-element.46.current, f32[48,128]{1,0:T(8,128)S(1)} %collective-permute-done.8.far, f32[48,128]{1,0:T(8,128)S(1)} %collective-permute-done.9.near, ...), custom_call_target="tpu_custom_call" | custom-call | flops 1000000 | tf_op jit(solution)/shard_map/pallas_call | solution.py:424
  90.9 6.4 %all-to-all-start.2 = ((f32[128,1,384]{2,1,0:T(1,128)}), f32[128,1,384]{2,1,0:T(1,128)S(1)}, u32[]{:S(2)}, u32[]{:S(2)}) async-start(f32[128,1,384]{2,1,0:T(1,128)} %bitcast.13), calls=%async_computation.2 | async-start | bytes 393216 | tf_op jit(solution)/shard_map/all_to_all | solution.py:505
  97.3 7.1 %collective-permute-start.12 = (f32[48,128]{1,0:T(8,128)S(1)}, f32[48,128]{1,0:T(8,128)S(1)}, u32[]{:S(2)}, u32[]{:S(2)}) collective-permute-start(f32[48,128]{1,0:T(8,128)S(1)} %get-tuple-element.54), channel_id=1, source_target_pairs={{0,252},{4,8},{8,4},{12,16},{16,12},{20,24},{24,20},{28,32},{32,28... | collective-permute-start | bytes 73736 | tf_op jit(solution)/shard_map/ppermute | solution.py:440
  104.4 3.2 %collective-permute-done.12.far = f32[48,128]{1,0:T(8,128)S(1)} collective-permute-done((f32[48,128]{1,0:T(8,128)S(1)}, f32[48,128]{1,0:T(8,128)S(1)}, u32[]{:S(2)}, u32[]{:S(2)}) %collective-permute-start.12) | collective-permute-done | bytes 24608 | tf_op jit(solution)/shard_map/ppermute | solution.py:440
  109.5 2.4 %collective-permute-start.15 = (f32[80,128]{1,0:T(8,128)S(1)}, f32[80,128]{1,0:T(8,128)S(1)}, u32[]{:S(2)}, u32[]{:S(2)}) collective-permute-start(f32[80,128]{1,0:T(8,128)S(1)} %get-tuple-element.58), channel_id=1, source_target_pairs={{0,1},{1,0},{2,3},{3,2},{4,5},{5,4},{6,7},{7,6},{8,9},{9,8},{10,11... | collective-permute-start | bytes 122888 | tf_op jit(solution)/shard_map/ppermute | solution.py:441
  112.3 3.0 %collective-permute-done.14.low = f32[72,128]{1,0:T(8,128)S(1)} collective-permute-done((f32[72,128]{1,0:T(8,128)S(1)}, f32[72,128]{1,0:T(8,128)S(1)}, u32[]{:S(2)}, u32[]{:S(2)}) %collective-permute-start.14) | collective-permute-done | bytes 36896 | tf_op jit(solution)/shard_map/ppermute | solution.py:440
  (25 shorter events, 7.2 us)
Async XLA Ops:
  1.8 14.2 %collective-permute-start = (f32[216,128]{1,0:T(8,128)S(1)}, f32[216,128]{1,0:T(8,128)S(1)}, u32[]{:S(2)}, u32[]{:S(2)}) collective-permute-start(f32[216,128]{1,0:T(8,128)S(1)} %get-tuple-element.31), channel_id=1, source_target_pairs={{0,252},{4,8},{8,4},{12,16},{16,12},{20,24},{24,20},{28,32},{32,28... | collective-permute-start | bytes 331784 | tf_op jit(solution)/shard_map/ppermute | solution.py:440
  13.2 5.1 %collective-permute-start.1 = (f32[216,128]{1,0:T(8,128)S(1)}, f32[216,128]{1,0:T(8,128)S(1)}, u32[]{:S(2)}, u32[]{:S(2)}) collective-permute-start(f32[216,128]{1,0:T(8,128)S(1)} %get-tuple-element.32), channel_id=1, source_target_pairs={{0,4},{4,0},{8,12},{12,8},{16,20},{20,16},{24,28},{28,24},{32,36},... | collective-permute-start | bytes 331784 | tf_op jit(solution)/shard_map/ppermute | solution.py:441
  18.4 6.7 %collective-permute-start.2 = (f32[324,128]{1,0:T(8,128)S(1)}, f32[324,128]{1,0:T(8,128)S(1)}, u32[]{:S(2)}, u32[]{:S(2)}) collective-permute-start(f32[324,128]{1,0:T(8,128)S(1)} %get-tuple-element.34), channel_id=1, source_target_pairs={{0,3},{1,2},{2,1},{3,0},{4,7},{5,6},{6,5},{7,4},{8,11},{9,10},{10,... | collective-permute-start | bytes 497672 | tf_op jit(solution)/shard_map/ppermute | solution.py:440
  20.7 4.3 %collective-permute-start.3 = (f32[324,128]{1,0:T(8,128)S(1)}, f32[324,128]{1,0:T(8,128)S(1)}, u32[]{:S(2)}, u32[]{:S(2)}) collective-permute-start(f32[324,128]{1,0:T(8,128)S(1)} %get-tuple-element.35), channel_id=1, source_target_pairs={{0,1},{1,0},{2,3},{3,2},{4,5},{5,4},{6,7},{7,6},{8,9},{9,8},{10,11... | collective-permute-start | bytes 497672 | tf_op jit(solution)/shard_map/ppermute | solution.py:441
  25.0 32.6 %copy-start = (f32[32,8192]{1,0:T(8,128)S(1)}, f32[32,8192]{1,0:T(8,128)}, u32[]{:S(2)}) copy-start(f32[32,8192]{1,0:T(8,128)} %coarse.3) | copy-start | bytes 3145732
  29.9 21.4 %all-to-all-start = ((f32[128,1,384]{2,1,0:T(1,128)}), f32[128,1,384]{2,1,0:T(1,128)S(1)}, u32[]{:S(2)}, u32[]{:S(2)}) async-start(f32[128,1,384]{2,1,0:T(1,128)} %bitcast.12), calls=%async_computation | async-start | bytes 393216 | tf_op jit(solution)/shard_map/all_to_all | solution.py:505
  39.5 10.0 %collective-permute-start.4 = (f32[48,128]{1,0:T(8,128)S(1)}, f32[48,128]{1,0:T(8,128)S(1)}, u32[]{:S(2)}, u32[]{:S(2)}) collective-permute-start(f32[48,128]{1,0:T(8,128)S(1)} %get-tuple-element.38), channel_id=1, source_target_pairs={{0,252},{4,8},{8,4},{12,16},{16,12},{20,24},{24,20},{28,32},{32,28... | collective-permute-start | bytes 73736 | tf_op jit(solution)/shard_map/ppermute | solution.py:440
  46.6 4.5 %collective-permute-start.5 = (f32[48,128]{1,0:T(8,128)S(1)}, f32[48,128]{1,0:T(8,128)S(1)}, u32[]{:S(2)}, u32[]{:S(2)}) collective-permute-start(f32[48,128]{1,0:T(8,128)S(1)} %get-tuple-element.39), channel_id=1, source_target_pairs={{0,4},{4,0},{8,12},{12,8},{16,20},{20,16},{24,28},{28,24},{32,36},... | collective-permute-start | bytes 73736 | tf_op jit(solution)/shard_map/ppermute | solution.py:441
  51.4 6.2 %collective-permute-start.7 = (f32[80,128]{1,0:T(8,128)S(1)}, f32[80,128]{1,0:T(8,128)S(1)}, u32[]{:S(2)}, u32[]{:S(2)}) collective-permute-start(f32[80,128]{1,0:T(8,128)S(1)} %get-tuple-element.42), channel_id=1, source_target_pairs={{0,1},{1,0},{2,3},{3,2},{4,5},{5,4},{6,7},{7,6},{8,9},{9,8},{10,11... | collective-permute-start | bytes 122888 | tf_op jit(solution)/shard_map/ppermute | solution.py:441
  54.2 3.4 %collective-permute-start.6 = (f32[72,128]{1,0:T(8,128)S(1)}, f32[72,128]{1,0:T(8,128)S(1)}, u32[]{:S(2)}, u32[]{:S(2)}) collective-permute-start(f32[72,128]{1,0:T(8,128)S(1)} %get-tuple-element.41), channel_id=1, source_target_pairs={{0,3},{1,2},{2,1},{3,0},{4,7},{5,6},{6,5},{7,4},{8,11},{9,10},{10,... | collective-permute-start | bytes 110600 | tf_op jit(solution)/shard_map/ppermute | solution.py:440
  62.0 18.8 %all-to-all-start.1 = ((f32[128,1,384]{2,1,0:T(1,128)}), f32[128,1,384]{2,1,0:T(1,128)S(1)}, u32[]{:S(2)}, u32[]{:S(2)}) async-start(f32[128,1,384]{2,1,0:T(1,128)} %bitcast.14), calls=%async_computation.1 | async-start | bytes 393216 | tf_op jit(solution)/shard_map/all_to_all | solution.py:505
  68.5 10.3 %collective-permute-start.8 = (f32[48,128]{1,0:T(8,128)S(1)}, f32[48,128]{1,0:T(8,128)S(1)}, u32[]{:S(2)}, u32[]{:S(2)}) collective-permute-start(f32[48,128]{1,0:T(8,128)S(1)} %get-tuple-element.47), channel_id=1, source_target_pairs={{0,252},{4,8},{8,4},{12,16},{16,12},{20,24},{24,20},{28,32},{32,28... | collective-permute-start | bytes 73736 | tf_op jit(solution)/shard_map/ppermute | solution.py:440
  75.7 4.5 %collective-permute-start.9 = (f32[48,128]{1,0:T(8,128)S(1)}, f32[48,128]{1,0:T(8,128)S(1)}, u32[]{:S(2)}, u32[]{:S(2)}) collective-permute-start(f32[48,128]{1,0:T(8,128)S(1)} %get-tuple-element.48), channel_id=1, source_target_pairs={{0,4},{4,0},{8,12},{12,8},{16,20},{20,16},{24,28},{28,24},{32,36},... | collective-permute-start | bytes 73736 | tf_op jit(solution)/shard_map/ppermute | solution.py:441
  80.8 5.8 %collective-permute-start.11 = (f32[80,128]{1,0:T(8,128)S(1)}, f32[80,128]{1,0:T(8,128)S(1)}, u32[]{:S(2)}, u32[]{:S(2)}) collective-permute-start(f32[80,128]{1,0:T(8,128)S(1)} %get-tuple-element.51), channel_id=1, source_target_pairs={{0,1},{1,0},{2,3},{3,2},{4,5},{5,4},{6,7},{7,6},{8,9},{9,8},{10,11... | collective-permute-start | bytes 122888 | tf_op jit(solution)/shard_map/ppermute | solution.py:441
  83.2 3.4 %collective-permute-start.10 = (f32[72,128]{1,0:T(8,128)S(1)}, f32[72,128]{1,0:T(8,128)S(1)}, u32[]{:S(2)}, u32[]{:S(2)}) collective-permute-start(f32[72,128]{1,0:T(8,128)S(1)} %get-tuple-element.50), channel_id=1, source_target_pairs={{0,3},{1,2},{2,1},{3,0},{4,7},{5,6},{6,5},{7,4},{8,11},{9,10},{10,... | collective-permute-start | bytes 110600 | tf_op jit(solution)/shard_map/ppermute | solution.py:440
  90.9 18.6 %all-to-all-start.2 = ((f32[128,1,384]{2,1,0:T(1,128)}), f32[128,1,384]{2,1,0:T(1,128)S(1)}, u32[]{:S(2)}, u32[]{:S(2)}) async-start(f32[128,1,384]{2,1,0:T(1,128)} %bitcast.13), calls=%async_computation.2 | async-start | bytes 393216 | tf_op jit(solution)/shard_map/all_to_all | solution.py:505
  97.3 10.3 %collective-permute-start.12 = (f32[48,128]{1,0:T(8,128)S(1)}, f32[48,128]{1,0:T(8,128)S(1)}, u32[]{:S(2)}, u32[]{:S(2)}) collective-permute-start(f32[48,128]{1,0:T(8,128)S(1)} %get-tuple-element.54), channel_id=1, source_target_pairs={{0,252},{4,8},{8,4},{12,16},{16,12},{20,24},{24,20},{28,32},{32,28... | collective-permute-start | bytes 73736 | tf_op jit(solution)/shard_map/ppermute | solution.py:440
  104.4 4.5 %collective-permute-start.13 = (f32[48,128]{1,0:T(8,128)S(1)}, f32[48,128]{1,0:T(8,128)S(1)}, u32[]{:S(2)}, u32[]{:S(2)}) collective-permute-start(f32[48,128]{1,0:T(8,128)S(1)} %get-tuple-element.55), channel_id=1, source_target_pairs={{0,4},{4,0},{8,12},{12,8},{16,20},{20,16},{24,28},{28,24},{32,36},... | collective-permute-start | bytes 73736 | tf_op jit(solution)/shard_map/ppermute | solution.py:441
  109.5 5.8 %collective-permute-start.15 = (f32[80,128]{1,0:T(8,128)S(1)}, f32[80,128]{1,0:T(8,128)S(1)}, u32[]{:S(2)}, u32[]{:S(2)}) collective-permute-start(f32[80,128]{1,0:T(8,128)S(1)} %get-tuple-element.58), channel_id=1, source_target_pairs={{0,1},{1,0},{2,3},{3,2},{4,5},{5,4},{6,7},{7,6},{8,9},{9,8},{10,11... | collective-permute-start | bytes 122888 | tf_op jit(solution)/shard_map/ppermute | solution.py:441
  111.9 3.4 %collective-permute-start.14 = (f32[72,128]{1,0:T(8,128)S(1)}, f32[72,128]{1,0:T(8,128)S(1)}, u32[]{:S(2)}, u32[]{:S(2)}) collective-permute-start(f32[72,128]{1,0:T(8,128)S(1)} %get-tuple-element.57), channel_id=1, source_target_pairs={{0,3},{1,2},{2,1},{3,0},{4,7},{5,6},{6,5},{7,4},{8,11},{9,10},{10,... | collective-permute-start | bytes 110600 | tf_op jit(solution)/shard_map/ppermute | solution.py:440

commit v8 on v7

--- a/solution.py
+++ b/solution.py
@@ -160,7 +160,7 @@
             high[at : at + 2] = pick(narrow_odd, v[0:2], v[6:8])
 
 
-def pack_current(current, far, near, received, low, high, part):
+def group_sums(received, part):
     total = received[0:24]
     for i in range(24, received.shape[0], 24):
         total += received[i : i + 24]
@@ -168,6 +168,10 @@
     part[...] = jnp.zeros((8, LANES), f32)
     for k in range(3):
         part[k : k + 1, :] = jnp.sum(jnp.where(block_of == k, total, 0.0), axis=0, keepdims=True)
+
+
+def pack_current(current, far, near, received, low, high, part):
+    group_sums(received, part)
     high[72:80] = part[...]
     odd = is_odd("wide")
     narrow_odd = is_odd("narrow")
@@ -354,8 +358,46 @@
     solve_box(values, coef, agg, coarse, factors_hbm, payload, moved, far_out, near_out, scratch)
 
 
+def pack_last_low(current, low):
+    narrow_odd = is_odd("narrow")
+    for c in range(3):
+        for p in range(4):
+            v = current[c, p]
+            low[4 * c + p : 4 * c + p + 1] = pick(narrow_odd, v[7:8], v[0:1])
+    low[12:16] = jnp.zeros((4, LANES), f32)
+
+
+def pack_last_high(current, received, _, high, part):
+    narrow_odd = is_odd("narrow")
+    for c in range(3):
+        for p in range(4):
+            v = current[c, p]
+            high[4 * c + p : 4 * c + p + 1] = pick(narrow_odd, v[0:1], v[7:8])
+    high[12:16] = jnp.zeros((4, LANES), f32)
+    group_sums(received, part)
+    high[16:24] = part[...]
+
+
 def last_misfit(current, far, near, low, high, part, slots, coef, iterate, residual, values):
-    gather_values(current, far, near, low, high, part, slots, values)
+    odd = is_odd("wide")
+    narrow_odd = is_odd("narrow")
+    total = part[...] + high[16:24]
+    blank = jnp.zeros((8, LANES), f32)
+    for a in range(1, 7):
+        block = 0 if a < 2 else 2 if a >= 6 else 1
+        table = jnp.broadcast_to(total[block : block + 1], (8, LANES))
+        for c in range(3):
+            values[c, a, 0:8] = rim_rows(odd, far, near, current, c, c * 16, 2, a)
+            values[c, a, 8:16] = blank
+            if 2 <= a < 6:
+                at = 4 * c + a - 2
+                first, second = low[at : at + 1], high[at : at + 1]
+                values[c, a, 8:9] = pick(narrow_odd, first, second)
+                values[c, a, 15:16] = pick(narrow_odd, second, first)
+        for half in range(2):
+            where = slots[a, 8 * half : 8 * half + 8]
+            lifted = jnp.take_along_axis(table, where, axis=1, mode="promise_in_bounds")
+            values[0, a, 8 * half : 8 * half + 8] += lifted
     rolled = {}
     for a in range(2, 6):
         applied = operate_pair(values, coef, a, rolled)
@@ -435,11 +477,17 @@
     )(*operands)
 
 
+def swap_far(axis, values):
+    count = lax.axis_size(axis)
+    return lax.ppermute(values, axis, [(i, (i + (1 if i % 2 else -1)) % count) for i in range(count)])
+
+
+def swap_near(axis, values):
+    return lax.ppermute(values, axis, [(i, i ^ 1) for i in range(lax.axis_size(axis))])
+
+
 def swaps(axis, far, near):
-    count = lax.axis_size(axis)
-    far = lax.ppermute(far, axis, [(i, (i + (1 if i % 2 else -1)) % count) for i in range(count)])
-    near = lax.ppermute(near, axis, [(i, i ^ 1) for i in range(count)])
-    return far, near
+    return swap_far(axis, far), swap_near(axis, near)
 
 
 def per_device(
@@ -504,10 +552,16 @@
         blocks = payload.reshape(members, 1, 3 * LANES)
         received = lax.all_to_all(blocks, ("wide", "narrow"), 0, 0, axis_index_groups=groups).reshape(payload_type[0])
         far, near = swaps("wide", far, near)
-        low, high, part = call(
-            pack_current, [narrow_type, ((80, LANES), f32), ((8, LANES), f32)], [], [current, far, near, received]
-        )
-        low, high = swaps("narrow", low, high)
+        if sweep < SWEEPS - 1:
+            low, high, part = call(
+                pack_current, [narrow_type, ((80, LANES), f32), ((8, LANES), f32)], [], [current, far, near, received]
+            )
+            low, high = swaps("narrow", low, high)
+        else:
+            (low,) = call(pack_last_low, [((16, LANES), f32)], [], [current])
+            low = swap_far("narrow", low)
+            high, part = call(pack_last_high, [((24, LANES), f32), ((8, LANES), f32)], [], [current, received, low])
+            high = swap_near("narrow", high)
         known = [current, far, near, low, high, part, slots, coef]
         if sweep < SWEEPS - 1:
             payload, current, far, near = call(

time: 116 us -> 114 us (0.983)
  waiting for transfers between devices: 33.4 us -> 30 us
    ppermute x16, waiting for transfers between devices: 32 us -> 27.6 us  [the longest x8 21.5 us: swap_far(): lax.ppermute(values, axis, [(i, (i + (1 if i % 2 else -1)) % count) for i...]
    pallas_call x9 -> x10, Pallas kernels: 15.7 us -> 15.7 us  [call(): pl.pallas_call(body, out_shape=[pltpu.HBM(shape, dtype) if i in out_hbm e...]
  transfers between devices with their start and end apart: 19 -> 19, of which waited for: 15 -> 14; matrix products, arithmetic and copies ran while one was open for 0% -> 0% of each run, Pallas kernels for 0% -> 0%
where the time goes in v8:
time: 114 us
  starting transfers between devices  67.1 us (59%)
  waiting for transfers between devices  30 us (26%)
  Pallas kernels  15.7 us (14%)
    ppermute x8, starting transfers between devices, swap_far(): lax.ppermute(values, axis, [(i, (i + (1 if i % 2 else -1)) % count) for i...  37 us
    all_to_all x3, starting transfers between devices, per_device(): lax.all_to_all(blocks, ('wide', 'narrow'), 0, 0, axis_index_groups=groups)  22.4 us
    ppermute x8, waiting for transfers between devices, swap_far(): lax.ppermute(values, axis, [(i, (i + (1 if i % 2 else -1)) % count) for i...  21.5 us
    pallas_call x10, Pallas kernels, call(): pl.pallas_call(body, out_shape=[pltpu.HBM(shape, dtype) if i in out_hbm e...  15.7 us
    ppermute x8, starting transfers between devices, swap_near(): lax.ppermute(values, axis, [(i, i ^ 1) for i in range(lax.axis_size(axis))])  7.67 us
    ppermute x8, waiting for transfers between devices, swap_near(): lax.ppermute(values, axis, [(i, i ^ 1) for i in range(lax.axis_size(axis))])  6.09 us
    all_to_all x3, waiting for transfers between devices, per_device(): lax.all_to_all(blocks, ('wide', 'narrow'), 0, 0, axis_index_groups=groups)  2.39 us
  transfers between devices with their start and end apart: 19, of which 14 were waited for; matrix products, arithmetic and copies ran while one was open for 0% of the time, Pallas kernels for 0%

profile of v8, /device:TPU:1, one launch (start us, length us, event | category | flops | bytes accessed | tf_op | source)
XLA Modules:
  0.0 113.5 jit_solution(13360432091371040942)
XLA Ops:
  1.8 11.4 %collective-permute-start = (f32[216,128]{1,0:T(8,128)S(1)}, f32[216,128]{1,0:T(8,128)S(1)}, u32[]{:S(2)}, u32[]{:S(2)}) collective-permute-start(f32[216,128]{1,0:T(8,128)S(1)} %get-tuple-element.30), channel_id=1, source_target_pairs={{0,252},{4,8},{8,4},{12,16},{16,12},{20,24},{24,20},{28,32},{32,28... | collective-permute-start | bytes 331784 | tf_op jit(solution)/shard_map/ppermute | solution.py:482
  13.2 2.8 %collective-permute-done.far = f32[216,128]{1,0:T(8,128)S(1)} collective-permute-done((f32[216,128]{1,0:T(8,128)S(1)}, f32[216,128]{1,0:T(8,128)S(1)}, u32[]{:S(2)}, u32[]{:S(2)}) %collective-permute-start) | collective-permute-done | bytes 110624 | tf_op jit(solution)/shard_map/ppermute | solution.py:482
  15.9 2.3 %collective-permute-done.1.near = f32[216,128]{1,0:T(8,128)S(1)} collective-permute-done((f32[216,128]{1,0:T(8,128)S(1)}, f32[216,128]{1,0:T(8,128)S(1)}, u32[]{:S(2)}, u32[]{:S(2)}) %collective-permute-start.1) | collective-permute-done | bytes 110624 | tf_op jit(solution)/shard_map/ppermute | solution.py:486
  18.4 2.4 %collective-permute-start.2 = (f32[324,128]{1,0:T(8,128)S(1)}, f32[324,128]{1,0:T(8,128)S(1)}, u32[]{:S(2)}, u32[]{:S(2)}) collective-permute-start(f32[324,128]{1,0:T(8,128)S(1)} %get-tuple-element.33), channel_id=1, source_target_pairs={{0,3},{1,2},{2,1},{3,0},{4,7},{5,6},{6,5},{7,4},{8,11},{9,10},{10,... | collective-permute-start | bytes 497672 | tf_op jit(solution)/shard_map/ppermute | solution.py:482
  20.8 4.3 %collective-permute-done.2.low = f32[324,128]{1,0:T(8,128)S(1)} collective-permute-done((f32[324,128]{1,0:T(8,128)S(1)}, f32[324,128]{1,0:T(8,128)S(1)}, u32[]{:S(2)}, u32[]{:S(2)}) %collective-permute-start.2) | collective-permute-done | bytes 165920 | tf_op jit(solution)/shard_map/ppermute | solution.py:482
  25.0 4.9 %shard_map.115 = (f32[22,6,16,128]{3,2,1,0:T(8,128)S(1)}, s32[8,16,128]{2,1,0:T(8,128)S(1)}, f32[384,128]{1,0:T(8,128)}, f32[3,4,8,128]{3,2,1,0:T(8,128)S(1)}, f...) custom-call(f32[216,128]{1,0:T(8,128)S(1)} %collective-permute-done.far, f32[216,128]{1,0:T(8,128)S(1)} %collective-permute-done.1.near, ...), custom_call_target="tpu_custom_call" | custom-call | flops 1000000 | tf_op jit(solution)/shard_map/pallas_call | solution.py:466
  29.9 9.5 %all-to-all-start = ((f32[128,1,384]{2,1,0:T(1,128)}), f32[128,1,384]{2,1,0:T(1,128)S(1)}, u32[]{:S(2)}, u32[]{:S(2)}) async-start(f32[128,1,384]{2,1,0:T(1,128)} %bitcast.13), calls=%async_computation | async-start | bytes 393216 | tf_op jit(solution)/shard_map/all_to_all | solution.py:553
  39.5 7.1 %collective-permute-start.4 = (f32[48,128]{1,0:T(8,128)S(1)}, f32[48,128]{1,0:T(8,128)S(1)}, u32[]{:S(2)}, u32[]{:S(2)}) collective-permute-start(f32[48,128]{1,0:T(8,128)S(1)} %get-tuple-element.37), channel_id=1, source_target_pairs={{0,252},{4,8},{8,4},{12,16},{16,12},{20,24},{24,20},{28,32},{32,28... | collective-permute-start | bytes 73736 | tf_op jit(solution)/shard_map/ppermute | solution.py:482
  46.6 2.9 %collective-permute-done.4.far = f32[48,128]{1,0:T(8,128)S(1)} collective-permute-done((f32[48,128]{1,0:T(8,128)S(1)}, f32[48,128]{1,0:T(8,128)S(1)}, u32[]{:S(2)}, u32[]{:S(2)}) %collective-permute-start.4) | collective-permute-done | bytes 24608 | tf_op jit(solution)/shard_map/ppermute | solution.py:482
  49.5 1.6 %collective-permute-done.5.near = f32[48,128]{1,0:T(8,128)S(1)} collective-permute-done((f32[48,128]{1,0:T(8,128)S(1)}, f32[48,128]{1,0:T(8,128)S(1)}, u32[]{:S(2)}, u32[]{:S(2)}) %collective-permute-start.5) | collective-permute-done | bytes 24608 | tf_op jit(solution)/shard_map/ppermute | solution.py:486
  51.4 2.9 %collective-permute-start.7 = (f32[80,128]{1,0:T(8,128)S(1)}, f32[80,128]{1,0:T(8,128)S(1)}, u32[]{:S(2)}, u32[]{:S(2)}) collective-permute-start(f32[80,128]{1,0:T(8,128)S(1)} %get-tuple-element.41), channel_id=1, source_target_pairs={{0,1},{1,0},{2,3},{3,2},{4,5},{5,4},{6,7},{7,6},{8,9},{9,8},{10,11... | collective-permute-start | bytes 122888 | tf_op jit(solution)/shard_map/ppermute | solution.py:486
  54.5 3.1 %collective-permute-done.6.low = f32[72,128]{1,0:T(8,128)S(1)} collective-permute-done((f32[72,128]{1,0:T(8,128)S(1)}, f32[72,128]{1,0:T(8,128)S(1)}, u32[]{:S(2)}, u32[]{:S(2)}) %collective-permute-start.6) | collective-permute-done | bytes 36896 | tf_op jit(solution)/shard_map/ppermute | solution.py:482
  57.6 4.4 %shard_map.117 = (f32[384,128]{1,0:T(8,128)}, f32[3,4,8,128]{3,2,1,0:T(8,128)S(1)}, f32[48,128]{1,0:T(8,128)S(1)}, f32[48,128]{1,0:T(8,128)S(1)}) custom-call(f32[3,4,8,128]{3,2,1,0:T(8,128)S(1)} %get-tuple-element.36.current, f32[48,128]{1,0:T(8,128)S(1)} %collective-permute-done.4.far, f32[48,128]{1,0:T(8,128)S(1)} %collective-permute-done.5.near, ...), custom_call_target="tpu_custom_call" | custom-call | flops 1000000 | tf_op jit(solution)/shard_map/pallas_call | solution.py:466
  62.0 6.6 %all-to-all-start.1 = ((f32[128,1,384]{2,1,0:T(1,128)}), f32[128,1,384]{2,1,0:T(1,128)S(1)}, u32[]{:S(2)}, u32[]{:S(2)}) async-start(f32[128,1,384]{2,1,0:T(1,128)} %bitcast.14), calls=%async_computation.1 | async-start | bytes 393216 | tf_op jit(solution)/shard_map/all_to_all | solution.py:553
  68.5 7.1 %collective-permute-start.8 = (f32[48,128]{1,0:T(8,128)S(1)}, f32[48,128]{1,0:T(8,128)S(1)}, u32[]{:S(2)}, u32[]{:S(2)}) collective-permute-start(f32[48,128]{1,0:T(8,128)S(1)} %get-tuple-element.46), channel_id=1, source_target_pairs={{0,252},{4,8},{8,4},{12,16},{16,12},{20,24},{24,20},{28,32},{32,28... | collective-permute-start | bytes 73736 | tf_op jit(solution)/shard_map/ppermute | solution.py:482
  75.7 3.2 %collective-permute-done.8.far = f32[48,128]{1,0:T(8,128)S(1)} collective-permute-done((f32[48,128]{1,0:T(8,128)S(1)}, f32[48,128]{1,0:T(8,128)S(1)}, u32[]{:S(2)}, u32[]{:S(2)}) %collective-permute-start.8) | collective-permute-done | bytes 24608 | tf_op jit(solution)/shard_map/ppermute | solution.py:482
  80.8 2.4 %collective-permute-start.11 = (f32[80,128]{1,0:T(8,128)S(1)}, f32[80,128]{1,0:T(8,128)S(1)}, u32[]{:S(2)}, u32[]{:S(2)}) collective-permute-start(f32[80,128]{1,0:T(8,128)S(1)} %get-tuple-element.50), channel_id=1, source_target_pairs={{0,1},{1,0},{2,3},{3,2},{4,5},{5,4},{6,7},{7,6},{8,9},{9,8},{10,11... | collective-permute-start | bytes 122888 | tf_op jit(solution)/shard_map/ppermute | solution.py:486
  83.5 3.0 %collective-permute-done.10.low = f32[72,128]{1,0:T(8,128)S(1)} collective-permute-done((f32[72,128]{1,0:T(8,128)S(1)}, f32[72,128]{1,0:T(8,128)S(1)}, u32[]{:S(2)}, u32[]{:S(2)}) %collective-permute-start.10) | collective-permute-done | bytes 36896 | tf_op jit(solution)/shard_map/ppermute | solution.py:482
  86.6 4.4 %shard_map.119 = (f32[384,128]{1,0:T(8,128)}, f32[3,4,8,128]{3,2,1,0:T(8,128)S(1)}, f32[48,128]{1,0:T(8,128)S(1)}, f32[48,128]{1,0:T(8,128)S(1)}) custom-call(f32[3,4,8,128]{3,2,1,0:T(8,128)S(1)} %get-tuple-element.45.current, f32[48,128]{1,0:T(8,128)S(1)} %collective-permute-done.8.far, f32[48,128]{1,0:T(8,128)S(1)} %collective-permute-done.9.near, ...), custom_call_target="tpu_custom_call" | custom-call | flops 1000000 | tf_op jit(solution)/shard_map/pallas_call | solution.py:466
  90.9 6.4 %all-to-all-start.2 = ((f32[128,1,384]{2,1,0:T(1,128)}), f32[128,1,384]{2,1,0:T(1,128)S(1)}, u32[]{:S(2)}, u32[]{:S(2)}) async-start(f32[128,1,384]{2,1,0:T(1,128)} %bitcast.12), calls=%async_computation.2 | async-start | bytes 393216 | tf_op jit(solution)/shard_map/all_to_all | solution.py:553
  97.3 7.1 %collective-permute-start.12 = (f32[48,128]{1,0:T(8,128)S(1)}, f32[48,128]{1,0:T(8,128)S(1)}, u32[]{:S(2)}, u32[]{:S(2)}) collective-permute-start(f32[48,128]{1,0:T(8,128)S(1)} %get-tuple-element.53), channel_id=1, source_target_pairs={{0,252},{4,8},{8,4},{12,16},{16,12},{20,24},{24,20},{28,32},{32,28... | collective-permute-start | bytes 73736 | tf_op jit(solution)/shard_map/ppermute | solution.py:482
  105.6 2.3 %collective-permute-done.14._.low = f32[16,128]{1,0:T(8,128)S(1)} collective-permute-done((f32[16,128]{1,0:T(8,128)S(1)}, f32[16,128]{1,0:T(8,128)S(1)}, u32[]{:S(2)}, u32[]{:S(2)}) %collective-permute-start.14) | collective-permute-done | bytes 8224 | tf_op jit(solution)/shard_map/ppermute | solution.py:482
  107.9 1.6 %all-to-all-done.2 = f32[128,1,384]{2,1,0:T(1,128)S(1)} async-done(((f32[128,1,384]{2,1,0:T(1,128)}), f32[128,1,384]{2,1,0:T(1,128)S(1)}, u32[]{:S(2)}, u32[]{:S(2)}) %all-to-all-start.2) | async-done | bytes 196640 | tf_op jit(solution)/shard_map/all_to_all | solution.py:553
  109.5 2.4 %collective-permute-start.15 = (f32[24,128]{1,0:T(8,128)S(1)}, f32[24,128]{1,0:T(8,128)S(1)}, u32[]{:S(2)}, u32[]{:S(2)}) collective-permute-start(f32[24,128]{1,0:T(8,128)S(1)} %get-tuple-element.56), channel_id=1, source_target_pairs={{0,1},{1,0},{2,3},{3,2},{4,5},{5,4},{6,7},{7,6},{8,9},{9,8},{10,11... | collective-permute-start | bytes 36872 | tf_op jit(solution)/shard_map/ppermute | solution.py:486
  (26 shorter events, 7.0 us)
Async XLA Ops:
  1.8 14.2 %collective-permute-start = (f32[216,128]{1,0:T(8,128)S(1)}, f32[216,128]{1,0:T(8,128)S(1)}, u32[]{:S(2)}, u32[]{:S(2)}) collective-permute-start(f32[216,128]{1,0:T(8,128)S(1)} %get-tuple-element.30), channel_id=1, source_target_pairs={{0,252},{4,8},{8,4},{12,16},{16,12},{20,24},{24,20},{28,32},{32,28... | collective-permute-start | bytes 331784 | tf_op jit(solution)/shard_map/ppermute | solution.py:482
  13.2 5.1 %collective-permute-start.1 = (f32[216,128]{1,0:T(8,128)S(1)}, f32[216,128]{1,0:T(8,128)S(1)}, u32[]{:S(2)}, u32[]{:S(2)}) collective-permute-start(f32[216,128]{1,0:T(8,128)S(1)} %get-tuple-element.31), channel_id=1, source_target_pairs={{0,4},{4,0},{8,12},{12,8},{16,20},{20,16},{24,28},{28,24},{32,36},... | collective-permute-start | bytes 331784 | tf_op jit(solution)/shard_map/ppermute | solution.py:486
  18.4 6.7 %collective-permute-start.2 = (f32[324,128]{1,0:T(8,128)S(1)}, f32[324,128]{1,0:T(8,128)S(1)}, u32[]{:S(2)}, u32[]{:S(2)}) collective-permute-start(f32[324,128]{1,0:T(8,128)S(1)} %get-tuple-element.33), channel_id=1, source_target_pairs={{0,3},{1,2},{2,1},{3,0},{4,7},{5,6},{6,5},{7,4},{8,11},{9,10},{10,... | collective-permute-start | bytes 497672 | tf_op jit(solution)/shard_map/ppermute | solution.py:482
  20.7 4.3 %collective-permute-start.3 = (f32[324,128]{1,0:T(8,128)S(1)}, f32[324,128]{1,0:T(8,128)S(1)}, u32[]{:S(2)}, u32[]{:S(2)}) collective-permute-start(f32[324,128]{1,0:T(8,128)S(1)} %get-tuple-element.34), channel_id=1, source_target_pairs={{0,1},{1,0},{2,3},{3,2},{4,5},{5,4},{6,7},{7,6},{8,9},{9,8},{10,11... | collective-permute-start | bytes 497672 | tf_op jit(solution)/shard_map/ppermute | solution.py:486
  25.0 32.6 %copy-start = (f32[32,8192]{1,0:T(8,128)S(1)}, f32[32,8192]{1,0:T(8,128)}, u32[]{:S(2)}) copy-start(f32[32,8192]{1,0:T(8,128)} %coarse.3) | copy-start | bytes 3145732
  29.9 21.4 %all-to-all-start = ((f32[128,1,384]{2,1,0:T(1,128)}), f32[128,1,384]{2,1,0:T(1,128)S(1)}, u32[]{:S(2)}, u32[]{:S(2)}) async-start(f32[128,1,384]{2,1,0:T(1,128)} %bitcast.13), calls=%async_computation | async-start | bytes 393216 | tf_op jit(solution)/shard_map/all_to_all | solution.py:553
  39.5 10.0 %collective-permute-start.4 = (f32[48,128]{1,0:T(8,128)S(1)}, f32[48,128]{1,0:T(8,128)S(1)}, u32[]{:S(2)}, u32[]{:S(2)}) collective-permute-start(f32[48,128]{1,0:T(8,128)S(1)} %get-tuple-element.37), channel_id=1, source_target_pairs={{0,252},{4,8},{8,4},{12,16},{16,12},{20,24},{24,20},{28,32},{32,28... | collective-permute-start | bytes 73736 | tf_op jit(solution)/shard_map/ppermute | solution.py:482
  46.6 4.5 %collective-permute-start.5 = (f32[48,128]{1,0:T(8,128)S(1)}, f32[48,128]{1,0:T(8,128)S(1)}, u32[]{:S(2)}, u32[]{:S(2)}) collective-permute-start(f32[48,128]{1,0:T(8,128)S(1)} %get-tuple-element.38), channel_id=1, source_target_pairs={{0,4},{4,0},{8,12},{12,8},{16,20},{20,16},{24,28},{28,24},{32,36},... | collective-permute-start | bytes 73736 | tf_op jit(solution)/shard_map/ppermute | solution.py:486
  51.4 6.2 %collective-permute-start.7 = (f32[80,128]{1,0:T(8,128)S(1)}, f32[80,128]{1,0:T(8,128)S(1)}, u32[]{:S(2)}, u32[]{:S(2)}) collective-permute-start(f32[80,128]{1,0:T(8,128)S(1)} %get-tuple-element.41), channel_id=1, source_target_pairs={{0,1},{1,0},{2,3},{3,2},{4,5},{5,4},{6,7},{7,6},{8,9},{9,8},{10,11... | collective-permute-start | bytes 122888 | tf_op jit(solution)/shard_map/ppermute | solution.py:486
  54.2 3.4 %collective-permute-start.6 = (f32[72,128]{1,0:T(8,128)S(1)}, f32[72,128]{1,0:T(8,128)S(1)}, u32[]{:S(2)}, u32[]{:S(2)}) collective-permute-start(f32[72,128]{1,0:T(8,128)S(1)} %get-tuple-element.40), channel_id=1, source_target_pairs={{0,3},{1,2},{2,1},{3,0},{4,7},{5,6},{6,5},{7,4},{8,11},{9,10},{10,... | collective-permute-start | bytes 110600 | tf_op jit(solution)/shard_map/ppermute | solution.py:482
  62.0 18.8 %all-to-all-start.1 = ((f32[128,1,384]{2,1,0:T(1,128)}), f32[128,1,384]{2,1,0:T(1,128)S(1)}, u32[]{:S(2)}, u32[]{:S(2)}) async-start(f32[128,1,384]{2,1,0:T(1,128)} %bitcast.14), calls=%async_computation.1 | async-start | bytes 393216 | tf_op jit(solution)/shard_map/all_to_all | solution.py:553
  68.5 10.3 %collective-permute-start.8 = (f32[48,128]{1,0:T(8,128)S(1)}, f32[48,128]{1,0:T(8,128)S(1)}, u32[]{:S(2)}, u32[]{:S(2)}) collective-permute-start(f32[48,128]{1,0:T(8,128)S(1)} %get-tuple-element.46), channel_id=1, source_target_pairs={{0,252},{4,8},{8,4},{12,16},{16,12},{20,24},{24,20},{28,32},{32,28... | collective-permute-start | bytes 73736 | tf_op jit(solution)/shard_map/ppermute | solution.py:482
  75.7 4.5 %collective-permute-start.9 = (f32[48,128]{1,0:T(8,128)S(1)}, f32[48,128]{1,0:T(8,128)S(1)}, u32[]{:S(2)}, u32[]{:S(2)}) collective-permute-start(f32[48,128]{1,0:T(8,128)S(1)} %get-tuple-element.47), channel_id=1, source_target_pairs={{0,4},{4,0},{8,12},{12,8},{16,20},{20,16},{24,28},{28,24},{32,36},... | collective-permute-start | bytes 73736 | tf_op jit(solution)/shard_map/ppermute | solution.py:486
  80.8 5.8 %collective-permute-start.11 = (f32[80,128]{1,0:T(8,128)S(1)}, f32[80,128]{1,0:T(8,128)S(1)}, u32[]{:S(2)}, u32[]{:S(2)}) collective-permute-start(f32[80,128]{1,0:T(8,128)S(1)} %get-tuple-element.50), channel_id=1, source_target_pairs={{0,1},{1,0},{2,3},{3,2},{4,5},{5,4},{6,7},{7,6},{8,9},{9,8},{10,11... | collective-permute-start | bytes 122888 | tf_op jit(solution)/shard_map/ppermute | solution.py:486
  83.2 3.4 %collective-permute-start.10 = (f32[72,128]{1,0:T(8,128)S(1)}, f32[72,128]{1,0:T(8,128)S(1)}, u32[]{:S(2)}, u32[]{:S(2)}) collective-permute-start(f32[72,128]{1,0:T(8,128)S(1)} %get-tuple-element.49), channel_id=1, source_target_pairs={{0,3},{1,2},{2,1},{3,0},{4,7},{5,6},{6,5},{7,4},{8,11},{9,10},{10,... | collective-permute-start | bytes 110600 | tf_op jit(solution)/shard_map/ppermute | solution.py:482
  90.9 18.6 %all-to-all-start.2 = ((f32[128,1,384]{2,1,0:T(1,128)}), f32[128,1,384]{2,1,0:T(1,128)S(1)}, u32[]{:S(2)}, u32[]{:S(2)}) async-start(f32[128,1,384]{2,1,0:T(1,128)} %bitcast.12), calls=%async_computation.2 | async-start | bytes 393216 | tf_op jit(solution)/shard_map/all_to_all | solution.py:553
  97.3 14.6 %collective-permute-start.12 = (f32[48,128]{1,0:T(8,128)S(1)}, f32[48,128]{1,0:T(8,128)S(1)}, u32[]{:S(2)}, u32[]{:S(2)}) collective-permute-start(f32[48,128]{1,0:T(8,128)S(1)} %get-tuple-element.53), channel_id=1, source_target_pairs={{0,252},{4,8},{8,4},{12,16},{16,12},{20,24},{24,20},{28,32},{32,28... | collective-permute-start | bytes 73736 | tf_op jit(solution)/shard_map/ppermute | solution.py:482
  104.4 7.5 %collective-permute-start.13 = (f32[48,128]{1,0:T(8,128)S(1)}, f32[48,128]{1,0:T(8,128)S(1)}, u32[]{:S(2)}, u32[]{:S(2)}) collective-permute-start(f32[48,128]{1,0:T(8,128)S(1)} %get-tuple-element.54), channel_id=1, source_target_pairs={{0,4},{4,0},{8,12},{12,8},{16,20},{20,16},{24,28},{28,24},{32,36},... | collective-permute-start | bytes 73736 | tf_op jit(solution)/shard_map/ppermute | solution.py:486
  104.4 3.5 %collective-permute-start.14 = (f32[16,128]{1,0:T(8,128)S(1)}, f32[16,128]{1,0:T(8,128)S(1)}, u32[]{:S(2)}, u32[]{:S(2)}) collective-permute-start(f32[16,128]{1,0:T(8,128)S(1)} %shard_map.120), channel_id=1, source_target_pairs={{0,3},{1,2},{2,1},{3,0},{4,7},{5,6},{6,5},{7,4},{8,11},{9,10},{10,... | collective-permute-start | bytes 24584 | tf_op jit(solution)/shard_map/ppermute | solution.py:482
  109.5 3.2 %collective-permute-start.15 = (f32[24,128]{1,0:T(8,128)S(1)}, f32[24,128]{1,0:T(8,128)S(1)}, u32[]{:S(2)}, u32[]{:S(2)}) collective-permute-start(f32[24,128]{1,0:T(8,128)S(1)} %get-tuple-element.56), channel_id=1, source_target_pairs={{0,1},{1,0},{2,3},{3,2},{4,5},{5,4},{6,7},{7,6},{8,9},{9,8},{10,11... | collective-permute-start | bytes 36872 | tf_op jit(solution)/shard_map/ppermute | solution.py:486
